TPU v7x, 512 devices: a whole 4x8x8 slice. The times are simulated.
512 devices in a mesh: seq: 128 (over z, y, core), mp: 4 (over x).
Axes of the slice: x: 4, y: 8, z: 8, core: 2. Of those that a mesh axis runs over, the one named last changes fastest.
Arguments:
- y_first: bfloat16 [32768, 896], P('seq', 'mp'), may hold values from -6 to 6
- y_second: bfloat16 [32768, 896], P('seq', 'mp'), may hold values from -10 to 10
- grad_first: bfloat16 [32768, 896], P('seq', 'mp'), may hold values from -6 to 6
- grad_second: bfloat16 [32768, 896], P('seq', 'mp'), may hold values from -6 to 6
- doc_blocks: int32 [192], replicated, may hold values from 1 to 2, as said below
- last_fill: int32 [192], replicated, may hold values from 1 to 128
- plan: int32 [256], replicated, may hold values from 0 to 255, as said below
- q_weight: bfloat16 [896, 512], P(None, 'mp'), may hold values from -1 to 1
- kv_weight: bfloat16 [2, 896, 128], P(None, 'mp'), may hold values from -1 to 1
- out_weight: bfloat16 [512, 896], P('mp'), may hold values from -0.25 to 0.25
- gate_up: bfloat16 [2, 896, 2560], P(None, None, 'mp'), may hold values from -0.1875 to 0.1875
- down_weight: bfloat16 [2560, 896], P('mp'), may hold values from -0.125 to 0.125
Outputs:
- first_input: bfloat16 [32768, 896], P('seq', 'mp')
- second_input: bfloat16 [32768, 896], P('seq', 'mp')
- first_grad: bfloat16 [32768, 896], P('seq', 'mp')
- second_grad: bfloat16 [32768, 896], P('seq', 'mp')
- q_weight_grad: float32 [896, 512], P('seq', 'mp')
- kv_weight_grad: float32 [2, 896, 128], P(None, 'seq')
- out_weight_grad: float32 [512, 896], P('mp', 'seq')
Inputs may be any that keep to these rules, and one draw needn't show every extreme that they name: `doc_blocks`: each document holds 1 or 2 blocks; together they fill all 256 blocks; exactly 64 documents hold 2. A permutation: block b goes to slot plan[b]; slots k * 2 to (k + 1) * 2 - 1 belong to index k of seq; the blocks of one document go to consecutive slots of one index, in order, the first at an even slot.
All inputs are finite; a program needn't handle non-finite values.
Results may differ from a plain program's by a relative error of at most 0.024.
Values may be sent and summed in bfloat16 or wider, within the bound.
No kernel may reach another device: no remote copies, remote signals or barrier semaphores. Data moves between devices by JAX's collectives and lax.ppermute only.
A program may use at most 64 MiB of HBM per device.

v0:
```python
import jax
import jax.numpy as jnp
from jax import lax
from jax.experimental import pallas as pl
from jax.experimental.pallas import tpu as pltpu
from jax.sharding import Mesh
from jax.sharding import PartitionSpec as P

BLOCK = 128
SEQ = ("seq_0", "seq_1", "seq_2")
EPSILON = 1e-06
MP = 4
INTERPRET = False
F32 = jnp.float32
BF16 = jnp.bfloat16


def exchange(value, axis):
    return lax.all_to_all(value, axis, split_axis=0, concat_axis=0, tiled=True)


def dot(left, right, dims):
    return lax.dot_general(left, right, (dims, ((), ())), preferred_element_type=F32)


NN = ((1,), (0,))
NT = ((1,), (1,))
TN = ((0,), (0,))


def slot_facts(doc_blocks, last_fill, plan, slots):
    blocks = plan.shape[0]
    index = jnp.arange(blocks, dtype=jnp.int32)
    mine = jnp.sum(jnp.where(plan[None, :] == slots[:, None], index[None, :], 0), axis=1)
    docs = doc_blocks.shape[0]
    order = jnp.arange(docs, dtype=jnp.int32)
    ends = jnp.sum(jnp.where(order[None, :] <= order[:, None], doc_blocks[None, :], 0), axis=1)
    starts = ends - doc_blocks
    inside = (starts[None, :] <= mine[:, None]) & (mine[:, None] < ends[None, :])
    owner = jnp.sum(jnp.where(inside, order[None, :], 0), axis=1)
    last = inside & (ends[None, :] - 1 == mine[:, None])
    limit = jnp.where(
        jnp.any(last, axis=1), jnp.sum(jnp.where(last, last_fill[None, :], 0), axis=1), BLOCK
    )
    same = (owner[0] == owner[1]).astype(jnp.int32)
    return jnp.stack([limit[0], limit[1], same, same]).astype(jnp.int32)


def feed_forward_kernel(rows_ref, gate_up_ref, down_ref, out_ref, inverse_ref):
    parts, _, lanes = rows_ref.shape
    width = lanes // 2
    total = None
    for m in range(parts):
        piece = rows_ref[m, :, :width].astype(F32)
        part = jnp.sum(piece * piece, axis=-1, keepdims=True)
        total = part if total is None else total + part
    inverse = lax.rsqrt(total / (parts * width) + EPSILON)
    inverse_ref[...] = inverse
    gate = up = dh = 0.0
    for m in range(parts):
        normed = (rows_ref[m, :, :width].astype(F32) * inverse).astype(BF16)
        at = slice(m * width, (m + 1) * width)
        gate += dot(normed, gate_up_ref[0, at, :], NN)
        up += dot(normed, gate_up_ref[1, at, :], NN)
        dh += dot(rows_ref[m, :, width:], down_ref[m], NT)
    sigma = jax.nn.sigmoid(gate)
    silu = gate * sigma
    hidden = (silu * up).astype(BF16)
    d_gate = (dh * up * sigma * (1.0 + gate * (1.0 - sigma))).astype(BF16)
    d_up = (dh * silu).astype(BF16)
    inner = jnp.sum(d_gate.astype(F32) * gate + d_up.astype(F32) * up, axis=-1, keepdims=True)
    inner = inner / (parts * width)
    spare = out_ref.shape[2] // 2
    tail = jnp.broadcast_to(inner, (inner.shape[0], spare - width)).astype(BF16)
    for m in range(parts):
        at = slice(m * width, (m + 1) * width)
        out_ref[m, :, :width] = dot(hidden, down_ref[m], NN).astype(BF16)
        out_ref[m, :, width:spare] = tail
        out_ref[m, :, spare : spare + width] = (
            dot(d_gate, gate_up_ref[0, at, :], NT) + dot(d_up, gate_up_ref[1, at, :], NT)
        ).astype(BF16)
        out_ref[m, :, spare + width :] = tail


def feed_forward(rows, gate_up, down):
    parts, count, lanes = rows.shape
    return pl.pallas_call(
        feed_forward_kernel,
        out_shape=(
            jax.ShapeDtypeStruct((parts, count, 512), BF16),
            jax.ShapeDtypeStruct((count, 1), F32),
        ),
        interpret=INTERPRET,
        compiler_params=pltpu.CompilerParams(vmem_limit_bytes=48 * 2**20),
        name="feed_forward",
    )(rows, gate_up, down)


def attention_kernel(
    facts_ref, rows_ref, query_ref, keyval_ref, proj_ref, out_ref, grads_ref, inverse_ref
):
    parts, count, lanes = rows_ref.shape
    width = lanes // 2
    total = None
    for m in range(parts):
        piece = rows_ref[m, :, :width].astype(F32)
        part = jnp.sum(piece * piece, axis=-1, keepdims=True)
        total = part if total is None else total + part
    inverse = lax.rsqrt(total / (parts * width) + EPSILON)
    inverse_ref[...] = inverse
    normed = []
    query = keyval = d_out = 0.0
    for m in range(parts):
        at = slice(m * width, (m + 1) * width)
        piece = (rows_ref[m, :, :width].astype(F32) * inverse).astype(BF16)
        normed.append(piece)
        query += dot(piece, query_ref[at, :], NN)
        keyval += dot(piece, keyval_ref[at, :], NN)
        d_out += dot(rows_ref[m, :, width:], proj_ref[m], NT)
    query = query.astype(BF16)
    keyval = keyval.astype(BF16)
    d_out = d_out.astype(BF16)
    half = keyval.shape[1] // 2
    lane = lax.broadcasted_iota(jnp.int32, keyval.shape, 1)
    low = lane < half
    wide = keyval.astype(F32)
    turned = pltpu.roll(wide, half, 1)
    keys = jnp.where(low, wide, turned).astype(BF16)
    values = jnp.where(low, turned, wide).astype(BF16)
    row = lax.broadcasted_iota(jnp.int32, (count, count), 0)
    col = lax.broadcasted_iota(jnp.int32, (count, count), 1)
    limit = jnp.where(col < BLOCK, facts_ref[0], facts_ref[1] + BLOCK)
    together = (facts_ref[2] == 1) | ((row >= BLOCK) == (col >= BLOCK))
    allowed = (col <= row) & together & ((col < limit) | (col == row))
    scale = 1.0 / (half**0.5)
    heads = d_query = d_key = d_value = 0.0
    for h in range(2):
        own = low if h == 0 else jnp.logical_not(low)
        zero = jnp.zeros_like(query)
        scores = dot(jnp.where(own, query, zero), keys, NT) * scale
        scores = jnp.where(allowed, scores, -1e30)
        expo = jnp.exp(scores - jnp.max(scores, axis=-1, keepdims=True))
        probs = expo / jnp.sum(expo, axis=-1, keepdims=True)
        probs_b = probs.astype(BF16)
        heads += jnp.where(own, dot(probs_b, values, NN), 0.0)
        d_prob = dot(jnp.where(own, d_out, zero), values, NT)
        delta = jnp.sum(probs * d_prob, axis=-1, keepdims=True)
        d_score = (probs * (d_prob - delta) * scale).astype(BF16)
        d_query += jnp.where(own, dot(d_score, keys, NN), 0.0)
        d_key += jnp.where(own, dot(d_score, query, TN), 0.0)
        d_value += jnp.where(own, dot(probs_b, d_out, TN), 0.0)
    heads = heads.astype(BF16)
    d_query = d_query.astype(BF16)
    d_key = d_key + pltpu.roll(d_key, half, 1)
    d_value = d_value + pltpu.roll(d_value, half, 1)
    d_keyval = jnp.where(low, d_key, d_value).astype(BF16)
    inner = jnp.sum(
        d_query.astype(F32) * query.astype(F32) + d_keyval.astype(F32) * wide,
        axis=-1,
        keepdims=True,
    ) / (parts * width)
    spare = out_ref.shape[2] // 2
    tail = jnp.broadcast_to(inner, (count, spare - width)).astype(BF16)
    for m in range(parts):
        at = slice(m * width, (m + 1) * width)
        out_ref[m, :, :width] = dot(heads, proj_ref[m], NN).astype(BF16)
        out_ref[m, :, width:spare] = tail
        out_ref[m, :, spare : spare + width] = (
            dot(d_query, query_ref[at, :], NT) + dot(d_keyval, keyval_ref[at, :], NT)
        ).astype(BF16)
        out_ref[m, :, spare + width :] = tail
        grads_ref[0, at, :] = dot(normed[m], d_query, TN).astype(BF16)
        grads_ref[1, at, :] = dot(normed[m], d_keyval, TN).astype(BF16)
        grads_ref[2, at, :] = dot(rows_ref[m, :, width:], heads, TN).astype(BF16)


def attention(facts, rows, query, keyval, proj):
    parts, count, lanes = rows.shape
    smem = pl.BlockSpec(memory_space=pltpu.SMEM)
    vmem = pl.BlockSpec(memory_space=pltpu.VMEM)
    return pl.pallas_call(
        attention_kernel,
        in_specs=[smem, vmem, vmem, vmem, vmem],
        out_shape=(
            jax.ShapeDtypeStruct((parts, count, 512), BF16),
            jax.ShapeDtypeStruct((3, query.shape[0], 128), BF16),
            jax.ShapeDtypeStruct((count, 1), F32),
        ),
        interpret=INTERPRET,
        compiler_params=pltpu.CompilerParams(vmem_limit_bytes=48 * 2**20),
        name="attention",
    )(facts, rows, query, keyval, proj)


def to_slots(streams, plan):
    peers = lax.axis_size(SEQ)
    share = BLOCK // peers
    width = streams[0].shape[1]
    whole = len(streams) * width
    sent = jnp.concatenate(
        [s[t * BLOCK : (t + 1) * BLOCK] for t in range(2) for s in streams], axis=1
    ).reshape(peers, share * 2 * whole)
    held = exchange(sent, SEQ).reshape(peers, share, 2 * whole)
    even = held[:, :, :whole].reshape(peers, share * whole)
    odd = held[:, :, whole:].reshape(peers, share * whole)
    pairs = plan.reshape(peers, 2)
    slot = 2 * jnp.arange(peers, dtype=jnp.int32)[:, None]
    halves = []
    for t in range(2):
        pick_even = (pairs[None, :, 0] == slot + t).astype(BF16)
        pick_odd = (pairs[None, :, 1] == slot + t).astype(BF16)
        picked = jnp.dot(pick_even, even, preferred_element_type=F32) + jnp.dot(
            pick_odd, odd, preferred_element_type=F32
        )
        halves.append(picked.astype(BF16).reshape(peers, share, whole))
    placed = jnp.concatenate(halves, axis=2).reshape(peers, share * 2 * whole)
    owned = exchange(placed, SEQ).reshape(BLOCK, 2 * whole)
    return jnp.concatenate([owned[:, :whole], owned[:, whole:]], axis=0)


def shards(
    y_first,
    y_second,
    grad_first,
    grad_second,
    doc_blocks,
    last_fill,
    plan,
    q_weight,
    kv_weight,
    out_weight,
    gate_up,
    down_weight,
):
    count, width = y_first.shape
    seq_size = lax.axis_size(SEQ)
    me = lax.axis_index("mp")
    slots = lax.axis_index(SEQ) * 2 + jnp.arange(2, dtype=jnp.int32)
    facts = slot_facts(doc_blocks, last_fill, plan, slots)
    row = jnp.arange(count, dtype=jnp.int32)
    row_limit = jnp.where(row < BLOCK, facts[0], facts[1] + BLOCK)
    live = (row < row_limit)[:, None]

    groups = kv_weight.shape[0]
    per = MP // groups
    keyval = exchange(jnp.repeat(kv_weight, per, axis=0), "mp").reshape(MP * width, -1)
    down = jnp.moveaxis(down_weight.reshape(-1, MP, width), 1, 0)
    proj = jnp.moveaxis(out_weight.reshape(-1, MP, width), 1, 0)

    moved = to_slots((y_first, grad_second, y_second, grad_first), plan)
    first = moved[:, :width].astype(F32)
    cot_second = moved[:, width : 2 * width].astype(F32)
    second = moved[:, 2 * width : 3 * width].astype(F32)
    cot_first = moved[:, 3 * width :].astype(F32)

    rows = lax.all_gather(moved[:, : 2 * width], "mp", axis=0)
    parts, r_one = feed_forward(rows, gate_up, down)
    arrived = jnp.sum(exchange(parts, "mp").astype(F32), axis=0)
    mixed = arrived[:, :width]
    inner = arrived[:, width : width + 1]
    d_norm = arrived[:, 256 : 256 + width]
    second_in = (second - mixed).astype(BF16)
    first_cot = (cot_first + (d_norm - first * r_one * inner) * r_one).astype(BF16)
    masked = jnp.where(live, first_cot, jnp.zeros_like(first_cot))

    rows = lax.all_gather(jnp.concatenate([second_in, masked], axis=1), "mp", axis=0)
    parts, grads, r_two = attention(facts, rows, q_weight, keyval, proj)
    sent = jnp.moveaxis(grads.reshape(3, seq_size, -1), 0, 1).reshape(seq_size, -1)
    summed = jnp.sum(exchange(sent, SEQ).astype(F32), axis=0).reshape(3, -1, 128)
    arrived = jnp.sum(exchange(parts, "mp").astype(F32), axis=0)
    attn = arrived[:, :width]
    inner = arrived[:, width : width + 1]
    d_norm = arrived[:, 256 : 256 + width]
    first_in = (first - jnp.where(live, attn, 0.0)).astype(BF16)
    normed = second_in.astype(F32) * r_two
    second_cot = (cot_second + (d_norm - normed * inner) * r_two).astype(BF16)

    shares = exchange(jnp.broadcast_to(summed[1], (MP, *summed[1].shape)), "mp")
    kv_grad = shares.reshape(groups, per, *summed[1].shape).sum(axis=1)
    return (
        first_in,
        second_in,
        first_cot,
        second_cot,
        summed[0],
        kv_grad,
        summed[2].T,
    )


def solution(mesh):
    if "seq" in mesh.shape and mesh.shape["seq"] == 128:
        shape = (8, 8, 2, MP)
    else:
        shape = (2, 2, 2, MP)
    finer = Mesh(mesh.devices.reshape(shape), ("seq_0", "seq_1", "seq_2", "mp"))
    return jax.shard_map(
        shards,
        mesh=finer,
        in_specs=(
            P(SEQ, "mp"),
            P(SEQ, "mp"),
            P(SEQ, "mp"),
            P(SEQ, "mp"),
            P(),
            P(),
            P(),
            P(None, "mp"),
            P(None, "mp", None),
            P("mp", None),
            P(None, None, "mp"),
            P("mp", None),
        ),
        out_specs=(
            P(SEQ, "mp"),
            P(SEQ, "mp"),
            P(SEQ, "mp"),
            P(SEQ, "mp"),
            P(SEQ, "mp"),
            P(None, SEQ, None),
            P("mp", SEQ),
        ),
        check_vma=False,
    )
```

profile of v0, /device:TPU:1, one launch (start us, length us, event | category | flops | bytes accessed | tf_op | source)
XLA Modules:
  0.0 193.8 jit_solution(15452877300813863752)
XLA Ops:
  5.7 1.0 reduce.11
  7.6 18.4 %all-to-all-start = ((bf16[128,2,896]{2,1,0:T(2,128)(2,1)}), bf16[128,2,896]{2,1,0:T(2,128)(2,1)S(1)}, u32[]{:S(2)}, u32[]{:S(2)}) async-start(bf16[128,2,896]{2,1,0:T(2,128)(2,1)} %reshape.146), calls=%async_computation | async-start | bytes 917504 | tf_op jit(solution)/shard_map/all_to_all | solution.py:19
  26.3 18.9 %all-to-all-done = bf16[128,2,896]{2,1,0:T(2,128)(2,1)S(1)} async-done(((bf16[128,2,896]{2,1,0:T(2,128)(2,1)}), bf16[128,2,896]{2,1,0:T(2,128)(2,1)S(1)}, u32[]{:S(2)}, u32[]{:S(2)}) %all-to-all-start) | async-done | bytes 458784 | tf_op jit(solution)/shard_map/all_to_all | solution.py:19
  49.5 5.3 %all-to-all-start.1 = ((bf16[128,2,896]{2,1,0:T(2,128)(2,1)}), bf16[128,2,896]{2,1,0:T(2,128)(2,1)S(1)}, u32[]{:S(2)}, u32[]{:S(2)}) async-start(bf16[128,2,896]{2,1,0:T(2,128)(2,1)} %reshape.148), calls=%async_computation.1 | async-start | bytes 917504 | tf_op jit(solution)/shard_map/all_to_all | solution.py:19
  54.9 2.1 %copy.141 = bf16[640,896]{0,1:T(8,128)(2,1)S(1)} copy(bf16[640,896]{1,0:T(8,128)(2,1)} %param.23) | data formatting | bytes 2293760 | tf_op args[11]
  57.9 16.2 %all-to-all-done.1 = bf16[128,2,896]{2,1,0:T(2,128)(2,1)S(1)} async-done(((bf16[128,2,896]{2,1,0:T(2,128)(2,1)}), bf16[128,2,896]{2,1,0:T(2,128)(2,1)S(1)}, u32[]{:S(2)}, u32[]{:S(2)}) %all-to-all-start.1) | async-done | bytes 458784 | tf_op jit(solution)/shard_map/all_to_all | solution.py:19
  74.6 14.0 %all-gather = bf16[1024,448]{1,0:T(8,128)(2,1)S(1)} all-gather(bf16[256,448]{1,0:T(8,128)(2,1)S(1)} %fusion.10), channel_id=2, replica_groups=mesh['seq_0'=8,'seq_1'=8,'seq_2'=2,'mp'=4] {'mp'}, dimensions={0}, use_global_device_ids=true | all-gather | bytes 1146880 | tf_op jit(solution)/shard_map/all_gather | solution.py:256
  88.6 4.0 %feed_forward.1 = (bf16[4,256,512]{2,1,0:T(8,128)(2,1)}, f32[256,1]{1,0:T(8,128)S(1)}) custom-call(bf16[4,256,448]{2,1,0:T(8,128)(2,1)S(1)} %bitcast.41, bf16[2,896,640]{2,1,0:T(8,128)(2,1)S(1)} %copy-done, bf16[4,640,224]{2,1,0:T(8,128)(2,1)S(1)} %bitcast.39), custom_call_target="tpu_custom_call" | custom-call | tf_op jit(solution)/shard_map/feed_forward/pallas_call | solution.py:87
  92.5 3.6 %all-to-all-start.2 = ((bf16[4,256,512]{2,1,0:T(8,128)(2,1)}), bf16[4,256,512]{2,1,0:T(8,128)(2,1)S(1)}, u32[]{:S(2)}, u32[]{:S(2)}) async-start(bf16[4,256,512]{2,1,0:T(8,128)(2,1)} %get-tuple-element.12), calls=%async_computation.2 | async-start | bytes 2097152 | tf_op jit(solution)/shard_map/all_to_all | solution.py:19
  101.0 8.1 %all-to-all-done.2 = bf16[4,256,512]{2,1,0:T(8,128)(2,1)S(1)} async-done(((bf16[4,256,512]{2,1,0:T(8,128)(2,1)}), bf16[4,256,512]{2,1,0:T(8,128)(2,1)S(1)}, u32[]{:S(2)}, u32[]{:S(2)}) %all-to-all-start.2) | async-done | bytes 1048608 | tf_op jit(solution)/shard_map/all_to_all | solution.py:19
  109.7 3.6 %all-to-all-start.3 = ((bf16[4,224,128]{2,1,0:T(8,128)(2,1)}), bf16[4,224,128]{2,1,0:T(8,128)(2,1)S(1)}, u32[]{:S(2)}, u32[]{:S(2)}) async-start(bf16[4,224,128]{2,1,0:T(8,128)(2,1)} %bitcast.11), calls=%async_computation.3 | async-start | bytes 458752 | tf_op jit(solution)/shard_map/all_to_all | solution.py:19
  114.1 13.2 %all-gather.1 = bf16[1024,448]{1,0:T(8,128)(2,1)S(1)} all-gather(bf16[256,448]{1,0:T(8,128)(2,1)S(1)} %pad_maximum_fusion.1), channel_id=3, replica_groups=mesh['seq_0'=8,'seq_1'=8,'seq_2'=2,'mp'=4] {'mp'}, dimensions={0}, use_global_device_ids=true | all-gather | bytes 1146880 | tf_op jit(solution)/shard_map/all_gather | solution.py:266
  127.4 4.7 %attention.1 = (bf16[4,256,512]{2,1,0:T(8,128)(2,1)}, bf16[3,896,128]{2,1,0:T(8,128)(2,1)S(1)}, f32[256,1]{1,0:T(8,128)S(1)}) custom-call(s32[4]{0:T(128)S(1)} %pad_add_fusion.facts_ref, bf16[4,256,448]{2,1,0:T(8,128)(2,1)S(1)} %bitcast.40, bf16[896,128]{1,0:T(8,128)(2,1)S(1)} %copy-done.1, bf16[896,128]{1,0:T(8,128)(2,1)S(1)} %bitcast.43, ...), custom_call_target="tpu_custom_call" | custom-call | tf_op jit(solution)/shard_map/attention/pallas_call | solution.py:181
  132.0 4.2 %all-to-all-start.4 = ((bf16[4,256,512]{2,1,0:T(8,128)(2,1)}), bf16[4,256,512]{2,1,0:T(8,128)(2,1)S(1)}, u32[]{:S(2)}, u32[]{:S(2)}) async-start(bf16[4,256,512]{2,1,0:T(8,128)(2,1)} %get-tuple-element.14), calls=%async_computation.4 | async-start | bytes 2097152 | tf_op jit(solution)/shard_map/all_to_all | solution.py:19
  136.2 1.6 reshape.136
  137.8 1.4 copy.145
  139.3 1.2 reduce.13
  140.8 1.6 reshape.150
  142.4 3.6 %all-to-all-done.4 = bf16[4,256,512]{2,1,0:T(8,128)(2,1)S(1)} async-done(((bf16[4,256,512]{2,1,0:T(8,128)(2,1)}), bf16[4,256,512]{2,1,0:T(8,128)(2,1)S(1)}, u32[]{:S(2)}, u32[]{:S(2)}) %all-to-all-start.4) | async-done | bytes 1048608 | tf_op jit(solution)/shard_map/all_to_all | solution.py:19
  146.0 11.5 %all-to-all-start.5 = ((bf16[128,2,1344]{2,1,0:T(2,128)(2,1)}), bf16[128,2,1344]{2,1,0:T(2,128)(2,1)S(1)}, u32[]{:S(2)}, u32[]{:S(2)}) async-start(bf16[128,2,1344]{2,1,0:T(2,128)(2,1)} %reshape.150), calls=%async_computation.5 | async-start | bytes 1441792 | tf_op jit(solution)/shard_map/all_to_all | solution.py:19
  160.3 22.0 %all-to-all-done.5 = bf16[128,2,1344]{2,1,0:T(2,128)(2,1)S(1)} async-done(((bf16[128,2,1344]{2,1,0:T(2,128)(2,1)}), bf16[128,2,1344]{2,1,0:T(2,128)(2,1)S(1)}, u32[]{:S(2)}, u32[]{:S(2)}) %all-to-all-start.5) | async-done | bytes 688160 | tf_op jit(solution)/shard_map/all_to_all | solution.py:19
  183.2 1.3 convert_reduce_fusion.2
  185.7 3.2 %all-to-all-start.6 = ((f32[4,7,128]{2,1,0:T(8,128)}), f32[4,7,128]{2,1,0:T(8,128)S(1)}, u32[]{:S(2)}, u32[]{:S(2)}) async-start(f32[4,7,128]{2,1,0:T(8,128)} %broadcast_in_dim.111), calls=%async_computation.6 | async-start | bytes 32768 | tf_op jit(solution)/shard_map/all_to_all | solution.py:19
  190.7 2.5 %all-to-all-done.6 = f32[4,7,128]{2,1,0:T(8,128)S(1)} async-done(((f32[4,7,128]{2,1,0:T(8,128)}), f32[4,7,128]{2,1,0:T(8,128)S(1)}, u32[]{:S(2)}, u32[]{:S(2)}) %all-to-all-start.6) | async-done | bytes 14368 | tf_op jit(solution)/shard_map/all_to_all | solution.py:19
  (87 shorter events, 23.6 us)
Async XLA Ops:
  5.7 20.3 %copy-start.6 = (s32[256]{0:T(256)S(1)}, s32[256]{0:T(256)}, u32[]{:S(2)}) copy-start(s32[256]{0:T(256)} %param.18) | copy-start | bytes 3076
  7.6 37.6 %all-to-all-start = ((bf16[128,2,896]{2,1,0:T(2,128)(2,1)}), bf16[128,2,896]{2,1,0:T(2,128)(2,1)S(1)}, u32[]{:S(2)}, u32[]{:S(2)}) async-start(bf16[128,2,896]{2,1,0:T(2,128)(2,1)} %reshape.146), calls=%async_computation | async-start | bytes 917504 | tf_op jit(solution)/shard_map/all_to_all | solution.py:19
  49.5 24.6 %all-to-all-start.1 = ((bf16[128,2,896]{2,1,0:T(2,128)(2,1)}), bf16[128,2,896]{2,1,0:T(2,128)(2,1)S(1)}, u32[]{:S(2)}, u32[]{:S(2)}) async-start(bf16[128,2,896]{2,1,0:T(2,128)(2,1)} %reshape.148), calls=%async_computation.1 | async-start | bytes 917504 | tf_op jit(solution)/shard_map/all_to_all | solution.py:19
  56.9 0.9 copy-start.7
  74.5 14.1 %copy-start = (bf16[2,896,640]{2,1,0:T(8,128)(2,1)S(1)}, bf16[2,896,640]{2,1,0:T(8,128)(2,1)}, u32[]{:S(2)}) copy-start(bf16[2,896,640]{2,1,0:T(8,128)(2,1)} %gate_up_ref.1) | copy-start | bytes 6881284
  92.5 3.7 %copy-start.8 = (s32[192]{0:T(256)S(1)}, s32[192]{0:T(256)}, u32[]{:S(2)}) copy-start(s32[192]{0:T(256)} %param.17) | copy-start | bytes 2308
  92.5 5.9 %copy-start.4 = (bf16[128,896]{1,0:T(8,128)(2,1)S(1)}, bf16[128,896]{1,0:T(8,128)(2,1)}, u32[]{:S(2)}) copy-start(bf16[128,896]{1,0:T(8,128)(2,1)} %param.21) | copy-start | bytes 688132
  92.5 16.5 %copy-start.5 = (bf16[2,224,128]{2,1,0:T(8,128)(2,1)S(1)}, bf16[2,224,128]{2,1,0:T(8,128)(2,1)}, u32[]{:S(2)}) copy-start(bf16[2,224,128]{2,1,0:T(8,128)(2,1)} %param.20) | copy-start | bytes 344068
  92.5 16.5 %all-to-all-start.2 = ((bf16[4,256,512]{2,1,0:T(8,128)(2,1)}), bf16[4,256,512]{2,1,0:T(8,128)(2,1)S(1)}, u32[]{:S(2)}, u32[]{:S(2)}) async-start(bf16[4,256,512]{2,1,0:T(8,128)(2,1)} %get-tuple-element.12), calls=%async_computation.2 | async-start | bytes 2097152 | tf_op jit(solution)/shard_map/all_to_all | solution.py:19
  109.7 17.6 %all-to-all-start.3 = ((bf16[4,224,128]{2,1,0:T(8,128)(2,1)}), bf16[4,224,128]{2,1,0:T(8,128)(2,1)S(1)}, u32[]{:S(2)}, u32[]{:S(2)}) async-start(bf16[4,224,128]{2,1,0:T(8,128)(2,1)} %bitcast.11), calls=%async_computation.3 | async-start | bytes 458752 | tf_op jit(solution)/shard_map/all_to_all | solution.py:19
  113.8 13.6 %copy-start.1 = (bf16[896,128]{1,0:T(8,128)(2,1)S(1)}, bf16[896,128]{1,0:T(8,128)(2,1)}, u32[]{:S(2)}) copy-start(bf16[896,128]{1,0:T(8,128)(2,1)} %query_ref.1) | copy-start | bytes 688132
  132.0 14.0 %all-to-all-start.4 = ((bf16[4,256,512]{2,1,0:T(8,128)(2,1)}), bf16[4,256,512]{2,1,0:T(8,128)(2,1)S(1)}, u32[]{:S(2)}, u32[]{:S(2)}) async-start(bf16[4,256,512]{2,1,0:T(8,128)(2,1)} %get-tuple-element.14), calls=%async_computation.4 | async-start | bytes 2097152 | tf_op jit(solution)/shard_map/all_to_all | solution.py:19
  146.0 36.3 %all-to-all-start.5 = ((bf16[128,2,1344]{2,1,0:T(2,128)(2,1)}), bf16[128,2,1344]{2,1,0:T(2,128)(2,1)S(1)}, u32[]{:S(2)}, u32[]{:S(2)}) async-start(bf16[128,2,1344]{2,1,0:T(2,128)(2,1)} %reshape.150), calls=%async_computation.5 | async-start | bytes 1441792 | tf_op jit(solution)/shard_map/all_to_all | solution.py:19
  159.3 0.8 copy-start.2
  183.2 5.8 %copy-start.3 = (f32[256,512]{1,0:T(8,128)S(1)}, f32[256,512]{1,0:T(8,128)}, u32[]{:S(2)}) copy-start(f32[256,512]{1,0:T(8,128)} %copy-done.2) | copy-start | bytes 1572868
  185.7 7.4 %all-to-all-start.6 = ((f32[4,7,128]{2,1,0:T(8,128)}), f32[4,7,128]{2,1,0:T(8,128)S(1)}, u32[]{:S(2)}, u32[]{:S(2)}) async-start(f32[4,7,128]{2,1,0:T(8,128)} %broadcast_in_dim.111), calls=%async_computation.6 | async-start | bytes 32768 | tf_op jit(solution)/shard_map/all_to_all | solution.py:19
where the time goes:
time: 195 us; the launch traced here: 194 us
  waiting for transfers between devices  71.2 us (37%)
  starting transfers between devices  49.9 us (26%)
  blocking collectives  27.2 us (14%)
  local copies, waits for them, and re-layouts  25.6 us (13%)
  Pallas kernels  8.62 us (4%)
  other arithmetic  7.09 us (4%)
  between operations  3.03 us (2%)
    all_to_all x7, waiting for transfers between devices, exchange(): return lax.all_to_all(value, axis, split_axis=0, concat_axis=0, tiled=True)  71.2 us
    all_to_all x7, starting transfers between devices, exchange(): return lax.all_to_all(value, axis, split_axis=0, concat_axis=0, tiled=True)  49.9 us
    all_gather x1, blocking collectives, shards(): rows = lax.all_gather(moved[:, :2 * width], 'mp', axis=0)  14 us
    all_gather x1, blocking collectives, shards(): lax.all_gather(jnp.concatenate([second_in, masked], axis=1), 'mp', axis=0)  13.2 us
    unnamed x41, local copies, waits for them, and re-layouts  12.9 us
    pallas_call x1, Pallas kernels, attention(): pl.pallas_call(attention_kernel, in_specs=[smem, vmem, vmem, vmem, vmem],...  4.65 us
    pallas_call x1, Pallas kernels, feed_forward(): pl.pallas_call(feed_forward_kernel, out_shape=(jax.ShapeDtypeStruct((part...  3.97 us
  transfers between devices with their start and end apart: 7, of which 6 were waited for; matrix products, arithmetic and copies ran while one was open for 9% of the time, Pallas kernels for 0%

commit v1 on v0

v1 whole, which is shorter than its diff:
```python
import jax
import jax.numpy as jnp
from jax import lax
from jax.experimental import pallas as pl
from jax.experimental.pallas import tpu as pltpu
from jax.sharding import Mesh
from jax.sharding import PartitionSpec as P

BLOCK = 128
SEQ = ("seq_0", "seq_1", "seq_2")
EPSILON = 1e-06
MP = 4
INTERPRET = False
F32 = jnp.float32
BF16 = jnp.bfloat16


PAD = 16


def exchange(value, axis):
    return lax.all_to_all(value, axis, split_axis=0, concat_axis=0, tiled=True)


def dot(left, right, dims):
    return lax.dot_general(left, right, (dims, ((), ())), preferred_element_type=F32)


NN = ((1,), (0,))
NT = ((1,), (1,))
TN = ((0,), (0,))


def slot_facts(doc_blocks, last_fill, plan, slots):
    blocks = plan.shape[0]
    index = jnp.arange(blocks, dtype=jnp.int32)
    mine = jnp.sum(jnp.where(plan[None, :] == slots[:, None], index[None, :], 0), axis=1)
    docs = doc_blocks.shape[0]
    order = jnp.arange(docs, dtype=jnp.int32)
    ends = jnp.sum(jnp.where(order[None, :] <= order[:, None], doc_blocks[None, :], 0), axis=1)
    starts = ends - doc_blocks
    inside = (starts[None, :] <= mine[:, None]) & (mine[:, None] < ends[None, :])
    owner = jnp.sum(jnp.where(inside, order[None, :], 0), axis=1)
    last = inside & (ends[None, :] - 1 == mine[:, None])
    limit = jnp.where(
        jnp.any(last, axis=1), jnp.sum(jnp.where(last, last_fill[None, :], 0), axis=1), BLOCK
    )
    same = (owner[0] == owner[1]).astype(jnp.int32)
    return jnp.stack([limit[0], limit[1], same, lax.axis_index("mp")]).astype(jnp.int32)


def call(kernel, out_shape, *args, scratch=(), smem=0, name=None):
    specs = [pl.BlockSpec(memory_space=pltpu.SMEM)] * smem
    specs += [pl.BlockSpec(memory_space=pltpu.VMEM)] * (len(args) - smem)
    return pl.pallas_call(
        kernel,
        in_specs=specs,
        out_shape=out_shape,
        scratch_shapes=scratch,
        interpret=INTERPRET,
        compiler_params=pltpu.CompilerParams(vmem_limit_bytes=48 * 2**20),
        name=name,
    )(*args)


def put(ref, at, values):
    for j in range(ref.shape[0]):
        ref[pl.ds(j, 1), at, :] = values[None, :, j * 128 : (j + 1) * 128]


def get(ref, at):
    return jnp.concatenate([ref[pl.ds(j, 1), at, :][0] for j in range(ref.shape[0])], axis=1)


def pack_kernel(*refs):
    *streams, out_ref, rows_ref = refs
    for k, stream in enumerate(streams):
        width, count = stream.shape
        gap = jnp.zeros((out_ref.shape[1] - width, count), F32)
        rows = jnp.concatenate([stream[...].astype(F32), gap], axis=0).T
        for t in range(2):
            at = pl.ds(4 * t + k, BLOCK, stride=8)
            put(rows_ref, at, rows[t * BLOCK : (t + 1) * BLOCK])
    out_ref[...] = get(rows_ref, slice(None)).astype(BF16)


def reorder_kernel(plan_ref, held_ref, out_ref, rows_ref, next_ref):
    blocks = plan_ref.shape[1]
    slot = lax.broadcasted_iota(jnp.int32, (blocks, blocks), 0)
    pick = (plan_ref[...] == slot).astype(BF16)
    put(rows_ref, slice(None), held_ref[...].astype(F32))
    for k in range(4):
        at = pl.ds(k, blocks, stride=4)
        put(next_ref, at, dot(pick, get(rows_ref, at).astype(BF16), NN))
    out_ref[...] = get(next_ref, slice(None)).astype(BF16)


def unpack_kernel(rows_in_ref, send_ref, kept_ref, rows_ref):
    width = kept_ref.shape[0] // 4
    put(rows_ref, slice(None), rows_in_ref[...].astype(F32))
    for k in range(4):
        halves = [get(rows_ref, pl.ds(4 * t + k, BLOCK, stride=8)).T for t in range(2)]
        stream = jnp.concatenate(halves, axis=1)[:width].astype(BF16)
        at = slice(k * width, (k + 1) * width)
        kept_ref[at, :] = stream
        if k < 2:
            for m in range(MP):
                send_ref[m, at, :] = stream


def to_slots(streams, plan):
    peers = lax.axis_size(SEQ)
    share = BLOCK // peers
    width = streams[0].shape[0]
    lanes = -(-width // 128) * 128
    rows = 8 * BLOCK
    shape = jax.ShapeDtypeStruct((rows, lanes), BF16)
    scratch = pltpu.VMEM((lanes // 128, rows, 128), F32)
    sent = call(pack_kernel, shape, *streams, scratch=[scratch], name="pack")
    with jax.named_scope("hop_one"):
        held = exchange(sent.reshape(peers, share * 8, lanes), SEQ)
    held = held.reshape(peers, share, 8, lanes)
    placed = []
    for r in range(share):
        placed.append(
            call(
                reorder_kernel,
                jax.ShapeDtypeStruct((peers * 8, lanes), BF16),
                plan.reshape(1, -1),
                held[:, r].reshape(peers * 8, lanes),
                scratch=[pltpu.VMEM((lanes // 128, peers * 8, 128), F32)] * 2,
                name="reorder",
            ).reshape(peers, 8, lanes)
        )
    placed = placed[0] if share == 1 else jnp.stack(placed, axis=1).reshape(peers, -1, lanes)
    with jax.named_scope("hop_two"):
        owned = exchange(placed, SEQ)
    return call(
        unpack_kernel,
        (
            jax.ShapeDtypeStruct((MP, 2 * width, 2 * BLOCK), BF16),
            jax.ShapeDtypeStruct((4 * width, 2 * BLOCK), BF16),
        ),
        owned.reshape(rows, lanes),
        scratch=[scratch],
        name="unpack",
    )


def assemble(rows_ref, whole_ref, first):
    parts, both, _ = rows_ref.shape
    width = both // 2
    for m in range(parts):
        whole_ref[m * width : (m + 1) * width, :] = rows_ref[m, first : first + width, :]


def normalized(whole_ref):
    values = whole_ref[...].astype(F32)
    inverse = lax.rsqrt(jnp.mean(values * values, axis=0, keepdims=True) + EPSILON)
    return (values * inverse).astype(BF16), inverse


def row_sums(values, width):
    ones = jnp.ones((PAD, values.shape[1]), F32)
    sums = lax.dot_general(
        ones, values, (NT, ((), ())), preferred_element_type=F32, precision=lax.Precision.HIGHEST
    )
    return (sums / width).astype(BF16)


def feed_forward_kernel(
    rows_ref, gate_up_ref, down_ref, out_ref, inverse_ref, first_ref, second_ref
):
    parts, both, count = rows_ref.shape
    width = both // 2
    assemble(rows_ref, first_ref, 0)
    assemble(rows_ref, second_ref, width)
    normed, inverse_ref[...] = normalized(first_ref)
    normed = normed.T
    gate = dot(normed, gate_up_ref[0], NN)
    up = dot(normed, gate_up_ref[1], NN)
    dh = dot(second_ref[...].T, down_ref[...], NT)
    sigma = jax.nn.sigmoid(gate)
    silu = gate * sigma
    hidden = (silu * up).astype(BF16)
    d_gate = (dh * up * sigma * (1.0 + gate * (1.0 - sigma))).astype(BF16)
    d_up = (dh * silu).astype(BF16)
    inner = row_sums(d_gate.astype(F32) * gate + d_up.astype(F32) * up, parts * width)
    mixed = dot(hidden, down_ref[...], NN).astype(BF16).T
    for m in range(parts):
        at = slice(m * width, (m + 1) * width)
        out_ref[m, :width, :] = mixed[at]
        out_ref[m, width:both, :] = (
            dot(gate_up_ref[0, at, :], d_gate, NT) + dot(gate_up_ref[1, at, :], d_up, NT)
        ).astype(BF16)
        out_ref[m, both:, :] = inner


def live_columns(facts_ref, shape):
    column = lax.broadcasted_iota(jnp.int32, shape, 1)
    return column < jnp.where(column < BLOCK, facts_ref[0], facts_ref[1] + BLOCK)


def middle_kernel(
    facts_ref, parts_ref, kept_ref, inverse_ref, second_ref, first_cot_ref, send_ref
):
    parts, rows, count = parts_ref.shape
    width = (rows - PAD) // 2
    total = parts_ref[0].astype(F32)
    for m in range(1, parts):
        total += parts_ref[m].astype(F32)
    inverse = inverse_ref[...]
    first = kept_ref[:width, :].astype(F32)
    second = kept_ref[2 * width : 3 * width, :].astype(F32)
    cot = kept_ref[3 * width :, :].astype(F32)
    second = (second - total[:width]).astype(BF16)
    d_norm = total[width : 2 * width]
    inner = total[2 * width : 2 * width + 1]
    cot = (cot + (d_norm - first * inverse * inner) * inverse).astype(BF16)
    second_ref[...] = second
    first_cot_ref[...] = cot
    masked = jnp.where(live_columns(facts_ref, cot.shape), cot.astype(F32), 0.0).astype(BF16)
    for m in range(parts):
        send_ref[m, :width, :] = second
        send_ref[m, width:, :] = masked


def last_kernel(
    facts_ref, *refs
):
    *parts, kept_ref, second_ref, inverse_ref, first_ref, cot_ref = refs
    width = second_ref.shape[0]
    total = parts[0][...].astype(F32)
    for part in parts[1:]:
        total += part[...].astype(F32)
    attn = total[:width]
    d_norm = total[width : 2 * width]
    inner = total[2 * width : 2 * width + 1]
    inverse = inverse_ref[...]
    first = kept_ref[:width, :].astype(F32)
    cot = kept_ref[width : 2 * width, :].astype(F32)
    live = live_columns(facts_ref, attn.shape)
    first_ref[...] = (first - jnp.where(live, attn, 0.0)).astype(BF16)
    normed = second_ref[...].astype(F32) * inverse
    cot_ref[...] = (cot + (d_norm - normed * inner) * inverse).astype(BF16)


def attention_kernel(facts_ref, rows_ref, query_ref, proj_ref, *refs):
    parts, both, count = rows_ref.shape
    width = both // 2
    pieces, refs = refs[:parts], refs[parts:]
    out_refs, refs = refs[:parts], refs[parts:]
    grads_ref, inverse_ref, second_ref, cot_ref, keyval_ref, turned_ref = refs
    me = facts_ref[3]
    for k in range(parts):
        keyval_ref[(me + parts - k) % parts] = pieces[k][...]
    assemble(rows_ref, second_ref, 0)
    assemble(rows_ref, cot_ref, width)
    normed, inverse_ref[...] = normalized(second_ref)
    turned = normed.T
    whole = keyval_ref[...].reshape(parts * width, -1)
    query = dot(turned, query_ref[...].reshape(parts * width, -1), NN).astype(BF16)
    keyval = dot(turned, whole, NN).astype(BF16)
    d_out = dot(cot_ref[...].T, proj_ref[...], NT).astype(BF16)
    half = keyval.shape[1] // 2
    low = lax.broadcasted_iota(jnp.int32, keyval.shape, 1) < half
    wide = keyval.astype(F32)
    rolled = pltpu.roll(wide, half, 1)
    keys = jnp.where(low, wide, rolled).astype(BF16)
    values = jnp.where(low, rolled, wide).astype(BF16)
    row = lax.broadcasted_iota(jnp.int32, (count, count), 0)
    col = lax.broadcasted_iota(jnp.int32, (count, count), 1)
    together = (facts_ref[2] == 1) | ((row >= BLOCK) == (col >= BLOCK))
    allowed = (col <= row) & together & (live_columns(facts_ref, (count, count)) | (col == row))
    scale = 1.0 / (half**0.5)
    heads = d_query = d_key = d_value = 0.0
    for h in range(2):
        own = low if h == 0 else jnp.logical_not(low)
        zero = jnp.zeros_like(query)
        scores = dot(jnp.where(own, query, zero), keys, NT) * scale
        scores = jnp.where(allowed, scores, -1e30)
        expo = jnp.exp(scores - jnp.max(scores, axis=-1, keepdims=True))
        probs = expo / jnp.sum(expo, axis=-1, keepdims=True)
        probs_b = probs.astype(BF16)
        heads += jnp.where(own, dot(probs_b, values, NN), 0.0)
        d_prob = dot(jnp.where(own, d_out, zero), values, NT)
        delta = jnp.sum(probs * d_prob, axis=-1, keepdims=True)
        d_score = (probs * (d_prob - delta) * scale).astype(BF16)
        d_query += jnp.where(own, dot(d_score, keys, NN), 0.0)
        d_key += jnp.where(own, dot(d_score, query, TN), 0.0)
        d_value += jnp.where(own, dot(probs_b, d_out, TN), 0.0)
    heads = heads.astype(BF16)
    d_query = d_query.astype(BF16)
    d_key = d_key + pltpu.roll(d_key, half, 1)
    d_value = d_value + pltpu.roll(d_value, half, 1)
    d_keyval = jnp.where(low, d_key, d_value).astype(BF16)
    spread = lax.broadcasted_iota(jnp.int32, (8 * width // 7, width), 0)
    source = jnp.where(spread % 8 < 7, 7 * (spread // 8) + spread % 8, -1)
    pick = (lax.broadcasted_iota(jnp.int32, source.shape, 1) == source).astype(BF16)
    for m in range(parts):
        at = slice(m * width, (m + 1) * width)
        to = slice(m * pick.shape[0], (m + 1) * pick.shape[0])
        grads = [dot(normed[at], d_query, NN), dot(normed[at], d_keyval, NN)]
        grads.append(dot(cot_ref[at, :], heads, NN))
        grads = jnp.concatenate(grads, axis=1).astype(BF16)
        grads_ref[to, :] = dot(pick, grads, NN).astype(BF16)
    turned_ref[...] = proj_ref[...].T.reshape(turned_ref.shape)
    inner = row_sums(
        d_query.astype(F32) * query.astype(F32) + d_keyval.astype(F32) * wide, parts * width
    )
    for k in range(parts):
        m = (me + k) % parts
        out_refs[k][:width, :] = dot(turned_ref[m], heads, NT).astype(BF16)
        out_refs[k][width:both, :] = (
            dot(query_ref[m], d_query, NT) + dot(keyval_ref[m], d_keyval, NT)
        ).astype(BF16)
        out_refs[k][both:, :] = inner


def turn(value, by):
    return lax.ppermute(value, "mp", [(i, (i + by) % MP) for i in range(MP)])


def shards(
    y_first,
    y_second,
    grad_first,
    grad_second,
    doc_blocks,
    last_fill,
    plan,
    q_weight,
    kv_weight,
    out_weight,
    gate_up,
    down_weight,
):
    count, width = y_first.shape
    seq_size = lax.axis_size(SEQ)
    me = lax.axis_index("mp")
    slots = lax.axis_index(SEQ) * 2 + jnp.arange(2, dtype=jnp.int32)
    facts = slot_facts(doc_blocks, last_fill, plan, slots)
    groups = kv_weight.shape[0]
    with jax.named_scope("weights"):
        pieces = [kv_weight[me >> 1]]
        for k in range(1, MP):
            pieces.append(turn(kv_weight[((me + k) & 3) >> 1], k))

    send, kept = to_slots((y_first.T, grad_second.T, y_second.T, grad_first.T), plan)
    stream = jax.ShapeDtypeStruct((width, count), BF16)
    line = jax.ShapeDtypeStruct((1, count), F32)
    part = jax.ShapeDtypeStruct((2 * width + PAD, count), BF16)
    with jax.named_scope("gather_one"):
        rows = exchange(send, "mp")
    whole = pltpu.VMEM((MP * width, count), BF16)
    parts, r_one = call(
        feed_forward_kernel,
        (jax.ShapeDtypeStruct((MP, *part.shape), BF16), line),
        rows,
        gate_up,
        down_weight,
        scratch=[whole, whole],
        name="feed_forward",
    )
    with jax.named_scope("sum_one"):
        parts = exchange(parts, "mp")
    second_in, first_cot, send = call(
        middle_kernel,
        (stream, stream, jax.ShapeDtypeStruct((MP, 2 * width, count), BF16)),
        facts,
        parts,
        kept,
        r_one,
        smem=1,
        name="middle",
    )
    with jax.named_scope("gather_two"):
        rows = exchange(send, "mp")
    *parts, grads, r_two = call(
        attention_kernel,
        (*[part] * MP, jax.ShapeDtypeStruct((8 * BLOCK, 384), BF16), line),
        facts,
        rows,
        q_weight.reshape(MP, width, -1),
        out_weight,
        *pieces,
        scratch=[whole, whole] + [pltpu.VMEM((MP, width, 128), BF16)] * 2,
        smem=1,
        name="attention",
    )
    with jax.named_scope("weight_grads"):
        grads = exchange(grads.reshape(seq_size, -1, grads.shape[1]), SEQ)
    with jax.named_scope("last_sum"):
        parts = [parts[0]] + [turn(parts[k], k) for k in range(1, MP)]
    first_in, second_cot = call(
        last_kernel, (stream, stream), facts, *parts, kept, second_in, r_two, smem=1, name="last"
    )
    summed = jnp.sum(grads.astype(F32), axis=0).reshape(-1, 8, grads.shape[2])[:, :7]
    summed = summed.reshape(-1, grads.shape[2])
    own = summed[:, 128:256]
    with jax.named_scope("key_grads"):
        shares = exchange(jnp.broadcast_to(own, (MP, *own.shape)), "mp")
    kv_grad = shares.reshape(groups, MP // groups, *own.shape).sum(axis=1)
    return (
        first_in.T,
        second_in.T,
        first_cot.T,
        second_cot.T,
        summed[:, :128],
        kv_grad,
        summed[:, 256:].T,
    )


def solution(mesh):
    if "seq" in mesh.shape and mesh.shape["seq"] == 128:
        shape = (8, 8, 2, MP)
    else:
        shape = (2, 2, 2, MP)
    finer = Mesh(mesh.devices.reshape(shape), ("seq_0", "seq_1", "seq_2", "mp"))
    return jax.shard_map(
        shards,
        mesh=finer,
        in_specs=(
            P(SEQ, "mp"),
            P(SEQ, "mp"),
            P(SEQ, "mp"),
            P(SEQ, "mp"),
            P(),
            P(),
            P(),
            P(None, "mp"),
            P(None, "mp", None),
            P("mp", None),
            P(None, None, "mp"),
            P("mp", None),
        ),
        out_specs=(
            P(SEQ, "mp"),
            P(SEQ, "mp"),
            P(SEQ, "mp"),
            P(SEQ, "mp"),
            P(SEQ, "mp"),
            P(None, SEQ, None),
            P("mp", SEQ),
        ),
        check_vma=False,
    )
```

time: 195 us -> 184 us (0.944)
  blocking collectives: 27.2 us -> 64.6 us
  waiting for transfers between devices: 71.2 us -> 47.7 us
  local copies, waits for them, and re-layouts: 25.6 us -> 9.98 us
  starting transfers between devices: 49.9 us -> 43.1 us
  other arithmetic: 7.09 us -> 2.12 us
  Pallas kernels: 8.62 us -> 12.7 us
    all_to_all x0 -> x2, blocking collectives: none -> 64.6 us  [exchange(): return lax.all_to_all(value, axis, split_axis=0, concat_axis=0, tiled=True)]
    all_to_all x7 -> x5, waiting for transfers between devices: 71.2 us -> 43.6 us  [exchange(): return lax.all_to_all(value, axis, split_axis=0, concat_axis=0, tiled=True)]
    all_gather x2 -> x0, blocking collectives: 27.2 us -> none  [the longest x1 14 us: shards(): rows = lax.all_gather(moved[:, :2 * width], 'mp', axis=0)]
    all_to_all x7 -> x5, starting transfers between devices: 49.9 us -> 23.6 us  [exchange(): return lax.all_to_all(value, axis, split_axis=0, concat_axis=0, tiled=True)]
    ppermute x0 -> x6, starting transfers between devices: none -> 19.5 us  [turn(): return lax.ppermute(value, 'mp', [(i, (i + by) % MP) for i in range(MP)])]
    slice x10 -> x0, local copies, waits for them, and re-layouts: 5.54 us -> none  [the longest x4 3.44 us: to_slots(): s[t * BLOCK:(t + 1) * BLOCK]]
    unnamed x41 -> x35, local copies, waits for them, and re-layouts: 12.9 us -> 8.16 us
    ppermute x0 -> x6, waiting for transfers between devices: none -> 4.12 us  [turn(): return lax.ppermute(value, 'mp', [(i, (i + by) % MP) for i in range(MP)])]
  transfers between devices with their start and end apart: 7 -> 11, of which waited for: 6 -> 7; matrix products, arithmetic and copies ran while one was open for 9% -> 2% of each run, Pallas kernels for 0% -> 1%
where the time goes in v1:
time: 184 us; the launch traced here: 182 us
  blocking collectives  64.6 us (35%)
  waiting for transfers between devices  47.7 us (26%)
  starting transfers between devices  43.1 us (23%)
  Pallas kernels  12.7 us (7%)
  local copies, waits for them, and re-layouts  9.98 us (5%)
  between operations  2.18 us (1%)
  other arithmetic  2.12 us (1%)
    all_to_all x2, blocking collectives, exchange(): return lax.all_to_all(value, axis, split_axis=0, concat_axis=0, tiled=True)  64.6 us
    all_to_all x5, waiting for transfers between devices, exchange(): return lax.all_to_all(value, axis, split_axis=0, concat_axis=0, tiled=True)  43.6 us
    all_to_all x5, starting transfers between devices, exchange(): return lax.all_to_all(value, axis, split_axis=0, concat_axis=0, tiled=True)  23.6 us
    ppermute x6, starting transfers between devices, turn(): return lax.ppermute(value, 'mp', [(i, (i + by) % MP) for i in range(MP)])  19.5 us
    pallas_call x7, Pallas kernels, call(): pl.pallas_call(kernel, in_specs=specs, out_shape=out_shape, scratch_shape...  12.7 us
    unnamed x35, local copies, waits for them, and re-layouts  8.16 us
    ppermute x6, waiting for transfers between devices, turn(): return lax.ppermute(value, 'mp', [(i, (i + by) % MP) for i in range(MP)])  4.12 us
  transfers between devices with their start and end apart: 11, of which 7 were waited for; matrix products, arithmetic and copies ran while one was open for 2% of the time, Pallas kernels for 1%

profile of v1, /device:TPU:1, one launch (start us, length us, event | category | flops | bytes accessed | tf_op | source)
XLA Modules:
  0.0 182.4 jit_solution(6767365414284224660)
XLA Ops:
  4.5 38.8 %all_to_all.35 = bf16[128,8,256]{2,1,0:T(8,128)(2,1)S(1)} all-to-all(bf16[128,8,256]{2,1,0:T(8,128)(2,1)S(1)} %bitcast.34), channel_id=1, replica_groups=mesh['seq_0'=8,'seq_1'=8,'seq_2'=2,'mp'=4] {'seq_0','seq_1','seq_2'}, dimensions={0} | all-to-all | bytes 1048576 | tf_op jit(solution)/shard_map/hop_one/all_to_all | solution.py:22
  43.7 25.9 %all_to_all.36 = bf16[128,8,256]{2,1,0:T(8,128)(2,1)S(1)} all-to-all(bf16[128,8,256]{2,1,0:T(8,128)(2,1)S(1)} %bitcast.32), channel_id=1, replica_groups=mesh['seq_0'=8,'seq_1'=8,'seq_2'=2,'mp'=4] {'seq_0','seq_1','seq_2'}, dimensions={0} | all-to-all | bytes 1048576 | tf_op jit(solution)/shard_map/hop_two/all_to_all | solution.py:22
  71.7 4.0 %all-to-all-start.2 = ((bf16[4,448,256]{2,1,0:T(8,128)(2,1)}), bf16[4,448,256]{2,1,0:T(8,128)(2,1)S(1)}, u32[]{:S(2)}, u32[]{:S(2)}) async-start(bf16[4,448,256]{2,1,0:T(8,128)(2,1)} %copy-done.5), calls=%async_computation.2 | async-start | bytes 1835008 | tf_op jit(solution)/shard_map/gather_one/all_to_all | solution.py:22
  76.0 13.4 %all-to-all-done.2.rows_ref = bf16[4,448,256]{2,1,0:T(8,128)(2,1)S(1)} async-done(((bf16[4,448,256]{2,1,0:T(8,128)(2,1)}), bf16[4,448,256]{2,1,0:T(8,128)(2,1)S(1)}, u32[]{:S(2)}, u32[]{:S(2)}) %all-to-all-start.2) | async-done | bytes 917536 | tf_op jit(solution)/shard_map/gather_one/all_to_all | solution.py:22
  90.7 3.4 %feed_forward.1 = (bf16[4,464,256]{2,1,0:T(8,128)(2,1)S(1)}, f32[1,256]{1,0:T(1,128)S(1)}) custom-call(bf16[4,448,256]{2,1,0:T(8,128)(2,1)S(1)} %all-to-all-done.2.rows_ref, bf16[2,896,640]{2,1,0:T(8,128)(2,1)S(1)} %copy-done, bf16[640,896]{1,0:T(8,128)(2,1)S(1)} %copy-done.3), custom_call_target="tpu_custom_call" | custom-call | tf_op jit(solution)/shard_map/feed_forward/pallas_call | solution.py:55
  95.1 3.6 %all-to-all-start.3 = ((bf16[4,464,256]{2,1,0:T(8,128)(2,1)}), bf16[4,464,256]{2,1,0:T(8,128)(2,1)S(1)}, u32[]{:S(2)}, u32[]{:S(2)}) async-start(bf16[4,464,256]{2,1,0:T(8,128)(2,1)} %copy-done.4), calls=%async_computation.3 | async-start | bytes 1900544 | tf_op jit(solution)/shard_map/sum_one/all_to_all | solution.py:22
  101.1 10.8 %all-to-all-done.3.parts_ref = bf16[4,464,256]{2,1,0:T(8,128)(2,1)S(1)} async-done(((bf16[4,464,256]{2,1,0:T(8,128)(2,1)}), bf16[4,464,256]{2,1,0:T(8,128)(2,1)S(1)}, u32[]{:S(2)}, u32[]{:S(2)}) %all-to-all-start.3) | async-done | bytes 950304 | tf_op jit(solution)/shard_map/sum_one/all_to_all | solution.py:22
  112.0 1.7 middle.1
  113.7 3.5 %all-to-all-start.4 = ((bf16[4,448,256]{2,1,0:T(8,128)(2,1)}), bf16[4,448,256]{2,1,0:T(8,128)(2,1)S(1)}, u32[]{:S(2)}, u32[]{:S(2)}) async-start(bf16[4,448,256]{2,1,0:T(8,128)(2,1)} %get-tuple-element.26), calls=%async_computation.4 | async-start | bytes 1835008 | tf_op jit(solution)/shard_map/gather_two/all_to_all | solution.py:22
  117.2 4.5 %collective-permute-start.2 = (bf16[224,128]{1,0:T(8,128)(2,1)S(1)}, bf16[224,128]{1,0:T(8,128)(2,1)S(1)}, u32[]{:S(2)}, u32[]{:S(2)}) collective-permute-start(bf16[224,128]{1,0:T(8,128)(2,1)S(1)} %get-tuple-element.61), channel_id=1, source_target_pairs={{0,3},{1,0},{2,1},{3,2},{4,7},{5,4},{6,5},{7,6},{8,11},{9,8},{10,9... | collective-permute-start | bytes 172040 | tf_op jit(solution)/shard_map/weights/ppermute | solution.py:321
  121.8 1.9 %collective-permute-start = (bf16[224,128]{1,0:T(8,128)(2,1)S(1)}, bf16[224,128]{1,0:T(8,128)(2,1)S(1)}, u32[]{:S(2)}, u32[]{:S(2)}) collective-permute-start(bf16[224,128]{1,0:T(8,128)(2,1)S(1)} %get-tuple-element.62), channel_id=1, source_target_pairs={{0,1},{1,2},{2,3},{3,0},{4,5},{5,6},{6,7},{7,4},{8,9},{9,10},{10,1... | collective-permute-start | bytes 172040 | tf_op jit(solution)/shard_map/weights/ppermute | solution.py:321
  123.7 3.8 %collective-permute-start.1 = (bf16[224,128]{1,0:T(8,128)(2,1)S(1)}, bf16[224,128]{1,0:T(8,128)(2,1)S(1)}, u32[]{:S(2)}, u32[]{:S(2)}) collective-permute-start(bf16[224,128]{1,0:T(8,128)(2,1)S(1)} %get-tuple-element.64), channel_id=1, source_target_pairs={{0,2},{1,3},{2,0},{3,1},{4,6},{5,7},{6,4},{7,5},{8,10},{9,11},{10,... | collective-permute-start | bytes 172040 | tf_op jit(solution)/shard_map/weights/ppermute | solution.py:321
  127.5 1.4 collective-permute-done.2.refs_3_
  129.8 1.8 collective-permute-done.1.refs_2_
  131.7 5.2 %attention.1 = (bf16[464,256]{1,0:T(8,128)(2,1)S(1)}, bf16[464,256]{1,0:T(8,128)(2,1)S(1)}, bf16[464,256]{1,0:T(8,128)(2,1)S(1)}, bf16[464,256]{1,0:T(8,128)(2,1...) custom-call(s32[4]{0:T(128)S(1)} %pad_add_fusion.facts_ref, bf16[4,448,256]{2,1,0:T(8,128)(2,1)S(1)} %all-to-all-done.4.rows_ref, ...), custom_call_target="tpu_custom_call" | custom-call | tf_op jit(solution)/shard_map/attention/pallas_call | solution.py:55
  136.9 8.9 %all-to-all-start.5 = ((bf16[128,8,384]{2,1,0:T(8,128)(2,1)}), bf16[128,8,384]{2,1,0:T(8,128)(2,1)}, u32[]{:S(2)}, u32[]{:S(2)}) async-start(bf16[128,8,384]{2,1,0:T(8,128)(2,1)} %bitcast.19), calls=%async_computation.5 | async-start | bytes 1572864 | tf_op jit(solution)/shard_map/weight_grads/all_to_all | solution.py:22
  145.8 2.2 %collective-permute-start.3 = (bf16[464,256]{1,0:T(8,128)(2,1)S(1)}, bf16[464,256]{1,0:T(8,128)(2,1)S(1)}, u32[]{:S(2)}, u32[]{:S(2)}) collective-permute-start(bf16[464,256]{1,0:T(8,128)(2,1)S(1)} %get-tuple-element.28), channel_id=1, source_target_pairs={{0,1},{1,2},{2,3},{3,0},{4,5},{5,6},{6,7},{7,4},{8,9},{9,10},{10,1... | collective-permute-start | bytes 712712 | tf_op jit(solution)/shard_map/last_sum/ppermute | solution.py:321
  148.0 5.1 %collective-permute-start.4 = (bf16[464,256]{1,0:T(8,128)(2,1)S(1)}, bf16[464,256]{1,0:T(8,128)(2,1)S(1)}, u32[]{:S(2)}, u32[]{:S(2)}) collective-permute-start(bf16[464,256]{1,0:T(8,128)(2,1)S(1)} %get-tuple-element.29), channel_id=1, source_target_pairs={{0,2},{1,3},{2,0},{3,1},{4,6},{5,7},{6,4},{7,5},{8,10},{9,11},{10,... | collective-permute-start | bytes 712712 | tf_op jit(solution)/shard_map/last_sum/ppermute | solution.py:321
  153.1 1.9 %collective-permute-start.5 = (bf16[464,256]{1,0:T(8,128)(2,1)S(1)}, bf16[464,256]{1,0:T(8,128)(2,1)S(1)}, u32[]{:S(2)}, u32[]{:S(2)}) collective-permute-start(bf16[464,256]{1,0:T(8,128)(2,1)S(1)} %get-tuple-element.30), channel_id=1, source_target_pairs={{0,3},{1,0},{2,1},{3,2},{4,7},{5,4},{6,5},{7,6},{8,11},{9,8},{10,9... | collective-permute-start | bytes 712712 | tf_op jit(solution)/shard_map/last_sum/ppermute | solution.py:321
  155.0 16.5 %all-to-all-done.5 = bf16[128,8,384]{2,1,0:T(8,128)(2,1)} async-done(((bf16[128,8,384]{2,1,0:T(8,128)(2,1)}), bf16[128,8,384]{2,1,0:T(8,128)(2,1)}, u32[]{:S(2)}, u32[]{:S(2)}) %all-to-all-start.5) | async-done | bytes 786464 | tf_op jit(solution)/shard_map/weight_grads/all_to_all | solution.py:22
  171.6 1.3 convert_reduce_fusion
  174.1 3.5 %all-to-all-start.6 = ((f32[4,7,128]{2,1,0:T(8,128)}), f32[4,7,128]{2,1,0:T(8,128)S(1)}, u32[]{:S(2)}, u32[]{:S(2)}) async-start(f32[4,7,128]{2,1,0:T(8,128)} %broadcast_in_dim.74), calls=%async_computation.6 | async-start | bytes 32768 | tf_op jit(solution)/shard_map/key_grads/all_to_all | solution.py:22
  177.6 1.4 last.1
  179.0 2.8 %all-to-all-done.6 = f32[4,7,128]{2,1,0:T(8,128)S(1)} async-done(((f32[4,7,128]{2,1,0:T(8,128)}), f32[4,7,128]{2,1,0:T(8,128)S(1)}, u32[]{:S(2)}, u32[]{:S(2)}) %all-to-all-start.6) | async-done | bytes 14368 | tf_op jit(solution)/shard_map/key_grads/all_to_all | solution.py:22
  (58 shorter events, 12.7 us)
Async XLA Ops:
  0.6 42.6 %copy-start.13 = (s32[256]{0:T(256)S(1)}, s32[256]{0:T(256)}, u32[]{:S(2)}) copy-start(s32[256]{0:T(256)} %param.18) | copy-start | bytes 3076
  0.6 0.9 copy-start.9
  43.7 32.2 %copy-start.15 = (s32[192]{0:T(256)S(1)}, s32[192]{0:T(256)}, u32[]{:S(2)}) copy-start(s32[192]{0:T(256)} %param.16) | copy-start | bytes 2308
  43.7 45.7 %copy-start = (bf16[2,896,640]{2,1,0:T(8,128)(2,1)S(1)}, bf16[2,896,640]{2,1,0:T(8,128)(2,1)}, u32[]{:S(2)}) copy-start(bf16[2,896,640]{2,1,0:T(8,128)(2,1)} %gate_up_ref.1) | copy-start | bytes 6881284
  70.7 0.9 copy-start.5
  71.7 17.8 %all-to-all-start.2 = ((bf16[4,448,256]{2,1,0:T(8,128)(2,1)}), bf16[4,448,256]{2,1,0:T(8,128)(2,1)S(1)}, u32[]{:S(2)}, u32[]{:S(2)}) async-start(bf16[4,448,256]{2,1,0:T(8,128)(2,1)} %copy-done.5), calls=%async_computation.2 | async-start | bytes 1835008 | tf_op jit(solution)/shard_map/gather_one/all_to_all | solution.py:22
  89.4 1.3 copy-start.3
  94.1 0.9 copy-start.4
  95.1 3.7 %copy-start.16 = (s32[192]{0:T(256)S(1)}, s32[192]{0:T(256)}, u32[]{:S(2)}) copy-start(s32[192]{0:T(256)} %param.17) | copy-start | bytes 2308
  95.1 16.9 %copy-start.2 = (bf16[896,256]{1,0:T(8,128)(2,1)S(1)}, bf16[896,256]{1,0:T(8,128)(2,1)}, u32[]{:S(2)}) copy-start(bf16[896,256]{1,0:T(8,128)(2,1)} %copy-done.1) | copy-start | bytes 1376260
  95.1 16.9 %all-to-all-start.3 = ((bf16[4,464,256]{2,1,0:T(8,128)(2,1)}), bf16[4,464,256]{2,1,0:T(8,128)(2,1)S(1)}, u32[]{:S(2)}, u32[]{:S(2)}) async-start(bf16[4,464,256]{2,1,0:T(8,128)(2,1)} %copy-done.4), calls=%async_computation.3 | async-start | bytes 1900544 | tf_op jit(solution)/shard_map/sum_one/all_to_all | solution.py:22
  111.9 5.3 %copy-start.14 = (bf16[2,224,128]{2,1,0:T(8,128)(2,1)S(1)}, bf16[2,224,128]{2,1,0:T(8,128)(2,1)}, u32[]{:S(2)}) copy-start(bf16[2,224,128]{2,1,0:T(8,128)(2,1)} %param.20) | copy-start | bytes 344068
  111.9 19.7 %copy-start.6 = (bf16[896,128]{1,0:T(8,128)(2,1)S(1)}, bf16[896,128]{1,0:T(8,128)(2,1)}, u32[]{:S(2)}) copy-start(bf16[896,128]{1,0:T(8,128)(2,1)} %param.19) | copy-start | bytes 688132
  112.0 19.7 %copy-start.7 = (bf16[128,896]{1,0:T(8,128)(2,1)S(1)}, bf16[128,896]{1,0:T(8,128)(2,1)}, u32[]{:S(2)}) copy-start(bf16[128,896]{1,0:T(8,128)(2,1)} %proj_ref.1) | copy-start | bytes 688132
  113.7 18.0 %all-to-all-start.4 = ((bf16[4,448,256]{2,1,0:T(8,128)(2,1)}), bf16[4,448,256]{2,1,0:T(8,128)(2,1)S(1)}, u32[]{:S(2)}, u32[]{:S(2)}) async-start(bf16[4,448,256]{2,1,0:T(8,128)(2,1)} %get-tuple-element.26), calls=%async_computation.4 | async-start | bytes 1835008 | tf_op jit(solution)/shard_map/gather_two/all_to_all | solution.py:22
  117.2 11.7 %collective-permute-start.2 = (bf16[224,128]{1,0:T(8,128)(2,1)S(1)}, bf16[224,128]{1,0:T(8,128)(2,1)S(1)}, u32[]{:S(2)}, u32[]{:S(2)}) collective-permute-start(bf16[224,128]{1,0:T(8,128)(2,1)S(1)} %get-tuple-element.61), channel_id=1, source_target_pairs={{0,3},{1,0},{2,1},{3,2},{4,7},{5,4},{6,5},{7,6},{8,11},{9,8},{10,9... | collective-permute-start | bytes 172040 | tf_op jit(solution)/shard_map/weights/ppermute | solution.py:321
  121.8 8.1 %collective-permute-start = (bf16[224,128]{1,0:T(8,128)(2,1)S(1)}, bf16[224,128]{1,0:T(8,128)(2,1)S(1)}, u32[]{:S(2)}, u32[]{:S(2)}) collective-permute-start(bf16[224,128]{1,0:T(8,128)(2,1)S(1)} %get-tuple-element.62), channel_id=1, source_target_pairs={{0,1},{1,2},{2,3},{3,0},{4,5},{5,6},{6,7},{7,4},{8,9},{9,10},{10,1... | collective-permute-start | bytes 172040 | tf_op jit(solution)/shard_map/weights/ppermute | solution.py:321
  123.7 8.0 %collective-permute-start.1 = (bf16[224,128]{1,0:T(8,128)(2,1)S(1)}, bf16[224,128]{1,0:T(8,128)(2,1)S(1)}, u32[]{:S(2)}, u32[]{:S(2)}) collective-permute-start(bf16[224,128]{1,0:T(8,128)(2,1)S(1)} %get-tuple-element.64), channel_id=1, source_target_pairs={{0,2},{1,3},{2,0},{3,1},{4,6},{5,7},{6,4},{7,5},{8,10},{9,11},{10,... | collective-permute-start | bytes 172040 | tf_op jit(solution)/shard_map/weights/ppermute | solution.py:321
  136.9 40.7 %copy-start.8 = (bf16[224,256]{1,0:T(8,128)(2,1)S(1)}, bf16[224,256]{1,0:T(8,128)(2,1)}, u32[]{:S(2)}) copy-start(bf16[224,256]{1,0:T(8,128)(2,1)} %get-tuple-element.31.refs_5_) | copy-start | bytes 344068
  136.9 34.7 %all-to-all-start.5 = ((bf16[128,8,384]{2,1,0:T(8,128)(2,1)}), bf16[128,8,384]{2,1,0:T(8,128)(2,1)}, u32[]{:S(2)}, u32[]{:S(2)}) async-start(bf16[128,8,384]{2,1,0:T(8,128)(2,1)} %bitcast.19), calls=%async_computation.5 | async-start | bytes 1572864 | tf_op jit(solution)/shard_map/weight_grads/all_to_all | solution.py:22
  145.8 31.8 %collective-permute-start.3 = (bf16[464,256]{1,0:T(8,128)(2,1)S(1)}, bf16[464,256]{1,0:T(8,128)(2,1)S(1)}, u32[]{:S(2)}, u32[]{:S(2)}) collective-permute-start(bf16[464,256]{1,0:T(8,128)(2,1)S(1)} %get-tuple-element.28), channel_id=1, source_target_pairs={{0,1},{1,2},{2,3},{3,0},{4,5},{5,6},{6,7},{7,4},{8,9},{9,10},{10,1... | collective-permute-start | bytes 712712 | tf_op jit(solution)/shard_map/last_sum/ppermute | solution.py:321
  148.0 29.6 %collective-permute-start.4 = (bf16[464,256]{1,0:T(8,128)(2,1)S(1)}, bf16[464,256]{1,0:T(8,128)(2,1)S(1)}, u32[]{:S(2)}, u32[]{:S(2)}) collective-permute-start(bf16[464,256]{1,0:T(8,128)(2,1)S(1)} %get-tuple-element.29), channel_id=1, source_target_pairs={{0,2},{1,3},{2,0},{3,1},{4,6},{5,7},{6,4},{7,5},{8,10},{9,11},{10,... | collective-permute-start | bytes 712712 | tf_op jit(solution)/shard_map/last_sum/ppermute | solution.py:321
  153.1 24.5 %collective-permute-start.5 = (bf16[464,256]{1,0:T(8,128)(2,1)S(1)}, bf16[464,256]{1,0:T(8,128)(2,1)S(1)}, u32[]{:S(2)}, u32[]{:S(2)}) collective-permute-start(bf16[464,256]{1,0:T(8,128)(2,1)S(1)} %get-tuple-element.30), channel_id=1, source_target_pairs={{0,3},{1,0},{2,1},{3,2},{4,7},{5,4},{6,5},{7,6},{8,11},{9,8},{10,9... | collective-permute-start | bytes 712712 | tf_op jit(solution)/shard_map/last_sum/ppermute | solution.py:321
  174.1 7.8 %all-to-all-start.6 = ((f32[4,7,128]{2,1,0:T(8,128)}), f32[4,7,128]{2,1,0:T(8,128)S(1)}, u32[]{:S(2)}, u32[]{:S(2)}) async-start(f32[4,7,128]{2,1,0:T(8,128)} %broadcast_in_dim.74), calls=%async_computation.6 | async-start | bytes 32768 | tf_op jit(solution)/shard_map/key_grads/all_to_all | solution.py:22
  (4 other events, 3.5 us)

commit v2 on v1

--- a/solution.py
+++ b/solution.py
@@ -49,16 +49,23 @@
     return jnp.stack([limit[0], limit[1], same, lax.axis_index("mp")]).astype(jnp.int32)
 
 
-def call(kernel, out_shape, *args, scratch=(), smem=0, name=None):
-    specs = [pl.BlockSpec(memory_space=pltpu.SMEM)] * smem
-    specs += [pl.BlockSpec(memory_space=pltpu.VMEM)] * (len(args) - smem)
+def call(kernel, out_shape, *args, scratch=(), smem=0, far=(), far_out=(), mib=16, name=None):
+    spaces = [pltpu.SMEM] * smem + [pltpu.VMEM] * (len(args) - smem)
+    for i in far:
+        spaces[i] = pltpu.HBM
+    one = not isinstance(out_shape, tuple)
+    outs = [pltpu.VMEM] * (1 if one else len(out_shape))
+    for i in far_out:
+        outs[i] = pltpu.HBM
+    outs = [pl.BlockSpec(memory_space=o) for o in outs]
     return pl.pallas_call(
         kernel,
-        in_specs=specs,
+        in_specs=[pl.BlockSpec(memory_space=s) for s in spaces],
+        out_specs=outs[0] if one else tuple(outs),
         out_shape=out_shape,
         scratch_shapes=scratch,
         interpret=INTERPRET,
-        compiler_params=pltpu.CompilerParams(vmem_limit_bytes=48 * 2**20),
+        compiler_params=pltpu.CompilerParams(vmem_limit_bytes=mib * 2**20),
         name=name,
     )(*args)
 
@@ -72,12 +79,12 @@
     return jnp.concatenate([ref[pl.ds(j, 1), at, :][0] for j in range(ref.shape[0])], axis=1)
 
 
-def pack_kernel(*refs):
-    *streams, out_ref, rows_ref = refs
-    for k, stream in enumerate(streams):
-        width, count = stream.shape
-        gap = jnp.zeros((out_ref.shape[1] - width, count), F32)
-        rows = jnp.concatenate([stream[...].astype(F32), gap], axis=0).T
+def pack_kernel(streams_ref, out_ref, rows_ref):
+    width = streams_ref.shape[0] // 4
+    gap = jnp.zeros((out_ref.shape[1] - width, streams_ref.shape[1]), F32)
+    for k in range(4):
+        stream = streams_ref[k * width : (k + 1) * width, :].astype(F32)
+        rows = jnp.concatenate([stream, gap], axis=0).T
         for t in range(2):
             at = pl.ds(4 * t + k, BLOCK, stride=8)
             put(rows_ref, at, rows[t * BLOCK : (t + 1) * BLOCK])
@@ -104,8 +111,7 @@
         at = slice(k * width, (k + 1) * width)
         kept_ref[at, :] = stream
         if k < 2:
-            for m in range(MP):
-                send_ref[m, at, :] = stream
+            send_ref[at, :] = stream
 
 
 def to_slots(streams, plan):
@@ -116,7 +122,9 @@
     rows = 8 * BLOCK
     shape = jax.ShapeDtypeStruct((rows, lanes), BF16)
     scratch = pltpu.VMEM((lanes // 128, rows, 128), F32)
-    sent = call(pack_kernel, shape, *streams, scratch=[scratch], name="pack")
+    sent = call(
+        pack_kernel, shape, jnp.concatenate(streams, axis=0), scratch=[scratch], name="pack"
+    )
     with jax.named_scope("hop_one"):
         held = exchange(sent.reshape(peers, share * 8, lanes), SEQ)
     held = held.reshape(peers, share, 8, lanes)
@@ -138,7 +146,7 @@
     return call(
         unpack_kernel,
         (
-            jax.ShapeDtypeStruct((MP, 2 * width, 2 * BLOCK), BF16),
+            jax.ShapeDtypeStruct((2 * width, 2 * BLOCK), BF16),
             jax.ShapeDtypeStruct((4 * width, 2 * BLOCK), BF16),
         ),
         owned.reshape(rows, lanes),
@@ -220,9 +228,8 @@
     second_ref[...] = second
     first_cot_ref[...] = cot
     masked = jnp.where(live_columns(facts_ref, cot.shape), cot.astype(F32), 0.0).astype(BF16)
-    for m in range(parts):
-        send_ref[m, :width, :] = second
-        send_ref[m, width:, :] = masked
+    send_ref[:width, :] = second
+    send_ref[width:, :] = masked
 
 
 def last_kernel(
@@ -250,7 +257,7 @@
     width = both // 2
     pieces, refs = refs[:parts], refs[parts:]
     out_refs, refs = refs[:parts], refs[parts:]
-    grads_ref, inverse_ref, second_ref, cot_ref, keyval_ref, turned_ref = refs
+    far_ref, inverse_ref, second_ref, cot_ref, keyval_ref, turned_ref, grads_ref, sem = refs
     me = facts_ref[3]
     for k in range(parts):
         keyval_ref[(me + parts - k) % parts] = pieces[k][...]
@@ -304,6 +311,8 @@
         grads.append(dot(cot_ref[at, :], heads, NN))
         grads = jnp.concatenate(grads, axis=1).astype(BF16)
         grads_ref[to, :] = dot(pick, grads, NN).astype(BF16)
+    copy = pltpu.make_async_copy(grads_ref, far_ref, sem)
+    copy.start()
     turned_ref[...] = proj_ref[...].T.reshape(turned_ref.shape)
     inner = row_sums(
         d_query.astype(F32) * query.astype(F32) + d_keyval.astype(F32) * wide, parts * width
@@ -315,6 +324,23 @@
             dot(query_ref[m], d_query, NT) + dot(keyval_ref[m], d_keyval, NT)
         ).astype(BF16)
         out_refs[k][both:, :] = inner
+    copy.wait()
+
+
+def finish_kernel(grads_ref, query_ref, out_ref, own_ref):
+    total = jnp.sum(grads_ref[...].astype(F32), axis=0)
+    total = total.reshape(-1, 8, total.shape[1])[:, :7].reshape(-1, total.shape[1])
+    query_ref[...] = total[:, :128]
+    out_ref[...] = total[:, 256:]
+    for m in range(MP):
+        own_ref[m] = total[:, 128:256]
+
+
+def pair_kernel(shares_ref, out_ref):
+    groups = out_ref.shape[1]
+    per = MP // groups
+    for g in range(groups):
+        out_ref[:, g, :] = shares_ref[g * per] + shares_ref[g * per + 1]
 
 
 def turn(value, by):
@@ -347,11 +373,12 @@
             pieces.append(turn(kv_weight[((me + k) & 3) >> 1], k))
 
     send, kept = to_slots((y_first.T, grad_second.T, y_second.T, grad_first.T), plan)
+    send, facts, pieces = lax.optimization_barrier((send, facts, pieces))
     stream = jax.ShapeDtypeStruct((width, count), BF16)
     line = jax.ShapeDtypeStruct((1, count), F32)
     part = jax.ShapeDtypeStruct((2 * width + PAD, count), BF16)
     with jax.named_scope("gather_one"):
-        rows = exchange(send, "mp")
+        rows = lax.all_gather(send, "mp", axis=0)
     whole = pltpu.VMEM((MP * width, count), BF16)
     parts, r_one = call(
         feed_forward_kernel,
@@ -366,7 +393,7 @@
         parts = exchange(parts, "mp")
     second_in, first_cot, send = call(
         middle_kernel,
-        (stream, stream, jax.ShapeDtypeStruct((MP, 2 * width, count), BF16)),
+        (stream, stream, jax.ShapeDtypeStruct((2 * width, count), BF16)),
         facts,
         parts,
         kept,
@@ -375,7 +402,7 @@
         name="middle",
     )
     with jax.named_scope("gather_two"):
-        rows = exchange(send, "mp")
+        rows = lax.all_gather(send, "mp", axis=0)
     *parts, grads, r_two = call(
         attention_kernel,
         (*[part] * MP, jax.ShapeDtypeStruct((8 * BLOCK, 384), BF16), line),
@@ -384,7 +411,14 @@
         q_weight.reshape(MP, width, -1),
         out_weight,
         *pieces,
-        scratch=[whole, whole] + [pltpu.VMEM((MP, width, 128), BF16)] * 2,
+        scratch=[
+            whole,
+            whole,
+            *[pltpu.VMEM((MP, width, 128), BF16)] * 2,
+            pltpu.VMEM((8 * BLOCK, 384), BF16),
+            pltpu.SemaphoreType.DMA,
+        ],
+        far_out=(MP,),
         smem=1,
         name="attention",
     )
@@ -395,20 +429,29 @@
     first_in, second_cot = call(
         last_kernel, (stream, stream), facts, *parts, kept, second_in, r_two, smem=1, name="last"
     )
-    summed = jnp.sum(grads.astype(F32), axis=0).reshape(-1, 8, grads.shape[2])[:, :7]
-    summed = summed.reshape(-1, grads.shape[2])
-    own = summed[:, 128:256]
+    share = jax.ShapeDtypeStruct((7 * BLOCK // seq_size, 128), F32)
+    query_grad, out_grad, own = call(
+        finish_kernel,
+        (share, share, jax.ShapeDtypeStruct((MP, *share.shape), F32)),
+        grads,
+        name="finish",
+    )
     with jax.named_scope("key_grads"):
-        shares = exchange(jnp.broadcast_to(own, (MP, *own.shape)), "mp")
-    kv_grad = shares.reshape(groups, MP // groups, *own.shape).sum(axis=1)
+        shares = exchange(own, "mp")
+    kv_grad = call(
+        pair_kernel,
+        jax.ShapeDtypeStruct((shares.shape[1], groups, 128), F32),
+        shares,
+        name="pair",
+    )
     return (
         first_in.T,
         second_in.T,
         first_cot.T,
         second_cot.T,
-        summed[:, :128],
-        kv_grad,
-        summed[:, 256:].T,
+        query_grad,
+        kv_grad.transpose(1, 0, 2),
+        out_grad.T,
     )
 
 

time: 184 us -> 165 us (0.90)
  blocking collectives: 64.6 us -> 39.6 us
  starting transfers between devices: 43.1 us -> 56.9 us
  local copies, waits for them, and re-layouts: 9.98 us -> 1.31 us
  Pallas kernels: 12.7 us -> 15.3 us
    all_to_all x2 -> x1, blocking collectives: 64.6 us -> 14.8 us  [exchange(): return lax.all_to_all(value, axis, split_axis=0, concat_axis=0, tiled=True)]
    all_gather x0 -> x2, blocking collectives: none -> 24.7 us  [shards(): rows = lax.all_gather(send, 'mp', axis=0)]
    all_to_all x5 -> x4, starting transfers between devices: 23.6 us -> 37.9 us  [exchange(): return lax.all_to_all(value, axis, split_axis=0, concat_axis=0, tiled=True)]
    unnamed x35 -> x18, local copies, waits for them, and re-layouts: 8.16 us -> 0.05 us
    ppermute x6, waiting for transfers between devices: 4.12 us -> 0.02 us  [turn(): return lax.ppermute(value, 'mp', [(i, (i + by) % MP) for i in range(MP)])]
    all_to_all x5 -> x4, waiting for transfers between devices: 43.6 us -> 47.4 us  [exchange(): return lax.all_to_all(value, axis, split_axis=0, concat_axis=0, tiled=True)]
    pallas_call x7 -> x9, Pallas kernels: 12.7 us -> 15.3 us  [call(): pl.pallas_call(kernel, in_specs=[pl.BlockSpec(memory_space=s) for s in sp...]
  transfers between devices with their start and end apart: 11 -> 10, of which waited for: 7 -> 4; matrix products, arithmetic and copies ran while one was open for 2% -> 1% of each run, Pallas kernels for 1% -> 2%
where the time goes in v2:
time: 165 us
  starting transfers between devices  56.9 us (34%)
  waiting for transfers between devices  47.4 us (29%)
  blocking collectives  39.6 us (24%)
  Pallas kernels  15.3 us (9%)
  between operations  2.22 us (1%)
  other arithmetic  1.97 us (1%)
    all_to_all x4, waiting for transfers between devices, exchange(): return lax.all_to_all(value, axis, split_axis=0, concat_axis=0, tiled=True)  47.4 us
    all_to_all x4, starting transfers between devices, exchange(): return lax.all_to_all(value, axis, split_axis=0, concat_axis=0, tiled=True)  37.9 us
    all_gather x2, blocking collectives, shards(): rows = lax.all_gather(send, 'mp', axis=0)  24.7 us
    ppermute x6, starting transfers between devices, turn(): return lax.ppermute(value, 'mp', [(i, (i + by) % MP) for i in range(MP)])  19 us
    pallas_call x9, Pallas kernels, call(): pl.pallas_call(kernel, in_specs=[pl.BlockSpec(memory_space=s) for s in sp...  15.3 us
    all_to_all x1, blocking collectives, exchange(): return lax.all_to_all(value, axis, split_axis=0, concat_axis=0, tiled=True)  14.8 us
  transfers between devices with their start and end apart: 10, of which 4 were waited for; matrix products, arithmetic and copies ran while one was open for 1% of the time, Pallas kernels for 2%

profile of v2, /device:TPU:1, one launch (start us, length us, event | category | flops | bytes accessed | tf_op | source)
XLA Modules:
  0.0 164.7 jit_solution(11209403809911271192)
XLA Ops:
  0.7 1.2 pad_maximum_fusion.streams_ref
  1.8 1.1 pack.1
  2.9 18.4 %all-to-all-start = ((bf16[128,8,256]{2,1,0:T(8,128)(2,1)}), bf16[128,8,256]{2,1,0:T(8,128)(2,1)S(1)}, u32[]{:S(2)}, u32[]{:S(2)}) async-start(bf16[128,8,256]{2,1,0:T(8,128)(2,1)} %bitcast.5), calls=%async_computation | async-start | bytes 1048576 | tf_op jit(solution)/shard_map/hop_one/all_to_all | solution.py:22
  22.0 4.5 %collective-permute-start.2 = (bf16[224,128]{1,0:T(8,128)(2,1)}, bf16[224,128]{1,0:T(8,128)(2,1)S(1)}, u32[]{:S(2)}, u32[]{:S(2)}) collective-permute-start(bf16[224,128]{1,0:T(8,128)(2,1)} %get-tuple-element.58), channel_id=1, source_target_pairs={{0,3},{1,0},{2,1},{3,2},{4,7},{5,4},{6,5},{7,6},{8,11},{9,8},{10,9... | collective-permute-start | bytes 172040 | tf_op jit(solution)/shard_map/weights/ppermute | solution.py:347
  26.5 1.9 %collective-permute-start = (bf16[224,128]{1,0:T(8,128)(2,1)}, bf16[224,128]{1,0:T(8,128)(2,1)S(1)}, u32[]{:S(2)}, u32[]{:S(2)}) collective-permute-start(bf16[224,128]{1,0:T(8,128)(2,1)} %get-tuple-element.59), channel_id=1, source_target_pairs={{0,1},{1,2},{2,3},{3,0},{4,5},{5,6},{6,7},{7,4},{8,9},{9,10},{10,1... | collective-permute-start | bytes 172040 | tf_op jit(solution)/shard_map/weights/ppermute | solution.py:347
  28.5 3.6 %collective-permute-start.1 = (bf16[224,128]{1,0:T(8,128)(2,1)}, bf16[224,128]{1,0:T(8,128)(2,1)S(1)}, u32[]{:S(2)}, u32[]{:S(2)}) collective-permute-start(bf16[224,128]{1,0:T(8,128)(2,1)} %get-tuple-element.61), channel_id=1, source_target_pairs={{0,2},{1,3},{2,0},{3,1},{4,6},{5,7},{6,4},{7,5},{8,10},{9,11},{10,... | collective-permute-start | bytes 172040 | tf_op jit(solution)/shard_map/weights/ppermute | solution.py:347
  32.3 9.6 %all-to-all-done = bf16[128,8,256]{2,1,0:T(8,128)(2,1)S(1)} async-done(((bf16[128,8,256]{2,1,0:T(8,128)(2,1)}), bf16[128,8,256]{2,1,0:T(8,128)(2,1)S(1)}, u32[]{:S(2)}, u32[]{:S(2)}) %all-to-all-start) | async-done | bytes 524320 | tf_op jit(solution)/shard_map/hop_one/all_to_all | solution.py:22
  41.9 1.2 reorder.1
  43.1 5.4 %all-to-all-start.1 = ((bf16[128,8,256]{2,1,0:T(8,128)(2,1)}), bf16[128,8,256]{2,1,0:T(8,128)(2,1)S(1)}, u32[]{:S(2)}, u32[]{:S(2)}) async-start(bf16[128,8,256]{2,1,0:T(8,128)(2,1)} %bitcast.7), calls=%async_computation.1 | async-start | bytes 1048576 | tf_op jit(solution)/shard_map/hop_two/all_to_all | solution.py:22
  51.1 18.0 %all-to-all-done.1 = bf16[128,8,256]{2,1,0:T(8,128)(2,1)S(1)} async-done(((bf16[128,8,256]{2,1,0:T(8,128)(2,1)}), bf16[128,8,256]{2,1,0:T(8,128)(2,1)S(1)}, u32[]{:S(2)}, u32[]{:S(2)}) %all-to-all-start.1) | async-done | bytes 524320 | tf_op jit(solution)/shard_map/hop_two/all_to_all | solution.py:22
  69.4 13.2 %all-gather = bf16[1792,256]{1,0:T(8,128)(2,1)S(1)} all-gather(bf16[448,256]{1,0:T(8,128)(2,1)S(1)} %get-tuple-element.33), channel_id=2, replica_groups=mesh['seq_0'=8,'seq_1'=8,'seq_2'=2,'mp'=4] {'mp'}, dimensions={0}, use_global_device_ids=true | all-gather | bytes 1146880 | tf_op jit(solution)/shard_map/gather_one/all_gather | solution.py:381
  82.6 3.4 %feed_forward.1 = (bf16[4,464,256]{2,1,0:T(8,128)(2,1)S(1)}, f32[1,256]{1,0:T(1,128)S(1)}) custom-call(bf16[4,448,256]{2,1,0:T(8,128)(2,1)S(1)} %bitcast.28, bf16[2,896,640]{2,1,0:T(8,128)(2,1)S(1)} %copy-done, bf16[640,896]{1,0:T(8,128)(2,1)S(1)} %copy-done.1), custom_call_target="tpu_custom_call" | custom-call | tf_op jit(solution)/shard_map/feed_forward/pallas_call | solution.py:61
  86.1 14.8 %all_to_all.25.parts_ref = bf16[4,464,256]{2,1,0:T(8,128)(2,1)S(1)} all-to-all(bf16[4,464,256]{2,1,0:T(8,128)(2,1)S(1)} %get-tuple-element.34), channel_id=1, replica_groups=mesh['seq_0'=8,'seq_1'=8,'seq_2'=2,'mp'=4] {'mp'}, dimensions={0} | all-to-all | bytes 1900544 | tf_op jit(solution)/shard_map/sum_one/all_to_all | solution.py:22
  100.9 1.4 middle.1
  102.3 11.5 %all-gather.1 = bf16[1792,256]{1,0:T(8,128)(2,1)S(1)} all-gather(bf16[448,256]{1,0:T(8,128)(2,1)S(1)} %get-tuple-element.37), channel_id=3, replica_groups=mesh['seq_0'=8,'seq_1'=8,'seq_2'=2,'mp'=4] {'mp'}, dimensions={0}, use_global_device_ids=true | all-gather | bytes 1146880 | tf_op jit(solution)/shard_map/gather_two/all_gather | solution.py:405
  113.8 5.2 %attention.1 = (bf16[464,256]{1,0:T(8,128)(2,1)S(1)}, bf16[464,256]{1,0:T(8,128)(2,1)S(1)}, bf16[464,256]{1,0:T(8,128)(2,1)S(1)}, bf16[464,256]{1,0:T(8,128)(2,1...) custom-call(s32[4]{0:T(128)S(1)} %pad_add_fusion.facts_ref, bf16[4,448,256]{2,1,0:T(8,128)(2,1)S(1)} %bitcast.29, ...), custom_call_target="tpu_custom_call" | custom-call | tf_op jit(solution)/shard_map/attention/pallas_call | solution.py:61
  119.0 10.8 %all-to-all-start.3 = ((bf16[128,8,384]{2,1,0:T(8,128)(2,1)}), bf16[128,8,384]{2,1,0:T(8,128)(2,1)S(1)}, u32[]{:S(2)}, u32[]{:S(2)}) async-start(bf16[128,8,384]{2,1,0:T(8,128)(2,1)} %bitcast.21), calls=%async_computation.3 | async-start | bytes 1572864 | tf_op jit(solution)/shard_map/weight_grads/all_to_all | solution.py:22
  129.9 2.3 %collective-permute-start.3 = (bf16[464,256]{1,0:T(8,128)(2,1)S(1)}, bf16[464,256]{1,0:T(8,128)(2,1)S(1)}, u32[]{:S(2)}, u32[]{:S(2)}) collective-permute-start(bf16[464,256]{1,0:T(8,128)(2,1)S(1)} %get-tuple-element.43), channel_id=1, source_target_pairs={{0,1},{1,2},{2,3},{3,0},{4,5},{5,6},{6,7},{7,4},{8,9},{9,10},{10,1... | collective-permute-start | bytes 712712 | tf_op jit(solution)/shard_map/last_sum/ppermute | solution.py:347
  132.2 4.3 %collective-permute-start.4 = (bf16[464,256]{1,0:T(8,128)(2,1)S(1)}, bf16[464,256]{1,0:T(8,128)(2,1)S(1)}, u32[]{:S(2)}, u32[]{:S(2)}) collective-permute-start(bf16[464,256]{1,0:T(8,128)(2,1)S(1)} %get-tuple-element.44), channel_id=1, source_target_pairs={{0,2},{1,3},{2,0},{3,1},{4,6},{5,7},{6,4},{7,5},{8,10},{9,11},{10,... | collective-permute-start | bytes 712712 | tf_op jit(solution)/shard_map/last_sum/ppermute | solution.py:347
  136.5 2.4 %collective-permute-start.5 = (bf16[464,256]{1,0:T(8,128)(2,1)S(1)}, bf16[464,256]{1,0:T(8,128)(2,1)S(1)}, u32[]{:S(2)}, u32[]{:S(2)}) collective-permute-start(bf16[464,256]{1,0:T(8,128)(2,1)S(1)} %get-tuple-element.45), channel_id=1, source_target_pairs={{0,3},{1,0},{2,1},{3,2},{4,7},{5,4},{6,5},{7,6},{8,11},{9,8},{10,9... | collective-permute-start | bytes 712712 | tf_op jit(solution)/shard_map/last_sum/ppermute | solution.py:347
  138.9 17.1 %all-to-all-done.3.grads_ref = bf16[128,8,384]{2,1,0:T(8,128)(2,1)S(1)} async-done(((bf16[128,8,384]{2,1,0:T(8,128)(2,1)}), bf16[128,8,384]{2,1,0:T(8,128)(2,1)S(1)}, u32[]{:S(2)}, u32[]{:S(2)}) %all-to-all-start.3) | async-done | bytes 786464 | tf_op jit(solution)/shard_map/weight_grads/all_to_all | solution.py:22
  156.7 3.2 %all-to-all-start.4 = ((f32[4,7,128]{2,1,0:T(8,128)}), f32[4,7,128]{2,1,0:T(8,128)S(1)}, u32[]{:S(2)}, u32[]{:S(2)}) async-start(f32[4,7,128]{2,1,0:T(8,128)} %get-tuple-element.53), calls=%async_computation.4 | async-start | bytes 32768 | tf_op jit(solution)/shard_map/key_grads/all_to_all | solution.py:22
  160.0 1.4 last.1
  161.4 2.8 %all-to-all-done.4.shares_ref = f32[4,7,128]{2,1,0:T(8,128)S(1)} async-done(((f32[4,7,128]{2,1,0:T(8,128)}), f32[4,7,128]{2,1,0:T(8,128)S(1)}, u32[]{:S(2)}, u32[]{:S(2)}) %all-to-all-start.4) | async-done | bytes 14368 | tf_op jit(solution)/shard_map/key_grads/all_to_all | solution.py:22
  (38 shorter events, 3.8 us)
Async XLA Ops:
  0.6 20.7 %copy-start.6 = (bf16[2,224,128]{2,1,0:T(8,128)(2,1)S(1)}, bf16[2,224,128]{2,1,0:T(8,128)(2,1)}, u32[]{:S(2)}) copy-start(bf16[2,224,128]{2,1,0:T(8,128)(2,1)} %param.20) | copy-start | bytes 344068
  0.6 31.5 %copy-start.7 = (s32[192]{0:T(256)S(1)}, s32[192]{0:T(256)}, u32[]{:S(2)}) copy-start(s32[192]{0:T(256)} %param.16) | copy-start | bytes 2308
  0.7 41.2 %copy-start.5 = (s32[256]{0:T(256)S(1)}, s32[256]{0:T(256)}, u32[]{:S(2)}) copy-start(s32[256]{0:T(256)} %param.18) | copy-start | bytes 3076
  1.8 46.9 %copy-start.8 = (s32[192]{0:T(256)S(1)}, s32[192]{0:T(256)}, u32[]{:S(2)}) copy-start(s32[192]{0:T(256)} %param.17) | copy-start | bytes 2308
  2.9 39.0 %all-to-all-start = ((bf16[128,8,256]{2,1,0:T(8,128)(2,1)}), bf16[128,8,256]{2,1,0:T(8,128)(2,1)S(1)}, u32[]{:S(2)}, u32[]{:S(2)}) async-start(bf16[128,8,256]{2,1,0:T(8,128)(2,1)} %bitcast.5), calls=%async_computation | async-start | bytes 1048576 | tf_op jit(solution)/shard_map/hop_one/all_to_all | solution.py:22
  21.3 61.3 %copy-start = (bf16[2,896,640]{2,1,0:T(8,128)(2,1)S(1)}, bf16[2,896,640]{2,1,0:T(8,128)(2,1)}, u32[]{:S(2)}) copy-start(bf16[2,896,640]{2,1,0:T(8,128)(2,1)} %gate_up_ref.1) | copy-start | bytes 6881284
  22.0 47.3 %collective-permute-start.2 = (bf16[224,128]{1,0:T(8,128)(2,1)}, bf16[224,128]{1,0:T(8,128)(2,1)S(1)}, u32[]{:S(2)}, u32[]{:S(2)}) collective-permute-start(bf16[224,128]{1,0:T(8,128)(2,1)} %get-tuple-element.58), channel_id=1, source_target_pairs={{0,3},{1,0},{2,1},{3,2},{4,7},{5,4},{6,5},{7,6},{8,11},{9,8},{10,9... | collective-permute-start | bytes 172040 | tf_op jit(solution)/shard_map/weights/ppermute | solution.py:347
  26.5 42.8 %collective-permute-start = (bf16[224,128]{1,0:T(8,128)(2,1)}, bf16[224,128]{1,0:T(8,128)(2,1)S(1)}, u32[]{:S(2)}, u32[]{:S(2)}) collective-permute-start(bf16[224,128]{1,0:T(8,128)(2,1)} %get-tuple-element.59), channel_id=1, source_target_pairs={{0,1},{1,2},{2,3},{3,0},{4,5},{5,6},{6,7},{7,4},{8,9},{9,10},{10,1... | collective-permute-start | bytes 172040 | tf_op jit(solution)/shard_map/weights/ppermute | solution.py:347
  28.5 40.9 %collective-permute-start.1 = (bf16[224,128]{1,0:T(8,128)(2,1)}, bf16[224,128]{1,0:T(8,128)(2,1)S(1)}, u32[]{:S(2)}, u32[]{:S(2)}) collective-permute-start(bf16[224,128]{1,0:T(8,128)(2,1)} %get-tuple-element.61), channel_id=1, source_target_pairs={{0,2},{1,3},{2,0},{3,1},{4,6},{5,7},{6,4},{7,5},{8,10},{9,11},{10,... | collective-permute-start | bytes 172040 | tf_op jit(solution)/shard_map/weights/ppermute | solution.py:347
  43.1 26.0 %all-to-all-start.1 = ((bf16[128,8,256]{2,1,0:T(8,128)(2,1)}), bf16[128,8,256]{2,1,0:T(8,128)(2,1)S(1)}, u32[]{:S(2)}, u32[]{:S(2)}) async-start(bf16[128,8,256]{2,1,0:T(8,128)(2,1)} %bitcast.7), calls=%async_computation.1 | async-start | bytes 1048576 | tf_op jit(solution)/shard_map/hop_two/all_to_all | solution.py:22
  69.1 13.5 %copy-start.1 = (bf16[640,896]{1,0:T(8,128)(2,1)S(1)}, bf16[640,896]{1,0:T(8,128)(2,1)}, u32[]{:S(2)}) copy-start(bf16[640,896]{1,0:T(8,128)(2,1)} %down_ref.1) | copy-start | bytes 3440644
  86.0 27.8 %copy-start.2 = (bf16[896,128]{1,0:T(8,128)(2,1)S(1)}, bf16[896,128]{1,0:T(8,128)(2,1)}, u32[]{:S(2)}) copy-start(bf16[896,128]{1,0:T(8,128)(2,1)} %param.19) | copy-start | bytes 688132
  86.0 27.8 %copy-start.3 = (bf16[128,896]{1,0:T(8,128)(2,1)S(1)}, bf16[128,896]{1,0:T(8,128)(2,1)}, u32[]{:S(2)}) copy-start(bf16[128,896]{1,0:T(8,128)(2,1)} %proj_ref.1) | copy-start | bytes 688132
  113.8 46.2 %copy-start.4 = (bf16[224,256]{1,0:T(8,128)(2,1)S(1)}, bf16[224,256]{1,0:T(8,128)(2,1)}, u32[]{:S(2)}) copy-start(bf16[224,256]{1,0:T(8,128)(2,1)} %get-tuple-element.46.refs_5_) | copy-start | bytes 344068
  119.0 36.9 %all-to-all-start.3 = ((bf16[128,8,384]{2,1,0:T(8,128)(2,1)}), bf16[128,8,384]{2,1,0:T(8,128)(2,1)S(1)}, u32[]{:S(2)}, u32[]{:S(2)}) async-start(bf16[128,8,384]{2,1,0:T(8,128)(2,1)} %bitcast.21), calls=%async_computation.3 | async-start | bytes 1572864 | tf_op jit(solution)/shard_map/weight_grads/all_to_all | solution.py:22
  129.9 30.1 %collective-permute-start.3 = (bf16[464,256]{1,0:T(8,128)(2,1)S(1)}, bf16[464,256]{1,0:T(8,128)(2,1)S(1)}, u32[]{:S(2)}, u32[]{:S(2)}) collective-permute-start(bf16[464,256]{1,0:T(8,128)(2,1)S(1)} %get-tuple-element.43), channel_id=1, source_target_pairs={{0,1},{1,2},{2,3},{3,0},{4,5},{5,6},{6,7},{7,4},{8,9},{9,10},{10,1... | collective-permute-start | bytes 712712 | tf_op jit(solution)/shard_map/last_sum/ppermute | solution.py:347
  132.2 27.8 %collective-permute-start.4 = (bf16[464,256]{1,0:T(8,128)(2,1)S(1)}, bf16[464,256]{1,0:T(8,128)(2,1)S(1)}, u32[]{:S(2)}, u32[]{:S(2)}) collective-permute-start(bf16[464,256]{1,0:T(8,128)(2,1)S(1)} %get-tuple-element.44), channel_id=1, source_target_pairs={{0,2},{1,3},{2,0},{3,1},{4,6},{5,7},{6,4},{7,5},{8,10},{9,11},{10,... | collective-permute-start | bytes 712712 | tf_op jit(solution)/shard_map/last_sum/ppermute | solution.py:347
  136.5 23.5 %collective-permute-start.5 = (bf16[464,256]{1,0:T(8,128)(2,1)S(1)}, bf16[464,256]{1,0:T(8,128)(2,1)S(1)}, u32[]{:S(2)}, u32[]{:S(2)}) collective-permute-start(bf16[464,256]{1,0:T(8,128)(2,1)S(1)} %get-tuple-element.45), channel_id=1, source_target_pairs={{0,3},{1,0},{2,1},{3,2},{4,7},{5,4},{6,5},{7,6},{8,11},{9,8},{10,9... | collective-permute-start | bytes 712712 | tf_op jit(solution)/shard_map/last_sum/ppermute | solution.py:347
  156.7 7.4 %all-to-all-start.4 = ((f32[4,7,128]{2,1,0:T(8,128)}), f32[4,7,128]{2,1,0:T(8,128)S(1)}, u32[]{:S(2)}, u32[]{:S(2)}) async-start(f32[4,7,128]{2,1,0:T(8,128)} %get-tuple-element.53), calls=%async_computation.4 | async-start | bytes 32768 | tf_op jit(solution)/shard_map/key_grads/all_to_all | solution.py:22

commit v3 on v2

--- a/solution.py
+++ b/solution.py
@@ -1,3 +1,5 @@
+from functools import partial
+
 import jax
 import jax.numpy as jnp
 from jax import lax
@@ -46,7 +48,9 @@
         jnp.any(last, axis=1), jnp.sum(jnp.where(last, last_fill[None, :], 0), axis=1), BLOCK
     )
     same = (owner[0] == owner[1]).astype(jnp.int32)
-    return jnp.stack([limit[0], limit[1], same, lax.axis_index("mp")]).astype(jnp.int32)
+    return jnp.stack([limit[0], limit[1], same, lax.axis_index("mp"), lax.axis_index("seq_2")]).astype(
+        jnp.int32
+    )
 
 
 def call(kernel, out_shape, *args, scratch=(), smem=0, far=(), far_out=(), mib=16, name=None):
@@ -114,8 +118,13 @@
             send_ref[at, :] = stream
 
 
-def to_slots(streams, plan):
+def turn(value, by):
+    return lax.ppermute(value, "mp", [(i, (i + by) % MP) for i in range(MP)])
+
+
+def to_slots(streams, kv_weight, *tables):
     peers = lax.axis_size(SEQ)
+    plan = tables[-1]
     share = BLOCK // peers
     width = streams[0].shape[0]
     lanes = -(-width // 128) * 128
@@ -127,6 +136,13 @@
     )
     with jax.named_scope("hop_one"):
         held = exchange(sent.reshape(peers, share * 8, lanes), SEQ)
+    slots = lax.axis_index(SEQ) * 2 + jnp.arange(2, dtype=jnp.int32)
+    facts = slot_facts(*tables, slots)
+    with jax.named_scope("weights"):
+        me = lax.axis_index("mp")
+        pieces = [kv_weight[me >> 1]]
+        for k in range(1, MP):
+            pieces.append(turn(kv_weight[((me + k) & 3) >> 1], k))
     held = held.reshape(peers, share, 8, lanes)
     placed = []
     for r in range(share):
@@ -143,7 +159,7 @@
     placed = placed[0] if share == 1 else jnp.stack(placed, axis=1).reshape(peers, -1, lanes)
     with jax.named_scope("hop_two"):
         owned = exchange(placed, SEQ)
-    return call(
+    return facts, pieces, *call(
         unpack_kernel,
         (
             jax.ShapeDtypeStruct((2 * width, 2 * BLOCK), BF16),
@@ -252,12 +268,12 @@
     cot_ref[...] = (cot + (d_norm - normed * inner) * inverse).astype(BF16)
 
 
-def attention_kernel(facts_ref, rows_ref, query_ref, proj_ref, *refs):
+def attention_kernel(groups, facts_ref, rows_ref, query_ref, proj_ref, *refs):
     parts, both, count = rows_ref.shape
     width = both // 2
     pieces, refs = refs[:parts], refs[parts:]
-    out_refs, refs = refs[:parts], refs[parts:]
-    far_ref, inverse_ref, second_ref, cot_ref, keyval_ref, turned_ref, grads_ref, sem = refs
+    kept_ref, given_ref, makings_ref, keyval_ref, inner_ref, inverse_ref = refs[:6]
+    second_ref, cot_ref, grads_ref = refs[6:]
     me = facts_ref[3]
     for k in range(parts):
         keyval_ref[(me + parts - k) % parts] = pieces[k][...]
@@ -301,30 +317,52 @@
     d_key = d_key + pltpu.roll(d_key, half, 1)
     d_value = d_value + pltpu.roll(d_value, half, 1)
     d_keyval = jnp.where(low, d_key, d_value).astype(BF16)
-    spread = lax.broadcasted_iota(jnp.int32, (8 * width // 7, width), 0)
-    source = jnp.where(spread % 8 < 7, 7 * (spread // 8) + spread % 8, -1)
+    makings_ref[0] = heads
+    makings_ref[1] = d_query
+    makings_ref[2] = d_keyval
+    inner_ref[...] = row_sums(
+        d_query.astype(F32) * query.astype(F32) + d_keyval.astype(F32) * wide, parts * width
+    )
+    lines = 8 * width // 7
+    spread = lax.broadcasted_iota(jnp.int32, (lines, width), 0)
+    core = (spread >= lines // 2).astype(jnp.int32)
+    place = (spread - core * (lines // 2)) // 8
+    group = (2 * (place // groups) + core) * groups + place % groups
+    source = jnp.where(spread % 8 < 7, 7 * group + spread % 8, -1)
     pick = (lax.broadcasted_iota(jnp.int32, source.shape, 1) == source).astype(BF16)
     for m in range(parts):
         at = slice(m * width, (m + 1) * width)
-        to = slice(m * pick.shape[0], (m + 1) * pick.shape[0])
         grads = [dot(normed[at], d_query, NN), dot(normed[at], d_keyval, NN)]
         grads.append(dot(cot_ref[at, :], heads, NN))
         grads = jnp.concatenate(grads, axis=1).astype(BF16)
-        grads_ref[to, :] = dot(pick, grads, NN).astype(BF16)
-    copy = pltpu.make_async_copy(grads_ref, far_ref, sem)
-    copy.start()
+        grads = dot(pick, grads, NN).astype(BF16)
+        to = slice(m * (lines // 2), (m + 1) * (lines // 2))
+        for c in range(2):
+            grads_ref[c, to, :] = grads[c * (lines // 2) : (c + 1) * (lines // 2)]
+    kept_ref[...] = grads_ref[facts_ref[4]]
+    given_ref[...] = grads_ref[1 - facts_ref[4]]
+
+
+def pieces_kernel(
+    facts_ref, makings_ref, keyval_ref, inner_ref, query_ref, proj_ref, *refs
+):
+    parts, width, _ = query_ref.shape
+    both = 2 * width
+    out_refs, turned_ref = refs[:parts], refs[parts]
+    me = facts_ref[3]
+    heads, d_query, d_keyval = makings_ref[0], makings_ref[1], makings_ref[2]
     turned_ref[...] = proj_ref[...].T.reshape(turned_ref.shape)
-    inner = row_sums(
-        d_query.astype(F32) * query.astype(F32) + d_keyval.astype(F32) * wide, parts * width
-    )
     for k in range(parts):
         m = (me + k) % parts
         out_refs[k][:width, :] = dot(turned_ref[m], heads, NT).astype(BF16)
         out_refs[k][width:both, :] = (
             dot(query_ref[m], d_query, NT) + dot(keyval_ref[m], d_keyval, NT)
         ).astype(BF16)
-        out_refs[k][both:, :] = inner
-    copy.wait()
+        out_refs[k][both:, :] = inner_ref[...]
+
+
+def add_kernel(left_ref, right_ref, out_ref):
+    out_ref[...] = (left_ref[...].astype(F32) + right_ref[...].astype(F32)).astype(BF16)
 
 
 def finish_kernel(grads_ref, query_ref, out_ref, own_ref):
@@ -341,10 +379,6 @@
     per = MP // groups
     for g in range(groups):
         out_ref[:, g, :] = shares_ref[g * per] + shares_ref[g * per + 1]
-
-
-def turn(value, by):
-    return lax.ppermute(value, "mp", [(i, (i + by) % MP) for i in range(MP)])
 
 
 def shards(
@@ -363,16 +397,9 @@
 ):
     count, width = y_first.shape
     seq_size = lax.axis_size(SEQ)
-    me = lax.axis_index("mp")
-    slots = lax.axis_index(SEQ) * 2 + jnp.arange(2, dtype=jnp.int32)
-    facts = slot_facts(doc_blocks, last_fill, plan, slots)
     groups = kv_weight.shape[0]
-    with jax.named_scope("weights"):
-        pieces = [kv_weight[me >> 1]]
-        for k in range(1, MP):
-            pieces.append(turn(kv_weight[((me + k) & 3) >> 1], k))
-
-    send, kept = to_slots((y_first.T, grad_second.T, y_second.T, grad_first.T), plan)
+    streams = (y_first.T, grad_second.T, y_second.T, grad_first.T)
+    facts, pieces, send, kept = to_slots(streams, kv_weight, doc_blocks, last_fill, plan)
     send, facts, pieces = lax.optimization_barrier((send, facts, pieces))
     stream = jax.ShapeDtypeStruct((width, count), BF16)
     line = jax.ShapeDtypeStruct((1, count), F32)
@@ -403,27 +430,45 @@
     )
     with jax.named_scope("gather_two"):
         rows = lax.all_gather(send, "mp", axis=0)
-    *parts, grads, r_two = call(
-        attention_kernel,
-        (*[part] * MP, jax.ShapeDtypeStruct((8 * BLOCK, 384), BF16), line),
+    query = q_weight.reshape(MP, width, -1)
+    half = jax.ShapeDtypeStruct((4 * BLOCK, 384), BF16)
+    kept_grads, given, makings, keyval, inner, r_two = call(
+        partial(attention_kernel, BLOCK // seq_size),
+        (
+            half,
+            half,
+            jax.ShapeDtypeStruct((3, count, 128), BF16),
+            jax.ShapeDtypeStruct((MP, width, 128), BF16),
+            jax.ShapeDtypeStruct((PAD, count), BF16),
+            line,
+        ),
         facts,
         rows,
-        q_weight.reshape(MP, width, -1),
+        query,
         out_weight,
         *pieces,
-        scratch=[
-            whole,
-            whole,
-            *[pltpu.VMEM((MP, width, 128), BF16)] * 2,
-            pltpu.VMEM((8 * BLOCK, 384), BF16),
-            pltpu.SemaphoreType.DMA,
-        ],
-        far_out=(MP,),
+        scratch=[whole, whole, pltpu.VMEM((2, *half.shape), BF16)],
         smem=1,
         name="attention",
     )
+    with jax.named_scope("core_sum"):
+        given = lax.ppermute(given, "seq_2", [(0, 1), (1, 0)])
+    grads = call(add_kernel, half, kept_grads, given, name="add")
     with jax.named_scope("weight_grads"):
-        grads = exchange(grads.reshape(seq_size, -1, grads.shape[1]), SEQ)
+        grads = exchange(grads.reshape(seq_size // 2, -1, grads.shape[1]), SEQ[:2])
+    parts = call(
+        pieces_kernel,
+        (part,) * MP,
+        facts,
+        makings,
+        keyval,
+        inner,
+        query,
+        out_weight,
+        scratch=[pltpu.VMEM((MP, width, 128), BF16)],
+        smem=1,
+        name="pieces",
+    )
     with jax.named_scope("last_sum"):
         parts = [parts[0]] + [turn(parts[k], k) for k in range(1, MP)]
     first_in, second_cot = call(

time: 165 us -> 159 us (0.964); the launches traced: 165 us -> 156 us
  waiting for transfers between devices: 47.4 us -> 36.9 us
    all_to_all x4, waiting for transfers between devices: 47.4 us -> 35.6 us  [exchange(): return lax.all_to_all(value, axis, split_axis=0, concat_axis=0, tiled=True)]
    ppermute x0 -> x1, starting transfers between devices: none -> 7.53 us  [shards(): given = lax.ppermute(given, 'seq_2', [(0, 1), (1, 0)])]
    all_to_all x4, starting transfers between devices: 37.9 us -> 31.7 us  [exchange(): return lax.all_to_all(value, axis, split_axis=0, concat_axis=0, tiled=True)]
    pallas_call x9 -> x11, Pallas kernels: 15.3 us -> 16.2 us  [call(): pl.pallas_call(kernel, in_specs=[pl.BlockSpec(memory_space=s) for s in sp...]
  transfers between devices with their start and end apart: 10 -> 11, of which waited for: 4 -> 5; matrix products, arithmetic and copies ran while one was open for 1% -> 1% of each run, Pallas kernels for 2% -> 3%
where the time goes in v3:
time: 159 us; the launch traced here: 156 us
  starting transfers between devices  58.2 us (37%)
  blocking collectives  39.4 us (25%)
  waiting for transfers between devices  36.9 us (23%)
  Pallas kernels  16.2 us (10%)
  between operations  2.24 us (1%)
  other arithmetic  1.97 us (1%)
    all_to_all x4, waiting for transfers between devices, exchange(): return lax.all_to_all(value, axis, split_axis=0, concat_axis=0, tiled=True)  35.6 us
    all_to_all x4, starting transfers between devices, exchange(): return lax.all_to_all(value, axis, split_axis=0, concat_axis=0, tiled=True)  31.7 us
    all_gather x2, blocking collectives, shards(): rows = lax.all_gather(send, 'mp', axis=0)  24.6 us
    ppermute x6, starting transfers between devices, turn(): return lax.ppermute(value, 'mp', [(i, (i + by) % MP) for i in range(MP)])  19 us
    pallas_call x11, Pallas kernels, call(): pl.pallas_call(kernel, in_specs=[pl.BlockSpec(memory_space=s) for s in sp...  16.2 us
    all_to_all x1, blocking collectives, exchange(): return lax.all_to_all(value, axis, split_axis=0, concat_axis=0, tiled=True)  14.8 us
    ppermute x1, starting transfers between devices, shards(): given = lax.ppermute(given, 'seq_2', [(0, 1), (1, 0)])  7.53 us
  transfers between devices with their start and end apart: 11, of which 5 were waited for; matrix products, arithmetic and copies ran while one was open for 1% of the time, Pallas kernels for 3%

profile of v3, /device:TPU:1, one launch (start us, length us, event | category | flops | bytes accessed | tf_op | source)
XLA Modules:
  0.0 156.2 jit_solution(9883897825994187196)
XLA Ops:
  2.9 18.4 %all-to-all-start = ((bf16[128,8,256]{2,1,0:T(8,128)(2,1)}), bf16[128,8,256]{2,1,0:T(8,128)(2,1)S(1)}, u32[]{:S(2)}, u32[]{:S(2)}) async-start(bf16[128,8,256]{2,1,0:T(8,128)(2,1)} %bitcast.5), calls=%async_computation | async-start | bytes 1048576 | tf_op jit(solution)/shard_map/hop_one/all_to_all | solution.py:24
  22.0 4.5 %collective-permute-start.2 = (bf16[224,128]{1,0:T(8,128)(2,1)}, bf16[224,128]{1,0:T(8,128)(2,1)S(1)}, u32[]{:S(2)}, u32[]{:S(2)}) collective-permute-start(bf16[224,128]{1,0:T(8,128)(2,1)} %get-tuple-element.66), channel_id=1, source_target_pairs={{0,3},{1,0},{2,1},{3,2},{4,7},{5,4},{6,5},{7,6},{8,11},{9,8},{10,9... | collective-permute-start | bytes 172040 | tf_op jit(solution)/shard_map/weights/ppermute | solution.py:122
  26.5 1.9 %collective-permute-start = (bf16[224,128]{1,0:T(8,128)(2,1)}, bf16[224,128]{1,0:T(8,128)(2,1)S(1)}, u32[]{:S(2)}, u32[]{:S(2)}) collective-permute-start(bf16[224,128]{1,0:T(8,128)(2,1)} %get-tuple-element.67), channel_id=1, source_target_pairs={{0,1},{1,2},{2,3},{3,0},{4,5},{5,6},{6,7},{7,4},{8,9},{9,10},{10,1... | collective-permute-start | bytes 172040 | tf_op jit(solution)/shard_map/weights/ppermute | solution.py:122
  28.5 3.6 %collective-permute-start.1 = (bf16[224,128]{1,0:T(8,128)(2,1)}, bf16[224,128]{1,0:T(8,128)(2,1)S(1)}, u32[]{:S(2)}, u32[]{:S(2)}) collective-permute-start(bf16[224,128]{1,0:T(8,128)(2,1)} %get-tuple-element.69), channel_id=1, source_target_pairs={{0,2},{1,3},{2,0},{3,1},{4,6},{5,7},{6,4},{7,5},{8,10},{9,11},{10,... | collective-permute-start | bytes 172040 | tf_op jit(solution)/shard_map/weights/ppermute | solution.py:122
  32.2 9.6 %all-to-all-done = bf16[128,8,256]{2,1,0:T(8,128)(2,1)S(1)} async-done(((bf16[128,8,256]{2,1,0:T(8,128)(2,1)}), bf16[128,8,256]{2,1,0:T(8,128)(2,1)S(1)}, u32[]{:S(2)}, u32[]{:S(2)}) %all-to-all-start) | async-done | bytes 524320 | tf_op jit(solution)/shard_map/hop_one/all_to_all | solution.py:24
  41.9 1.2 reorder.1
  43.1 5.4 %all-to-all-start.1 = ((bf16[128,8,256]{2,1,0:T(8,128)(2,1)}), bf16[128,8,256]{2,1,0:T(8,128)(2,1)S(1)}, u32[]{:S(2)}, u32[]{:S(2)}) async-start(bf16[128,8,256]{2,1,0:T(8,128)(2,1)} %bitcast.7), calls=%async_computation.1 | async-start | bytes 1048576 | tf_op jit(solution)/shard_map/hop_two/all_to_all | solution.py:24
  51.1 18.0 %all-to-all-done.1 = bf16[128,8,256]{2,1,0:T(8,128)(2,1)S(1)} async-done(((bf16[128,8,256]{2,1,0:T(8,128)(2,1)}), bf16[128,8,256]{2,1,0:T(8,128)(2,1)S(1)}, u32[]{:S(2)}, u32[]{:S(2)}) %all-to-all-start.1) | async-done | bytes 524320 | tf_op jit(solution)/shard_map/hop_two/all_to_all | solution.py:24
  69.4 13.2 %all-gather = bf16[1792,256]{1,0:T(8,128)(2,1)S(1)} all-gather(bf16[448,256]{1,0:T(8,128)(2,1)S(1)} %get-tuple-element.37), channel_id=2, replica_groups=mesh['seq_0'=8,'seq_1'=8,'seq_2'=2,'mp'=4] {'mp'}, dimensions={0}, use_global_device_ids=true | all-gather | bytes 1146880 | tf_op jit(solution)/shard_map/gather_one/all_gather | solution.py:408
  82.6 3.4 %feed_forward.1 = (bf16[4,464,256]{2,1,0:T(8,128)(2,1)S(1)}, f32[1,256]{1,0:T(1,128)S(1)}) custom-call(bf16[4,448,256]{2,1,0:T(8,128)(2,1)S(1)} %bitcast.29, bf16[2,896,640]{2,1,0:T(8,128)(2,1)S(1)} %copy-done, bf16[640,896]{1,0:T(8,128)(2,1)S(1)} %copy-done.1), custom_call_target="tpu_custom_call" | custom-call | tf_op jit(solution)/shard_map/feed_forward/pallas_call | solution.py:65
  86.0 14.8 %all_to_all.25.parts_ref = bf16[4,464,256]{2,1,0:T(8,128)(2,1)S(1)} all-to-all(bf16[4,464,256]{2,1,0:T(8,128)(2,1)S(1)} %get-tuple-element.38), channel_id=1, replica_groups=mesh['seq_0'=8,'seq_1'=8,'seq_2'=2,'mp'=4] {'mp'}, dimensions={0} | all-to-all | bytes 1900544 | tf_op jit(solution)/shard_map/sum_one/all_to_all | solution.py:24
  100.8 1.4 middle.1
  102.2 11.4 %all-gather.1 = bf16[1792,256]{1,0:T(8,128)(2,1)S(1)} all-gather(bf16[448,256]{1,0:T(8,128)(2,1)S(1)} %get-tuple-element.41), channel_id=3, replica_groups=mesh['seq_0'=8,'seq_1'=8,'seq_2'=2,'mp'=4] {'mp'}, dimensions={0}, use_global_device_ids=true | all-gather | bytes 1146880 | tf_op jit(solution)/shard_map/gather_two/all_gather | solution.py:432
  113.6 4.2 %attention.1 = (bf16[512,384]{1,0:T(8,128)(2,1)S(1)}, bf16[512,384]{1,0:T(8,128)(2,1)S(1)}, bf16[3,256,128]{2,1,0:T(8,128)(2,1)S(1)}, bf16[4,224,128]{2,1,0:T(8,...) custom-call(s32[5]{0:T(128)S(1)} %pad_add_fusion.facts_ref, bf16[4,448,256]{2,1,0:T(8,128)(2,1)S(1)} %bitcast.30, ...), custom_call_target="tpu_custom_call" | custom-call | tf_op jit(solution)/shard_map/attention/pallas_call | solution.py:65
  117.8 7.5 %collective-permute-start.6 = (bf16[512,384]{1,0:T(8,128)(2,1)S(1)}, bf16[512,384]{1,0:T(8,128)(2,1)S(1)}, u32[]{:S(2)}, u32[]{:S(2)}) collective-permute-start(bf16[512,384]{1,0:T(8,128)(2,1)S(1)} %get-tuple-element.59), channel_id=1, source_target_pairs={{0,4},{4,0},{1,5},{5,1},{2,6},{6,2},{3,7},{7,3},{8,12},{12,8},{9,1... | collective-permute-start | bytes 1179656 | tf_op jit(solution)/shard_map/core_sum/ppermute | solution.py:455
  125.3 1.3 collective-permute-done.6.right_ref
  127.5 4.6 %all-to-all-start.3 = ((bf16[64,8,384]{2,1,0:T(8,128)(2,1)}), bf16[64,8,384]{2,1,0:T(8,128)(2,1)S(1)}, u32[]{:S(2)}, u32[]{:S(2)}) async-start(bf16[64,8,384]{2,1,0:T(8,128)(2,1)} %bitcast.22), calls=%async_computation.3 | async-start | bytes 786432 | tf_op jit(solution)/shard_map/weight_grads/all_to_all | solution.py:24
  133.3 2.3 %collective-permute-start.3 = (bf16[464,256]{1,0:T(8,128)(2,1)S(1)}, bf16[464,256]{1,0:T(8,128)(2,1)S(1)}, u32[]{:S(2)}, u32[]{:S(2)}) collective-permute-start(bf16[464,256]{1,0:T(8,128)(2,1)S(1)} %get-tuple-element.50), channel_id=1, source_target_pairs={{0,1},{1,2},{2,3},{3,0},{4,5},{5,6},{6,7},{7,4},{8,9},{9,10},{10,1... | collective-permute-start | bytes 712712 | tf_op jit(solution)/shard_map/last_sum/ppermute | solution.py:122
  135.6 4.3 %collective-permute-start.4 = (bf16[464,256]{1,0:T(8,128)(2,1)S(1)}, bf16[464,256]{1,0:T(8,128)(2,1)S(1)}, u32[]{:S(2)}, u32[]{:S(2)}) collective-permute-start(bf16[464,256]{1,0:T(8,128)(2,1)S(1)} %get-tuple-element.51), channel_id=1, source_target_pairs={{0,2},{1,3},{2,0},{3,1},{4,6},{5,7},{6,4},{7,5},{8,10},{9,11},{10,... | collective-permute-start | bytes 712712 | tf_op jit(solution)/shard_map/last_sum/ppermute | solution.py:122
  139.9 2.4 %collective-permute-start.5 = (bf16[464,256]{1,0:T(8,128)(2,1)S(1)}, bf16[464,256]{1,0:T(8,128)(2,1)S(1)}, u32[]{:S(2)}, u32[]{:S(2)}) collective-permute-start(bf16[464,256]{1,0:T(8,128)(2,1)S(1)} %get-tuple-element.52), channel_id=1, source_target_pairs={{0,3},{1,0},{2,1},{3,2},{4,7},{5,4},{6,5},{7,6},{8,11},{9,8},{10,9... | collective-permute-start | bytes 712712 | tf_op jit(solution)/shard_map/last_sum/ppermute | solution.py:122
  142.3 5.2 %all-to-all-done.3.grads_ref = bf16[64,8,384]{2,1,0:T(8,128)(2,1)S(1)} async-done(((bf16[64,8,384]{2,1,0:T(8,128)(2,1)}), bf16[64,8,384]{2,1,0:T(8,128)(2,1)S(1)}, u32[]{:S(2)}, u32[]{:S(2)}) %all-to-all-start.3) | async-done | bytes 393248 | tf_op jit(solution)/shard_map/weight_grads/all_to_all | solution.py:24
  148.2 3.2 %all-to-all-start.4 = ((f32[4,7,128]{2,1,0:T(8,128)}), f32[4,7,128]{2,1,0:T(8,128)S(1)}, u32[]{:S(2)}, u32[]{:S(2)}) async-start(f32[4,7,128]{2,1,0:T(8,128)} %get-tuple-element.61), calls=%async_computation.4 | async-start | bytes 32768 | tf_op jit(solution)/shard_map/key_grads/all_to_all | solution.py:24
  151.5 1.4 last.1
  152.9 2.8 %all-to-all-done.4.shares_ref = f32[4,7,128]{2,1,0:T(8,128)S(1)} async-done(((f32[4,7,128]{2,1,0:T(8,128)}), f32[4,7,128]{2,1,0:T(8,128)S(1)}, u32[]{:S(2)}, u32[]{:S(2)}) %all-to-all-start.4) | async-done | bytes 14368 | tf_op jit(solution)/shard_map/key_grads/all_to_all | solution.py:24
  (42 shorter events, 7.9 us)
Async XLA Ops:
  0.6 20.7 %copy-start.6 = (bf16[2,224,128]{2,1,0:T(8,128)(2,1)S(1)}, bf16[2,224,128]{2,1,0:T(8,128)(2,1)}, u32[]{:S(2)}) copy-start(bf16[2,224,128]{2,1,0:T(8,128)(2,1)} %param.20) | copy-start | bytes 344068
  0.6 31.5 %copy-start.7 = (s32[192]{0:T(256)S(1)}, s32[192]{0:T(256)}, u32[]{:S(2)}) copy-start(s32[192]{0:T(256)} %param.16) | copy-start | bytes 2308
  0.7 41.2 %copy-start.5 = (s32[256]{0:T(256)S(1)}, s32[256]{0:T(256)}, u32[]{:S(2)}) copy-start(s32[256]{0:T(256)} %param.18) | copy-start | bytes 3076
  1.8 46.9 %copy-start.8 = (s32[192]{0:T(256)S(1)}, s32[192]{0:T(256)}, u32[]{:S(2)}) copy-start(s32[192]{0:T(256)} %param.17) | copy-start | bytes 2308
  2.9 39.0 %all-to-all-start = ((bf16[128,8,256]{2,1,0:T(8,128)(2,1)}), bf16[128,8,256]{2,1,0:T(8,128)(2,1)S(1)}, u32[]{:S(2)}, u32[]{:S(2)}) async-start(bf16[128,8,256]{2,1,0:T(8,128)(2,1)} %bitcast.5), calls=%async_computation | async-start | bytes 1048576 | tf_op jit(solution)/shard_map/hop_one/all_to_all | solution.py:24
  21.3 61.3 %copy-start = (bf16[2,896,640]{2,1,0:T(8,128)(2,1)S(1)}, bf16[2,896,640]{2,1,0:T(8,128)(2,1)}, u32[]{:S(2)}) copy-start(bf16[2,896,640]{2,1,0:T(8,128)(2,1)} %gate_up_ref.1) | copy-start | bytes 6881284
  22.0 47.3 %collective-permute-start.2 = (bf16[224,128]{1,0:T(8,128)(2,1)}, bf16[224,128]{1,0:T(8,128)(2,1)S(1)}, u32[]{:S(2)}, u32[]{:S(2)}) collective-permute-start(bf16[224,128]{1,0:T(8,128)(2,1)} %get-tuple-element.66), channel_id=1, source_target_pairs={{0,3},{1,0},{2,1},{3,2},{4,7},{5,4},{6,5},{7,6},{8,11},{9,8},{10,9... | collective-permute-start | bytes 172040 | tf_op jit(solution)/shard_map/weights/ppermute | solution.py:122
  26.5 42.8 %collective-permute-start = (bf16[224,128]{1,0:T(8,128)(2,1)}, bf16[224,128]{1,0:T(8,128)(2,1)S(1)}, u32[]{:S(2)}, u32[]{:S(2)}) collective-permute-start(bf16[224,128]{1,0:T(8,128)(2,1)} %get-tuple-element.67), channel_id=1, source_target_pairs={{0,1},{1,2},{2,3},{3,0},{4,5},{5,6},{6,7},{7,4},{8,9},{9,10},{10,1... | collective-permute-start | bytes 172040 | tf_op jit(solution)/shard_map/weights/ppermute | solution.py:122
  28.5 40.9 %collective-permute-start.1 = (bf16[224,128]{1,0:T(8,128)(2,1)}, bf16[224,128]{1,0:T(8,128)(2,1)S(1)}, u32[]{:S(2)}, u32[]{:S(2)}) collective-permute-start(bf16[224,128]{1,0:T(8,128)(2,1)} %get-tuple-element.69), channel_id=1, source_target_pairs={{0,2},{1,3},{2,0},{3,1},{4,6},{5,7},{6,4},{7,5},{8,10},{9,11},{10,... | collective-permute-start | bytes 172040 | tf_op jit(solution)/shard_map/weights/ppermute | solution.py:122
  43.1 26.0 %all-to-all-start.1 = ((bf16[128,8,256]{2,1,0:T(8,128)(2,1)}), bf16[128,8,256]{2,1,0:T(8,128)(2,1)S(1)}, u32[]{:S(2)}, u32[]{:S(2)}) async-start(bf16[128,8,256]{2,1,0:T(8,128)(2,1)} %bitcast.7), calls=%async_computation.1 | async-start | bytes 1048576 | tf_op jit(solution)/shard_map/hop_two/all_to_all | solution.py:24
  69.0 13.5 %copy-start.1 = (bf16[640,896]{1,0:T(8,128)(2,1)S(1)}, bf16[640,896]{1,0:T(8,128)(2,1)}, u32[]{:S(2)}) copy-start(bf16[640,896]{1,0:T(8,128)(2,1)} %down_ref.1) | copy-start | bytes 3440644
  86.0 27.6 %copy-start.2 = (bf16[896,128]{1,0:T(8,128)(2,1)S(1)}, bf16[896,128]{1,0:T(8,128)(2,1)}, u32[]{:S(2)}) copy-start(bf16[896,128]{1,0:T(8,128)(2,1)} %param.19) | copy-start | bytes 688132
  86.0 27.6 %copy-start.3 = (bf16[128,896]{1,0:T(8,128)(2,1)S(1)}, bf16[128,896]{1,0:T(8,128)(2,1)}, u32[]{:S(2)}) copy-start(bf16[128,896]{1,0:T(8,128)(2,1)} %proj_ref.3) | copy-start | bytes 688132
  113.6 37.9 %copy-start.4 = (bf16[224,256]{1,0:T(8,128)(2,1)S(1)}, bf16[224,256]{1,0:T(8,128)(2,1)}, u32[]{:S(2)}) copy-start(bf16[224,256]{1,0:T(8,128)(2,1)} %get-tuple-element.53.refs_5_) | copy-start | bytes 344068
  117.8 8.9 %collective-permute-start.6 = (bf16[512,384]{1,0:T(8,128)(2,1)S(1)}, bf16[512,384]{1,0:T(8,128)(2,1)S(1)}, u32[]{:S(2)}, u32[]{:S(2)}) collective-permute-start(bf16[512,384]{1,0:T(8,128)(2,1)S(1)} %get-tuple-element.59), channel_id=1, source_target_pairs={{0,4},{4,0},{1,5},{5,1},{2,6},{6,2},{3,7},{7,3},{8,12},{12,8},{9,1... | collective-permute-start | bytes 1179656 | tf_op jit(solution)/shard_map/core_sum/ppermute | solution.py:455
  127.5 20.0 %all-to-all-start.3 = ((bf16[64,8,384]{2,1,0:T(8,128)(2,1)}), bf16[64,8,384]{2,1,0:T(8,128)(2,1)S(1)}, u32[]{:S(2)}, u32[]{:S(2)}) async-start(bf16[64,8,384]{2,1,0:T(8,128)(2,1)} %bitcast.22), calls=%async_computation.3 | async-start | bytes 786432 | tf_op jit(solution)/shard_map/weight_grads/all_to_all | solution.py:24
  133.3 18.2 %collective-permute-start.3 = (bf16[464,256]{1,0:T(8,128)(2,1)S(1)}, bf16[464,256]{1,0:T(8,128)(2,1)S(1)}, u32[]{:S(2)}, u32[]{:S(2)}) collective-permute-start(bf16[464,256]{1,0:T(8,128)(2,1)S(1)} %get-tuple-element.50), channel_id=1, source_target_pairs={{0,1},{1,2},{2,3},{3,0},{4,5},{5,6},{6,7},{7,4},{8,9},{9,10},{10,1... | collective-permute-start | bytes 712712 | tf_op jit(solution)/shard_map/last_sum/ppermute | solution.py:122
  135.6 15.9 %collective-permute-start.4 = (bf16[464,256]{1,0:T(8,128)(2,1)S(1)}, bf16[464,256]{1,0:T(8,128)(2,1)S(1)}, u32[]{:S(2)}, u32[]{:S(2)}) collective-permute-start(bf16[464,256]{1,0:T(8,128)(2,1)S(1)} %get-tuple-element.51), channel_id=1, source_target_pairs={{0,2},{1,3},{2,0},{3,1},{4,6},{5,7},{6,4},{7,5},{8,10},{9,11},{10,... | collective-permute-start | bytes 712712 | tf_op jit(solution)/shard_map/last_sum/ppermute | solution.py:122
  139.9 11.6 %collective-permute-start.5 = (bf16[464,256]{1,0:T(8,128)(2,1)S(1)}, bf16[464,256]{1,0:T(8,128)(2,1)S(1)}, u32[]{:S(2)}, u32[]{:S(2)}) collective-permute-start(bf16[464,256]{1,0:T(8,128)(2,1)S(1)} %get-tuple-element.52), channel_id=1, source_target_pairs={{0,3},{1,0},{2,1},{3,2},{4,7},{5,4},{6,5},{7,6},{8,11},{9,8},{10,9... | collective-permute-start | bytes 712712 | tf_op jit(solution)/shard_map/last_sum/ppermute | solution.py:122
  148.2 7.4 %all-to-all-start.4 = ((f32[4,7,128]{2,1,0:T(8,128)}), f32[4,7,128]{2,1,0:T(8,128)S(1)}, u32[]{:S(2)}, u32[]{:S(2)}) async-start(f32[4,7,128]{2,1,0:T(8,128)} %get-tuple-element.61), calls=%async_computation.4 | async-start | bytes 32768 | tf_op jit(solution)/shard_map/key_grads/all_to_all | solution.py:24

commit v4 on v3

--- a/solution.py
+++ b/solution.py
@@ -33,34 +33,34 @@
 TN = ((0,), (0,))
 
 
-def slot_facts(doc_blocks, last_fill, plan, slots):
-    blocks = plan.shape[0]
-    index = jnp.arange(blocks, dtype=jnp.int32)
-    mine = jnp.sum(jnp.where(plan[None, :] == slots[:, None], index[None, :], 0), axis=1)
-    docs = doc_blocks.shape[0]
-    order = jnp.arange(docs, dtype=jnp.int32)
-    ends = jnp.sum(jnp.where(order[None, :] <= order[:, None], doc_blocks[None, :], 0), axis=1)
-    starts = ends - doc_blocks
-    inside = (starts[None, :] <= mine[:, None]) & (mine[:, None] < ends[None, :])
-    owner = jnp.sum(jnp.where(inside, order[None, :], 0), axis=1)
-    last = inside & (ends[None, :] - 1 == mine[:, None])
-    limit = jnp.where(
-        jnp.any(last, axis=1), jnp.sum(jnp.where(last, last_fill[None, :], 0), axis=1), BLOCK
-    )
-    same = (owner[0] == owner[1]).astype(jnp.int32)
-    return jnp.stack([limit[0], limit[1], same, lax.axis_index("mp"), lax.axis_index("seq_2")]).astype(
-        jnp.int32
-    )
-
-
-def call(kernel, out_shape, *args, scratch=(), smem=0, far=(), far_out=(), mib=16, name=None):
+def facts_kernel(blocks_ref, fill_ref, plan_ref, out_ref):
+    docs = blocks_ref.shape[1]
+    counts = jnp.broadcast_to(blocks_ref[...], (PAD, docs)).astype(F32)
+    fills = fill_ref[...].astype(F32)
+    row = lax.broadcasted_iota(jnp.int32, (docs, docs), 0)
+    col = lax.broadcasted_iota(jnp.int32, (docs, docs), 1)
+    ends = dot(counts.astype(BF16), (row <= col).astype(BF16), NN)[:1]
+    starts = ends - counts[:1]
+    order = lax.broadcasted_iota(jnp.int32, (1, docs), 1).astype(F32)
+    index = lax.broadcasted_iota(jnp.int32, plan_ref.shape, 1).astype(F32)
+    owners = []
+    for t in range(2):
+        slot = 2 * lax.axis_index(SEQ) + t
+        mine = jnp.sum(jnp.where(plan_ref[...] == slot, index, 0.0), axis=1, keepdims=True)
+        inside = (starts <= mine) & (mine < ends)
+        last = inside & (ends - 1.0 == mine)
+        short = jnp.sum(jnp.where(last, BLOCK - fills, 0.0))
+        out_ref[t] = BLOCK - short.astype(jnp.int32)
+        owners.append(jnp.sum(jnp.where(inside, order, 0.0)).astype(jnp.int32))
+    out_ref[2] = (owners[0] == owners[1]).astype(jnp.int32)
+    out_ref[3] = lax.axis_index("mp")
+    out_ref[4] = lax.axis_index("seq_2")
+
+
+def call(kernel, out_shape, *args, scratch=(), smem=0, out=pltpu.VMEM, mib=16, name=None):
     spaces = [pltpu.SMEM] * smem + [pltpu.VMEM] * (len(args) - smem)
-    for i in far:
-        spaces[i] = pltpu.HBM
     one = not isinstance(out_shape, tuple)
-    outs = [pltpu.VMEM] * (1 if one else len(out_shape))
-    for i in far_out:
-        outs[i] = pltpu.HBM
+    outs = [out] * (1 if one else len(out_shape))
     outs = [pl.BlockSpec(memory_space=o) for o in outs]
     return pl.pallas_call(
         kernel,
@@ -95,7 +95,10 @@
     out_ref[...] = get(rows_ref, slice(None)).astype(BF16)
 
 
-def reorder_kernel(plan_ref, held_ref, out_ref, rows_ref, next_ref):
+def reorder_kernel(plan_ref, held_ref, keyval_ref, out_ref, *refs):
+    *piece_refs, rows_ref, next_ref = refs
+    for k, piece_ref in enumerate(piece_refs):
+        piece_ref[...] = keyval_ref[((lax.axis_index("mp") + k) % MP) // 2]
     blocks = plan_ref.shape[1]
     slot = lax.broadcasted_iota(jnp.int32, (blocks, blocks), 0)
     pick = (plan_ref[...] == slot).astype(BF16)
@@ -129,34 +132,40 @@
     width = streams[0].shape[0]
     lanes = -(-width // 128) * 128
     rows = 8 * BLOCK
-    shape = jax.ShapeDtypeStruct((rows, lanes), BF16)
+    piece = jax.ShapeDtypeStruct(kv_weight.shape[1:], BF16)
     scratch = pltpu.VMEM((lanes // 128, rows, 128), F32)
     sent = call(
-        pack_kernel, shape, jnp.concatenate(streams, axis=0), scratch=[scratch], name="pack"
+        pack_kernel,
+        jax.ShapeDtypeStruct((rows, lanes), BF16),
+        jnp.concatenate(streams, axis=0),
+        scratch=[scratch],
+        name="pack",
+    )
+    facts = call(
+        facts_kernel,
+        jax.ShapeDtypeStruct((5,), jnp.int32),
+        *[table.reshape(1, -1) for table in tables],
+        out=pltpu.SMEM,
+        name="facts",
     )
     with jax.named_scope("hop_one"):
         held = exchange(sent.reshape(peers, share * 8, lanes), SEQ)
-    slots = lax.axis_index(SEQ) * 2 + jnp.arange(2, dtype=jnp.int32)
-    facts = slot_facts(*tables, slots)
-    with jax.named_scope("weights"):
-        me = lax.axis_index("mp")
-        pieces = [kv_weight[me >> 1]]
-        for k in range(1, MP):
-            pieces.append(turn(kv_weight[((me + k) & 3) >> 1], k))
     held = held.reshape(peers, share, 8, lanes)
     placed = []
     for r in range(share):
-        placed.append(
-            call(
-                reorder_kernel,
-                jax.ShapeDtypeStruct((peers * 8, lanes), BF16),
-                plan.reshape(1, -1),
-                held[:, r].reshape(peers * 8, lanes),
-                scratch=[pltpu.VMEM((lanes // 128, peers * 8, 128), F32)] * 2,
-                name="reorder",
-            ).reshape(peers, 8, lanes)
+        moved, *pieces = call(
+            reorder_kernel,
+            (jax.ShapeDtypeStruct((peers * 8, lanes), BF16), *[piece] * MP),
+            plan.reshape(1, -1),
+            held[:, r].reshape(peers * 8, lanes),
+            kv_weight,
+            scratch=[pltpu.VMEM((lanes // 128, peers * 8, 128), F32)] * 2,
+            name="reorder",
         )
+        placed.append(moved.reshape(peers, 8, lanes))
     placed = placed[0] if share == 1 else jnp.stack(placed, axis=1).reshape(peers, -1, lanes)
+    with jax.named_scope("weights"):
+        pieces = [pieces[0]] + [turn(pieces[k], k) for k in range(1, MP)]
     with jax.named_scope("hop_two"):
         owned = exchange(placed, SEQ)
     return facts, pieces, *call(

time: 159 us -> 158 us (level)
  blocking collectives: 39.4 us -> 78.3 us
  waiting for transfers between devices: 36.9 us -> 18.4 us
  starting transfers between devices: 58.2 us -> 40.3 us
    all_to_all x1 -> x2, blocking collectives: 14.8 us -> 53.7 us  [exchange(): return lax.all_to_all(value, axis, split_axis=0, concat_axis=0, tiled=True)]
    all_to_all x4 -> x3, waiting for transfers between devices: 35.6 us -> 17.1 us  [exchange(): return lax.all_to_all(value, axis, split_axis=0, concat_axis=0, tiled=True)]
    all_to_all x4 -> x3, starting transfers between devices: 31.7 us -> 13.3 us  [exchange(): return lax.all_to_all(value, axis, split_axis=0, concat_axis=0, tiled=True)]
    pallas_call x11 -> x12, Pallas kernels: 16.2 us -> 16.3 us  [call(): pl.pallas_call(kernel, in_specs=[pl.BlockSpec(memory_space=s) for s in sp...]
  transfers between devices with their start and end apart: 11 -> 10, of which waited for: 5 -> 4; matrix products, arithmetic and copies ran while one was open for 1% -> 0% of each run, Pallas kernels for 3% -> 3%
where the time goes in v4:
time: 158 us; the launch traced here: 155 us
  blocking collectives  78.3 us (50%)
  starting transfers between devices  40.3 us (26%)
  waiting for transfers between devices  18.4 us (12%)
  Pallas kernels  16.3 us (10%)
    all_to_all x2, blocking collectives, exchange(): return lax.all_to_all(value, axis, split_axis=0, concat_axis=0, tiled=True)  53.7 us
    all_gather x2, blocking collectives, shards(): rows = lax.all_gather(send, 'mp', axis=0)  24.6 us
    ppermute x6, starting transfers between devices, turn(): return lax.ppermute(value, 'mp', [(i, (i + by) % MP) for i in range(MP)])  19.5 us
    all_to_all x3, waiting for transfers between devices, exchange(): return lax.all_to_all(value, axis, split_axis=0, concat_axis=0, tiled=True)  17.1 us
    pallas_call x12, Pallas kernels, call(): pl.pallas_call(kernel, in_specs=[pl.BlockSpec(memory_space=s) for s in sp...  16.3 us
    all_to_all x3, starting transfers between devices, exchange(): return lax.all_to_all(value, axis, split_axis=0, concat_axis=0, tiled=True)  13.3 us
    ppermute x1, starting transfers between devices, shards(): given = lax.ppermute(given, 'seq_2', [(0, 1), (1, 0)])  7.53 us
  transfers between devices with their start and end apart: 10, of which 4 were waited for; matrix products, arithmetic and copies ran while one was open for 0% of the time, Pallas kernels for 3%

profile of v4, /device:TPU:1, one launch (start us, length us, event | category | flops | bytes accessed | tf_op | source)
XLA Modules:
  0.0 155.4 jit_solution(14383325656983757448)
XLA Ops:
  0.7 1.2 pad_maximum_fusion.streams_ref
  2.1 38.9 %all_to_all.25 = bf16[128,8,256]{2,1,0:T(8,128)(2,1)S(1)} all-to-all(bf16[128,8,256]{2,1,0:T(8,128)(2,1)S(1)} %bitcast.25), channel_id=1, replica_groups=mesh['seq_0'=8,'seq_1'=8,'seq_2'=2,'mp'=4] {'seq_0','seq_1','seq_2'}, dimensions={0} | all-to-all | bytes 1048576 | tf_op jit(solution)/shard_map/hop_one/all_to_all | solution.py:24
  41.0 1.2 reorder.1
  42.3 5.4 %all-to-all-start.1 = ((bf16[128,8,256]{2,1,0:T(8,128)(2,1)}), bf16[128,8,256]{2,1,0:T(8,128)(2,1)S(1)}, u32[]{:S(2)}, u32[]{:S(2)}) async-start(bf16[128,8,256]{2,1,0:T(8,128)(2,1)} %bitcast.7), calls=%async_computation.1 | async-start | bytes 1048576 | tf_op jit(solution)/shard_map/hop_two/all_to_all | solution.py:24
  47.7 3.1 %collective-permute-start = (bf16[224,128]{1,0:T(8,128)(2,1)}, bf16[224,128]{1,0:T(8,128)(2,1)S(1)}, u32[]{:S(2)}, u32[]{:S(2)}) collective-permute-start(bf16[224,128]{1,0:T(8,128)(2,1)} %get-tuple-element.43), channel_id=1, source_target_pairs={{0,1},{1,2},{2,3},{3,0},{4,5},{5,6},{6,7},{7,4},{8,9},{9,10},{10,1... | collective-permute-start | bytes 172040 | tf_op jit(solution)/shard_map/weights/ppermute | solution.py:125
  50.8 4.3 %collective-permute-start.1 = (bf16[224,128]{1,0:T(8,128)(2,1)}, bf16[224,128]{1,0:T(8,128)(2,1)S(1)}, u32[]{:S(2)}, u32[]{:S(2)}) collective-permute-start(bf16[224,128]{1,0:T(8,128)(2,1)} %get-tuple-element.44), channel_id=1, source_target_pairs={{0,2},{1,3},{2,0},{3,1},{4,6},{5,7},{6,4},{7,5},{8,10},{9,11},{10,... | collective-permute-start | bytes 172040 | tf_op jit(solution)/shard_map/weights/ppermute | solution.py:125
  55.2 3.1 %collective-permute-start.2 = (bf16[224,128]{1,0:T(8,128)(2,1)}, bf16[224,128]{1,0:T(8,128)(2,1)S(1)}, u32[]{:S(2)}, u32[]{:S(2)}) collective-permute-start(bf16[224,128]{1,0:T(8,128)(2,1)} %get-tuple-element.45), channel_id=1, source_target_pairs={{0,3},{1,0},{2,1},{3,2},{4,7},{5,4},{6,5},{7,6},{8,11},{9,8},{10,9... | collective-permute-start | bytes 172040 | tf_op jit(solution)/shard_map/weights/ppermute | solution.py:125
  59.1 9.1 %all-to-all-done.1 = bf16[128,8,256]{2,1,0:T(8,128)(2,1)S(1)} async-done(((bf16[128,8,256]{2,1,0:T(8,128)(2,1)}), bf16[128,8,256]{2,1,0:T(8,128)(2,1)S(1)}, u32[]{:S(2)}, u32[]{:S(2)}) %all-to-all-start.1) | async-done | bytes 524320 | tf_op jit(solution)/shard_map/hop_two/all_to_all | solution.py:24
  68.5 13.2 %all-gather = bf16[1792,256]{1,0:T(8,128)(2,1)S(1)} all-gather(bf16[448,256]{1,0:T(8,128)(2,1)S(1)} %get-tuple-element.47), channel_id=2, replica_groups=mesh['seq_0'=8,'seq_1'=8,'seq_2'=2,'mp'=4] {'mp'}, dimensions={0}, use_global_device_ids=true | all-gather | bytes 1146880 | tf_op jit(solution)/shard_map/gather_one/all_gather | solution.py:417
  81.8 3.4 %feed_forward.1 = (bf16[4,464,256]{2,1,0:T(8,128)(2,1)S(1)}, f32[1,256]{1,0:T(1,128)S(1)}) custom-call(bf16[4,448,256]{2,1,0:T(8,128)(2,1)S(1)} %bitcast.21, bf16[2,896,640]{2,1,0:T(8,128)(2,1)S(1)} %copy-done, bf16[640,896]{1,0:T(8,128)(2,1)S(1)} %copy-done.1), custom_call_target="tpu_custom_call" | custom-call | tf_op jit(solution)/shard_map/feed_forward/pallas_call | solution.py:65
  85.2 14.8 %all_to_all.26.parts_ref = bf16[4,464,256]{2,1,0:T(8,128)(2,1)S(1)} all-to-all(bf16[4,464,256]{2,1,0:T(8,128)(2,1)S(1)} %get-tuple-element.48), channel_id=1, replica_groups=mesh['seq_0'=8,'seq_1'=8,'seq_2'=2,'mp'=4] {'mp'}, dimensions={0} | all-to-all | bytes 1900544 | tf_op jit(solution)/shard_map/sum_one/all_to_all | solution.py:24
  100.0 1.4 middle.1
  101.4 11.4 %all-gather.1 = bf16[1792,256]{1,0:T(8,128)(2,1)S(1)} all-gather(bf16[448,256]{1,0:T(8,128)(2,1)S(1)} %get-tuple-element.51), channel_id=3, replica_groups=mesh['seq_0'=8,'seq_1'=8,'seq_2'=2,'mp'=4] {'mp'}, dimensions={0}, use_global_device_ids=true | all-gather | bytes 1146880 | tf_op jit(solution)/shard_map/gather_two/all_gather | solution.py:441
  112.8 4.2 %attention.1 = (bf16[512,384]{1,0:T(8,128)(2,1)S(1)}, bf16[512,384]{1,0:T(8,128)(2,1)S(1)}, bf16[3,256,128]{2,1,0:T(8,128)(2,1)S(1)}, bf16[4,224,128]{2,1,0:T(8,...) custom-call(s32[5]{0:T(128)S(1)} %facts.1.facts_ref, bf16[4,448,256]{2,1,0:T(8,128)(2,1)S(1)} %bitcast.22, ...), custom_call_target="tpu_custom_call" | custom-call | tf_op jit(solution)/shard_map/attention/pallas_call | solution.py:65
  117.0 7.5 %collective-permute-start.6 = (bf16[512,384]{1,0:T(8,128)(2,1)S(1)}, bf16[512,384]{1,0:T(8,128)(2,1)S(1)}, u32[]{:S(2)}, u32[]{:S(2)}) collective-permute-start(bf16[512,384]{1,0:T(8,128)(2,1)S(1)} %get-tuple-element.69), channel_id=1, source_target_pairs={{0,4},{4,0},{1,5},{5,1},{2,6},{6,2},{3,7},{7,3},{8,12},{12,8},{9,1... | collective-permute-start | bytes 1179656 | tf_op jit(solution)/shard_map/core_sum/ppermute | solution.py:464
  124.5 1.3 collective-permute-done.6.right_ref
  126.7 4.6 %all-to-all-start.3 = ((bf16[64,8,384]{2,1,0:T(8,128)(2,1)}), bf16[64,8,384]{2,1,0:T(8,128)(2,1)S(1)}, u32[]{:S(2)}, u32[]{:S(2)}) async-start(bf16[64,8,384]{2,1,0:T(8,128)(2,1)} %bitcast.18), calls=%async_computation.3 | async-start | bytes 786432 | tf_op jit(solution)/shard_map/weight_grads/all_to_all | solution.py:24
  132.5 2.3 %collective-permute-start.3 = (bf16[464,256]{1,0:T(8,128)(2,1)S(1)}, bf16[464,256]{1,0:T(8,128)(2,1)S(1)}, u32[]{:S(2)}, u32[]{:S(2)}) collective-permute-start(bf16[464,256]{1,0:T(8,128)(2,1)S(1)} %get-tuple-element.60), channel_id=1, source_target_pairs={{0,1},{1,2},{2,3},{3,0},{4,5},{5,6},{6,7},{7,4},{8,9},{9,10},{10,1... | collective-permute-start | bytes 712712 | tf_op jit(solution)/shard_map/last_sum/ppermute | solution.py:125
  134.8 4.3 %collective-permute-start.4 = (bf16[464,256]{1,0:T(8,128)(2,1)S(1)}, bf16[464,256]{1,0:T(8,128)(2,1)S(1)}, u32[]{:S(2)}, u32[]{:S(2)}) collective-permute-start(bf16[464,256]{1,0:T(8,128)(2,1)S(1)} %get-tuple-element.61), channel_id=1, source_target_pairs={{0,2},{1,3},{2,0},{3,1},{4,6},{5,7},{6,4},{7,5},{8,10},{9,11},{10,... | collective-permute-start | bytes 712712 | tf_op jit(solution)/shard_map/last_sum/ppermute | solution.py:125
  139.1 2.4 %collective-permute-start.5 = (bf16[464,256]{1,0:T(8,128)(2,1)S(1)}, bf16[464,256]{1,0:T(8,128)(2,1)S(1)}, u32[]{:S(2)}, u32[]{:S(2)}) collective-permute-start(bf16[464,256]{1,0:T(8,128)(2,1)S(1)} %get-tuple-element.62), channel_id=1, source_target_pairs={{0,3},{1,0},{2,1},{3,2},{4,7},{5,4},{6,5},{7,6},{8,11},{9,8},{10,9... | collective-permute-start | bytes 712712 | tf_op jit(solution)/shard_map/last_sum/ppermute | solution.py:125
  141.5 5.2 %all-to-all-done.3.grads_ref = bf16[64,8,384]{2,1,0:T(8,128)(2,1)S(1)} async-done(((bf16[64,8,384]{2,1,0:T(8,128)(2,1)}), bf16[64,8,384]{2,1,0:T(8,128)(2,1)S(1)}, u32[]{:S(2)}, u32[]{:S(2)}) %all-to-all-start.3) | async-done | bytes 393248 | tf_op jit(solution)/shard_map/weight_grads/all_to_all | solution.py:24
  147.4 3.2 %all-to-all-start.4 = ((f32[4,7,128]{2,1,0:T(8,128)}), f32[4,7,128]{2,1,0:T(8,128)S(1)}, u32[]{:S(2)}, u32[]{:S(2)}) async-start(f32[4,7,128]{2,1,0:T(8,128)} %get-tuple-element.71), calls=%async_computation.4 | async-start | bytes 32768 | tf_op jit(solution)/shard_map/key_grads/all_to_all | solution.py:24
  150.7 1.4 last.1
  152.1 2.8 %all-to-all-done.4.shares_ref = f32[4,7,128]{2,1,0:T(8,128)S(1)} async-done(((f32[4,7,128]{2,1,0:T(8,128)}), f32[4,7,128]{2,1,0:T(8,128)S(1)}, u32[]{:S(2)}, u32[]{:S(2)}) %all-to-all-start.4) | async-done | bytes 14368 | tf_op jit(solution)/shard_map/key_grads/all_to_all | solution.py:24
  (31 shorter events, 4.8 us)
Async XLA Ops:
  0.6 40.4 %copy-start.5 = (bf16[2,224,128]{2,1,0:T(8,128)(2,1)S(1)}, bf16[2,224,128]{2,1,0:T(8,128)(2,1)}, u32[]{:S(2)}) copy-start(bf16[2,224,128]{2,1,0:T(8,128)(2,1)} %keyval_ref.1) | copy-start | bytes 344068
  0.6 40.4 %copy-start.6 = (s32[256]{0:T(256)S(1)}, s32[256]{0:T(256)}, u32[]{:S(2)}) copy-start(s32[256]{0:T(256)} %param.18) | copy-start | bytes 3076
  0.7 57.6 %copy-start.7 = (s32[192]{0:T(256)S(1)}, s32[192]{0:T(256)}, u32[]{:S(2)}) copy-start(s32[192]{0:T(256)} %param.16) | copy-start | bytes 2308
  0.7 57.6 %copy-start.8 = (s32[192]{0:T(256)S(1)}, s32[192]{0:T(256)}, u32[]{:S(2)}) copy-start(s32[192]{0:T(256)} %param.17) | copy-start | bytes 2308
  2.1 79.6 %copy-start = (bf16[2,896,640]{2,1,0:T(8,128)(2,1)S(1)}, bf16[2,896,640]{2,1,0:T(8,128)(2,1)}, u32[]{:S(2)}) copy-start(bf16[2,896,640]{2,1,0:T(8,128)(2,1)} %gate_up_ref.1) | copy-start | bytes 6881284
  42.3 26.0 %all-to-all-start.1 = ((bf16[128,8,256]{2,1,0:T(8,128)(2,1)}), bf16[128,8,256]{2,1,0:T(8,128)(2,1)S(1)}, u32[]{:S(2)}, u32[]{:S(2)}) async-start(bf16[128,8,256]{2,1,0:T(8,128)(2,1)} %bitcast.7), calls=%async_computation.1 | async-start | bytes 1048576 | tf_op jit(solution)/shard_map/hop_two/all_to_all | solution.py:24
  47.7 20.8 %collective-permute-start = (bf16[224,128]{1,0:T(8,128)(2,1)}, bf16[224,128]{1,0:T(8,128)(2,1)S(1)}, u32[]{:S(2)}, u32[]{:S(2)}) collective-permute-start(bf16[224,128]{1,0:T(8,128)(2,1)} %get-tuple-element.43), channel_id=1, source_target_pairs={{0,1},{1,2},{2,3},{3,0},{4,5},{5,6},{6,7},{7,4},{8,9},{9,10},{10,1... | collective-permute-start | bytes 172040 | tf_op jit(solution)/shard_map/weights/ppermute | solution.py:125
  50.8 17.7 %collective-permute-start.1 = (bf16[224,128]{1,0:T(8,128)(2,1)}, bf16[224,128]{1,0:T(8,128)(2,1)S(1)}, u32[]{:S(2)}, u32[]{:S(2)}) collective-permute-start(bf16[224,128]{1,0:T(8,128)(2,1)} %get-tuple-element.44), channel_id=1, source_target_pairs={{0,2},{1,3},{2,0},{3,1},{4,6},{5,7},{6,4},{7,5},{8,10},{9,11},{10,... | collective-permute-start | bytes 172040 | tf_op jit(solution)/shard_map/weights/ppermute | solution.py:125
  55.2 13.4 %collective-permute-start.2 = (bf16[224,128]{1,0:T(8,128)(2,1)}, bf16[224,128]{1,0:T(8,128)(2,1)S(1)}, u32[]{:S(2)}, u32[]{:S(2)}) collective-permute-start(bf16[224,128]{1,0:T(8,128)(2,1)} %get-tuple-element.45), channel_id=1, source_target_pairs={{0,3},{1,0},{2,1},{3,2},{4,7},{5,4},{6,5},{7,6},{8,11},{9,8},{10,9... | collective-permute-start | bytes 172040 | tf_op jit(solution)/shard_map/weights/ppermute | solution.py:125
  68.2 13.5 %copy-start.1 = (bf16[640,896]{1,0:T(8,128)(2,1)S(1)}, bf16[640,896]{1,0:T(8,128)(2,1)}, u32[]{:S(2)}) copy-start(bf16[640,896]{1,0:T(8,128)(2,1)} %down_ref.1) | copy-start | bytes 3440644
  85.2 27.6 %copy-start.2 = (bf16[896,128]{1,0:T(8,128)(2,1)S(1)}, bf16[896,128]{1,0:T(8,128)(2,1)}, u32[]{:S(2)}) copy-start(bf16[896,128]{1,0:T(8,128)(2,1)} %param.19) | copy-start | bytes 688132
  85.2 27.6 %copy-start.3 = (bf16[128,896]{1,0:T(8,128)(2,1)S(1)}, bf16[128,896]{1,0:T(8,128)(2,1)}, u32[]{:S(2)}) copy-start(bf16[128,896]{1,0:T(8,128)(2,1)} %proj_ref.3) | copy-start | bytes 688132
  112.8 37.9 %copy-start.4 = (bf16[224,256]{1,0:T(8,128)(2,1)S(1)}, bf16[224,256]{1,0:T(8,128)(2,1)}, u32[]{:S(2)}) copy-start(bf16[224,256]{1,0:T(8,128)(2,1)} %get-tuple-element.63.refs_5_) | copy-start | bytes 344068
  117.0 8.9 %collective-permute-start.6 = (bf16[512,384]{1,0:T(8,128)(2,1)S(1)}, bf16[512,384]{1,0:T(8,128)(2,1)S(1)}, u32[]{:S(2)}, u32[]{:S(2)}) collective-permute-start(bf16[512,384]{1,0:T(8,128)(2,1)S(1)} %get-tuple-element.69), channel_id=1, source_target_pairs={{0,4},{4,0},{1,5},{5,1},{2,6},{6,2},{3,7},{7,3},{8,12},{12,8},{9,1... | collective-permute-start | bytes 1179656 | tf_op jit(solution)/shard_map/core_sum/ppermute | solution.py:464
  126.7 20.0 %all-to-all-start.3 = ((bf16[64,8,384]{2,1,0:T(8,128)(2,1)}), bf16[64,8,384]{2,1,0:T(8,128)(2,1)S(1)}, u32[]{:S(2)}, u32[]{:S(2)}) async-start(bf16[64,8,384]{2,1,0:T(8,128)(2,1)} %bitcast.18), calls=%async_computation.3 | async-start | bytes 786432 | tf_op jit(solution)/shard_map/weight_grads/all_to_all | solution.py:24
  132.5 18.2 %collective-permute-start.3 = (bf16[464,256]{1,0:T(8,128)(2,1)S(1)}, bf16[464,256]{1,0:T(8,128)(2,1)S(1)}, u32[]{:S(2)}, u32[]{:S(2)}) collective-permute-start(bf16[464,256]{1,0:T(8,128)(2,1)S(1)} %get-tuple-element.60), channel_id=1, source_target_pairs={{0,1},{1,2},{2,3},{3,0},{4,5},{5,6},{6,7},{7,4},{8,9},{9,10},{10,1... | collective-permute-start | bytes 712712 | tf_op jit(solution)/shard_map/last_sum/ppermute | solution.py:125
  134.8 15.9 %collective-permute-start.4 = (bf16[464,256]{1,0:T(8,128)(2,1)S(1)}, bf16[464,256]{1,0:T(8,128)(2,1)S(1)}, u32[]{:S(2)}, u32[]{:S(2)}) collective-permute-start(bf16[464,256]{1,0:T(8,128)(2,1)S(1)} %get-tuple-element.61), channel_id=1, source_target_pairs={{0,2},{1,3},{2,0},{3,1},{4,6},{5,7},{6,4},{7,5},{8,10},{9,11},{10,... | collective-permute-start | bytes 712712 | tf_op jit(solution)/shard_map/last_sum/ppermute | solution.py:125
  139.1 11.6 %collective-permute-start.5 = (bf16[464,256]{1,0:T(8,128)(2,1)S(1)}, bf16[464,256]{1,0:T(8,128)(2,1)S(1)}, u32[]{:S(2)}, u32[]{:S(2)}) collective-permute-start(bf16[464,256]{1,0:T(8,128)(2,1)S(1)} %get-tuple-element.62), channel_id=1, source_target_pairs={{0,3},{1,0},{2,1},{3,2},{4,7},{5,4},{6,5},{7,6},{8,11},{9,8},{10,9... | collective-permute-start | bytes 712712 | tf_op jit(solution)/shard_map/last_sum/ppermute | solution.py:125
  147.4 7.4 %all-to-all-start.4 = ((f32[4,7,128]{2,1,0:T(8,128)}), f32[4,7,128]{2,1,0:T(8,128)S(1)}, u32[]{:S(2)}, u32[]{:S(2)}) async-start(f32[4,7,128]{2,1,0:T(8,128)} %get-tuple-element.71), calls=%async_computation.4 | async-start | bytes 32768 | tf_op jit(solution)/shard_map/key_grads/all_to_all | solution.py:24

commit v5 on v4

--- a/solution.py
+++ b/solution.py
@@ -57,7 +57,7 @@
     out_ref[4] = lax.axis_index("seq_2")
 
 
-def call(kernel, out_shape, *args, scratch=(), smem=0, out=pltpu.VMEM, mib=16, name=None):
+def call(kernel, out_shape, *args, scratch=(), smem=0, out=pltpu.VMEM, mib=16):
     spaces = [pltpu.SMEM] * smem + [pltpu.VMEM] * (len(args) - smem)
     one = not isinstance(out_shape, tuple)
     outs = [out] * (1 if one else len(out_shape))
@@ -70,7 +70,6 @@
         scratch_shapes=scratch,
         interpret=INTERPRET,
         compiler_params=pltpu.CompilerParams(vmem_limit_bytes=mib * 2**20),
-        name=name,
     )(*args)
 
 
@@ -83,7 +82,10 @@
     return jnp.concatenate([ref[pl.ds(j, 1), at, :][0] for j in range(ref.shape[0])], axis=1)
 
 
-def pack_kernel(streams_ref, out_ref, rows_ref):
+def pack_kernel(streams_ref, keyval_ref, out_ref, *refs):
+    *piece_refs, rows_ref = refs
+    for k, piece_ref in enumerate(piece_refs):
+        piece_ref[...] = keyval_ref[((lax.axis_index("mp") + k) % MP) // 2]
     width = streams_ref.shape[0] // 4
     gap = jnp.zeros((out_ref.shape[1] - width, streams_ref.shape[1]), F32)
     for k in range(4):
@@ -95,30 +97,46 @@
     out_ref[...] = get(rows_ref, slice(None)).astype(BF16)
 
 
-def reorder_kernel(plan_ref, held_ref, keyval_ref, out_ref, *refs):
-    *piece_refs, rows_ref, next_ref = refs
-    for k, piece_ref in enumerate(piece_refs):
-        piece_ref[...] = keyval_ref[((lax.axis_index("mp") + k) % MP) // 2]
+def reorder_kernel(plan_ref, held_ref, *refs):
+    *out_refs, rows_ref, next_ref = refs
     blocks = plan_ref.shape[1]
     slot = lax.broadcasted_iota(jnp.int32, (blocks, blocks), 0)
     pick = (plan_ref[...] == slot).astype(BF16)
     put(rows_ref, slice(None), held_ref[...].astype(F32))
     for k in range(4):
-        at = pl.ds(k, blocks, stride=4)
-        put(next_ref, at, dot(pick, get(rows_ref, at).astype(BF16), NN))
-    out_ref[...] = get(next_ref, slice(None)).astype(BF16)
-
-
-def unpack_kernel(rows_in_ref, send_ref, kept_ref, rows_ref):
-    width = kept_ref.shape[0] // 4
-    put(rows_ref, slice(None), rows_in_ref[...].astype(F32))
-    for k in range(4):
-        halves = [get(rows_ref, pl.ds(4 * t + k, BLOCK, stride=8)).T for t in range(2)]
-        stream = jnp.concatenate(halves, axis=1)[:width].astype(BF16)
-        at = slice(k * width, (k + 1) * width)
-        kept_ref[at, :] = stream
-        if k < 2:
-            send_ref[at, :] = stream
+        rows = dot(pick, get(rows_ref, pl.ds(k, blocks, stride=4)).astype(BF16), NN)
+        for j in range(2):
+            at = pl.ds(2 * (k % 2) + j, blocks, stride=4)
+            next_ref[pl.ds(k // 2, 1), at, :] = rows[None, :, j * 128 : (j + 1) * 128]
+    for h, out_ref in enumerate(out_refs):
+        out_ref[...] = next_ref[h].astype(BF16)
+
+
+def unpack_kernel(rows_in_ref, *refs):
+    *out_refs, rows_ref = refs
+    width = out_refs[0].shape[0] // 2
+    rows_ref[0] = rows_in_ref[...].astype(F32)
+    for k in range(2):
+        halves = []
+        for t in range(2):
+            lanes = [
+                rows_ref[pl.ds(0, 1), pl.ds(4 * t + 2 * k + j, BLOCK, stride=8), :][0].T
+                for j in range(2)
+            ]
+            halves.append(jnp.concatenate(lanes, axis=0)[:width])
+        stream = jnp.concatenate(halves, axis=1).astype(BF16)
+        for out_ref in out_refs:
+            out_ref[k * width : (k + 1) * width, :] = stream
+
+
+def unpack(owned, width, copies):
+    rows = 8 * BLOCK
+    return call(
+        unpack_kernel,
+        (jax.ShapeDtypeStruct((2 * width, 2 * BLOCK), BF16),) * copies,
+        owned.reshape(rows, 128),
+        scratch=[pltpu.VMEM((1, rows, 128), F32)],
+    )
 
 
 def turn(value, by):
@@ -134,63 +152,60 @@
     rows = 8 * BLOCK
     piece = jax.ShapeDtypeStruct(kv_weight.shape[1:], BF16)
     scratch = pltpu.VMEM((lanes // 128, rows, 128), F32)
-    sent = call(
+    sent, *pieces = call(
         pack_kernel,
-        jax.ShapeDtypeStruct((rows, lanes), BF16),
+        (jax.ShapeDtypeStruct((rows, lanes), BF16), *[piece] * MP),
         jnp.concatenate(streams, axis=0),
+        kv_weight,
         scratch=[scratch],
-        name="pack",
     )
     facts = call(
         facts_kernel,
         jax.ShapeDtypeStruct((5,), jnp.int32),
         *[table.reshape(1, -1) for table in tables],
         out=pltpu.SMEM,
-        name="facts",
-    )
-    with jax.named_scope("hop_one"):
-        held = exchange(sent.reshape(peers, share * 8, lanes), SEQ)
+    )
+    held = exchange(sent.reshape(peers, share * 8, lanes), SEQ)
+    pieces = [pieces[0]] + [turn(pieces[k], k) for k in range(1, MP)]
     held = held.reshape(peers, share, 8, lanes)
     placed = []
     for r in range(share):
-        moved, *pieces = call(
-            reorder_kernel,
-            (jax.ShapeDtypeStruct((peers * 8, lanes), BF16), *[piece] * MP),
-            plan.reshape(1, -1),
-            held[:, r].reshape(peers * 8, lanes),
-            kv_weight,
-            scratch=[pltpu.VMEM((lanes // 128, peers * 8, 128), F32)] * 2,
-            name="reorder",
+        placed.append(
+            call(
+                reorder_kernel,
+                (jax.ShapeDtypeStruct((peers * 8, 128), BF16),) * 2,
+                plan.reshape(1, -1),
+                held[:, r].reshape(peers * 8, lanes),
+                scratch=[pltpu.VMEM((2, peers * 8, 128), F32)] * 2,
+            )
         )
-        placed.append(moved.reshape(peers, 8, lanes))
-    placed = placed[0] if share == 1 else jnp.stack(placed, axis=1).reshape(peers, -1, lanes)
-    with jax.named_scope("weights"):
-        pieces = [pieces[0]] + [turn(pieces[k], k) for k in range(1, MP)]
-    with jax.named_scope("hop_two"):
-        owned = exchange(placed, SEQ)
-    return facts, pieces, *call(
-        unpack_kernel,
-        (
-            jax.ShapeDtypeStruct((2 * width, 2 * BLOCK), BF16),
-            jax.ShapeDtypeStruct((4 * width, 2 * BLOCK), BF16),
-        ),
-        owned.reshape(rows, lanes),
-        scratch=[scratch],
-        name="unpack",
-    )
-
-
-def assemble(rows_ref, whole_ref, first):
-    parts, both, _ = rows_ref.shape
-    width = both // 2
-    for m in range(parts):
-        whole_ref[m * width : (m + 1) * width, :] = rows_ref[m, first : first + width, :]
+    owned = []
+    for h in range(2):
+        halves = [p[h].reshape(peers, 8, 128) for p in placed]
+        halves = halves[0] if share == 1 else jnp.stack(halves, axis=1).reshape(peers, -1, 128)
+        owned.extend(unpack(exchange(halves, SEQ), width, 3 - 2 * h))
+    return facts, pieces, *owned
+
+
+def around(value):
+    return [value] + [turn(value, k) for k in range(1, MP)]
+
+
+def assemble(me, pieces, whole_ref, first):
+    parts, width, _ = whole_ref.shape
+    for k, piece in enumerate(pieces):
+        whole_ref[(me + parts - k) % parts] = piece[first : first + width, :]
 
 
 def normalized(whole_ref):
-    values = whole_ref[...].astype(F32)
+    values = merged(whole_ref).astype(F32)
     inverse = lax.rsqrt(jnp.mean(values * values, axis=0, keepdims=True) + EPSILON)
     return (values * inverse).astype(BF16), inverse
+
+
+def merged(ref):
+    values = ref[...]
+    return values.reshape(-1, values.shape[-1])
 
 
 def row_sums(values, width):
@@ -201,32 +216,36 @@
     return (sums / width).astype(BF16)
 
 
-def feed_forward_kernel(
-    rows_ref, gate_up_ref, down_ref, out_ref, inverse_ref, first_ref, second_ref
-):
-    parts, both, count = rows_ref.shape
-    width = both // 2
-    assemble(rows_ref, first_ref, 0)
-    assemble(rows_ref, second_ref, width)
+def feed_forward_kernel(facts_ref, *refs):
+    pieces, refs = refs[:MP], refs[MP:]
+    gate_up_ref, down_ref = refs[:2]
+    out_refs = refs[2 : 2 + MP]
+    inverse_ref, first_ref, second_ref, mixed_ref = refs[2 + MP :]
+    gate_ref, up_ref = gate_up_ref.at[0], gate_up_ref.at[1]
+    parts, width, _ = first_ref.shape
+    both = 2 * width
+    me = facts_ref[3]
+    assemble(me, pieces, first_ref, 0)
+    assemble(me, pieces, second_ref, width)
     normed, inverse_ref[...] = normalized(first_ref)
     normed = normed.T
-    gate = dot(normed, gate_up_ref[0], NN)
-    up = dot(normed, gate_up_ref[1], NN)
-    dh = dot(second_ref[...].T, down_ref[...], NT)
+    gate = dot(normed, merged(gate_ref), NN)
+    up = dot(normed, merged(up_ref), NN)
+    dh = dot(merged(second_ref).T, down_ref[...], NT)
     sigma = jax.nn.sigmoid(gate)
     silu = gate * sigma
     hidden = (silu * up).astype(BF16)
     d_gate = (dh * up * sigma * (1.0 + gate * (1.0 - sigma))).astype(BF16)
     d_up = (dh * silu).astype(BF16)
     inner = row_sums(d_gate.astype(F32) * gate + d_up.astype(F32) * up, parts * width)
-    mixed = dot(hidden, down_ref[...], NN).astype(BF16).T
-    for m in range(parts):
-        at = slice(m * width, (m + 1) * width)
-        out_ref[m, :width, :] = mixed[at]
-        out_ref[m, width:both, :] = (
-            dot(gate_up_ref[0, at, :], d_gate, NT) + dot(gate_up_ref[1, at, :], d_up, NT)
+    mixed_ref[...] = dot(hidden, down_ref[...], NN).astype(BF16).T.reshape(mixed_ref.shape)
+    for k in range(parts):
+        m = (me + k) % parts
+        out_refs[k][:width, :] = mixed_ref[m]
+        out_refs[k][width:both, :] = (
+            dot(gate_ref[m], d_gate, NT) + dot(up_ref[m], d_up, NT)
         ).astype(BF16)
-        out_ref[m, both:, :] = inner
+        out_refs[k][both:, :] = inner
 
 
 def live_columns(facts_ref, shape):
@@ -234,18 +253,17 @@
     return column < jnp.where(column < BLOCK, facts_ref[0], facts_ref[1] + BLOCK)
 
 
-def middle_kernel(
-    facts_ref, parts_ref, kept_ref, inverse_ref, second_ref, first_cot_ref, send_ref
-):
-    parts, rows, count = parts_ref.shape
-    width = (rows - PAD) // 2
-    total = parts_ref[0].astype(F32)
-    for m in range(1, parts):
-        total += parts_ref[m].astype(F32)
+def middle_kernel(facts_ref, *refs):
+    parts, refs = refs[:MP], refs[MP:]
+    first_half_ref, second_half_ref, inverse_ref, second_ref, first_cot_ref, send_ref = refs
+    width = second_ref.shape[0]
+    total = parts[0][...].astype(F32)
+    for part in parts[1:]:
+        total += part[...].astype(F32)
     inverse = inverse_ref[...]
-    first = kept_ref[:width, :].astype(F32)
-    second = kept_ref[2 * width : 3 * width, :].astype(F32)
-    cot = kept_ref[3 * width :, :].astype(F32)
+    first = first_half_ref[:width, :].astype(F32)
+    second = second_half_ref[:width, :].astype(F32)
+    cot = second_half_ref[width:, :].astype(F32)
     second = (second - total[:width]).astype(BF16)
     d_norm = total[width : 2 * width]
     inner = total[2 * width : 2 * width + 1]
@@ -286,14 +304,15 @@
     me = facts_ref[3]
     for k in range(parts):
         keyval_ref[(me + parts - k) % parts] = pieces[k][...]
-    assemble(rows_ref, second_ref, 0)
-    assemble(rows_ref, cot_ref, width)
+    for m in range(parts):
+        second_ref[m] = rows_ref[m, :width, :]
+        cot_ref[m] = rows_ref[m, width:, :]
     normed, inverse_ref[...] = normalized(second_ref)
     turned = normed.T
     whole = keyval_ref[...].reshape(parts * width, -1)
     query = dot(turned, query_ref[...].reshape(parts * width, -1), NN).astype(BF16)
     keyval = dot(turned, whole, NN).astype(BF16)
-    d_out = dot(cot_ref[...].T, proj_ref[...], NT).astype(BF16)
+    d_out = dot(merged(cot_ref).T, proj_ref[...], NT).astype(BF16)
     half = keyval.shape[1] // 2
     low = lax.broadcasted_iota(jnp.int32, keyval.shape, 1) < half
     wide = keyval.astype(F32)
@@ -342,7 +361,7 @@
     for m in range(parts):
         at = slice(m * width, (m + 1) * width)
         grads = [dot(normed[at], d_query, NN), dot(normed[at], d_keyval, NN)]
-        grads.append(dot(cot_ref[at, :], heads, NN))
+        grads.append(dot(cot_ref[m], heads, NN))
         grads = jnp.concatenate(grads, axis=1).astype(BF16)
         grads = dot(pick, grads, NN).astype(BF16)
         to = slice(m * (lines // 2), (m + 1) * (lines // 2))
@@ -408,37 +427,34 @@
     seq_size = lax.axis_size(SEQ)
     groups = kv_weight.shape[0]
     streams = (y_first.T, grad_second.T, y_second.T, grad_first.T)
-    facts, pieces, send, kept = to_slots(streams, kv_weight, doc_blocks, last_fill, plan)
-    send, facts, pieces = lax.optimization_barrier((send, facts, pieces))
+    facts, pieces, send, near, kept, other = to_slots(streams, kv_weight, doc_blocks, last_fill, plan)
     stream = jax.ShapeDtypeStruct((width, count), BF16)
     line = jax.ShapeDtypeStruct((1, count), F32)
     part = jax.ShapeDtypeStruct((2 * width + PAD, count), BF16)
-    with jax.named_scope("gather_one"):
-        rows = lax.all_gather(send, "mp", axis=0)
-    whole = pltpu.VMEM((MP * width, count), BF16)
-    parts, r_one = call(
+    whole = pltpu.VMEM((MP, width, count), BF16)
+    rows = [near] + around(send)[1:]
+    *parts, r_one = call(
         feed_forward_kernel,
-        (jax.ShapeDtypeStruct((MP, *part.shape), BF16), line),
-        rows,
-        gate_up,
+        (*[part] * MP, line),
+        facts,
+        *rows,
+        gate_up.reshape(2, MP, width, -1),
         down_weight,
-        scratch=[whole, whole],
-        name="feed_forward",
-    )
-    with jax.named_scope("sum_one"):
-        parts = exchange(parts, "mp")
+        scratch=[whole] * 3,
+        smem=1,
+    )
+    parts = [parts[0]] + [turn(parts[k], k) for k in range(1, MP)]
     second_in, first_cot, send = call(
         middle_kernel,
         (stream, stream, jax.ShapeDtypeStruct((2 * width, count), BF16)),
         facts,
-        parts,
+        *parts,
         kept,
+        other,
         r_one,
         smem=1,
-        name="middle",
-    )
-    with jax.named_scope("gather_two"):
-        rows = lax.all_gather(send, "mp", axis=0)
+    )
+    rows = lax.all_gather(send, "mp", axis=0)
     query = q_weight.reshape(MP, width, -1)
     half = jax.ShapeDtypeStruct((4 * BLOCK, 384), BF16)
     kept_grads, given, makings, keyval, inner, r_two = call(
@@ -458,13 +474,10 @@
         *pieces,
         scratch=[whole, whole, pltpu.VMEM((2, *half.shape), BF16)],
         smem=1,
-        name="attention",
-    )
-    with jax.named_scope("core_sum"):
-        given = lax.ppermute(given, "seq_2", [(0, 1), (1, 0)])
-    grads = call(add_kernel, half, kept_grads, given, name="add")
-    with jax.named_scope("weight_grads"):
-        grads = exchange(grads.reshape(seq_size // 2, -1, grads.shape[1]), SEQ[:2])
+    )
+    given = lax.ppermute(given, "seq_2", [(0, 1), (1, 0)])
+    grads = call(add_kernel, half, kept_grads, given)
+    grads = exchange(grads.reshape(seq_size // 2, -1, grads.shape[1]), SEQ[:2])
     parts = call(
         pieces_kernel,
         (part,) * MP,
@@ -476,28 +489,17 @@
         out_weight,
         scratch=[pltpu.VMEM((MP, width, 128), BF16)],
         smem=1,
-        name="pieces",
-    )
-    with jax.named_scope("last_sum"):
-        parts = [parts[0]] + [turn(parts[k], k) for k in range(1, MP)]
+    )
+    parts = [parts[0]] + [turn(parts[k], k) for k in range(1, MP)]
     first_in, second_cot = call(
-        last_kernel, (stream, stream), facts, *parts, kept, second_in, r_two, smem=1, name="last"
+        last_kernel, (stream, stream), facts, *parts, kept, second_in, r_two, smem=1
     )
     share = jax.ShapeDtypeStruct((7 * BLOCK // seq_size, 128), F32)
     query_grad, out_grad, own = call(
-        finish_kernel,
-        (share, share, jax.ShapeDtypeStruct((MP, *share.shape), F32)),
-        grads,
-        name="finish",
-    )
-    with jax.named_scope("key_grads"):
-        shares = exchange(own, "mp")
-    kv_grad = call(
-        pair_kernel,
-        jax.ShapeDtypeStruct((shares.shape[1], groups, 128), F32),
-        shares,
-        name="pair",
-    )
+        finish_kernel, (share, share, jax.ShapeDtypeStruct((MP, *share.shape), F32)), grads
+    )
+    shares = exchange(own, "mp")
+    kv_grad = call(pair_kernel, jax.ShapeDtypeStruct((shares.shape[1], groups, 128), F32), shares)
     return (
         first_in.T,
         second_in.T,

time: 158 us -> 187 us (1.18)
  starting transfers between devices: 40.3 us -> 66.5 us
  local copies, waits for them, and re-layouts: 0.04 us -> 8.44 us
  blocking collectives: 78.3 us -> 71.8 us
  Pallas kernels: 16.3 us -> 18.6 us
    ppermute x6 -> x12, starting transfers between devices: 19.5 us -> 37 us  [turn(): return lax.ppermute(value, 'mp', [(i, (i + by) % MP) for i in range(MP)])]
    all_gather x2 -> x1, blocking collectives: 24.6 us -> 12.5 us  [shards(): rows = lax.all_gather(send, 'mp', axis=0)]
    all_to_all x3, starting transfers between devices: 13.3 us -> 22.5 us  [exchange(): return lax.all_to_all(value, axis, split_axis=0, concat_axis=0, tiled=True)]
    all_to_all x3, waiting for transfers between devices: 17.1 us -> 7.88 us  [exchange(): return lax.all_to_all(value, axis, split_axis=0, concat_axis=0, tiled=True)]
    unnamed x18 -> x36, local copies, waits for them, and re-layouts: 0.04 us -> 8.44 us
    ppermute x6 -> x12, waiting for transfers between devices: 0.02 us -> 7.51 us  [turn(): return lax.ppermute(value, 'mp', [(i, (i + by) % MP) for i in range(MP)])]
    all_to_all x2, blocking collectives: 53.7 us -> 59.3 us  [exchange(): return lax.all_to_all(value, axis, split_axis=0, concat_axis=0, tiled=True)]
    pallas_call x12 -> x13, Pallas kernels: 16.3 us -> 18.6 us  [call(): pl.pallas_call(kernel, in_specs=[pl.BlockSpec(memory_space=s) for s in sp...]
  transfers between devices with their start and end apart: 10 -> 16, of which waited for: 4 -> 5; matrix products, arithmetic and copies ran while one was open for 0% -> 0% of each run, Pallas kernels for 3% -> 6%
where the time goes in v5:
time: 187 us; the launch traced here: 184 us
  blocking collectives  71.8 us (38%)
  starting transfers between devices  66.5 us (36%)
  Pallas kernels  18.6 us (10%)
  waiting for transfers between devices  16.7 us (9%)
  local copies, waits for them, and re-layouts  8.44 us (5%)
    all_to_all x2, blocking collectives, exchange(): return lax.all_to_all(value, axis, split_axis=0, concat_axis=0, tiled=True)  59.3 us
    ppermute x12, starting transfers between devices, turn(): return lax.ppermute(value, 'mp', [(i, (i + by) % MP) for i in range(MP)])  37 us
    all_to_all x3, starting transfers between devices, exchange(): return lax.all_to_all(value, axis, split_axis=0, concat_axis=0, tiled=True)  22.5 us
    pallas_call x13, Pallas kernels, call(): pl.pallas_call(kernel, in_specs=[pl.BlockSpec(memory_space=s) for s in sp...  18.6 us
    all_gather x1, blocking collectives, shards(): rows = lax.all_gather(send, 'mp', axis=0)  12.5 us
    unnamed x36, local copies, waits for them, and re-layouts  8.44 us
    all_to_all x3, waiting for transfers between devices, exchange(): return lax.all_to_all(value, axis, split_axis=0, concat_axis=0, tiled=True)  7.88 us
    ppermute x12, waiting for transfers between devices, turn(): return lax.ppermute(value, 'mp', [(i, (i + by) % MP) for i in range(MP)])  7.51 us
  transfers between devices with their start and end apart: 16, of which 5 were waited for; matrix products, arithmetic and copies ran while one was open for 0% of the time, Pallas kernels for 6%

profile of v5, /device:TPU:1, one launch (start us, length us, event | category | flops | bytes accessed | tf_op | source)
XLA Modules:
  0.0 184.3 jit_solution(5077808219999292196)
XLA Ops:
  4.3 38.8 %all_to_all.25 = bf16[128,8,256]{2,1,0:T(8,128)(2,1)S(1)} all-to-all(bf16[128,8,256]{2,1,0:T(8,128)(2,1)S(1)} %bitcast.29), channel_id=1, replica_groups=mesh['seq_0'=8,'seq_1'=8,'seq_2'=2,'mp'=4] {'seq_0','seq_1','seq_2'}, dimensions={0} | all-to-all | bytes 1048576 | tf_op jit(solution)/shard_map/all_to_all | solution.py:24
  44.2 20.5 %all_to_all.26 = bf16[128,8,128]{2,1,0:T(8,128)(2,1)} all-to-all(bf16[128,8,128]{2,1,0:T(8,128)(2,1)S(1)} %bitcast.31), channel_id=1, replica_groups=mesh['seq_0'=8,'seq_1'=8,'seq_2'=2,'mp'=4] {'seq_0','seq_1','seq_2'}, dimensions={0} | all-to-all | bytes 524288 | tf_op jit(solution)/shard_map/all_to_all | solution.py:24
  64.8 6.6 %all-to-all-start.2 = ((bf16[128,8,128]{2,1,0:T(8,128)(2,1)}), bf16[128,8,128]{2,1,0:T(8,128)(2,1)}, u32[]{:S(2)}, u32[]{:S(2)}) async-start(bf16[128,8,128]{2,1,0:T(8,128)(2,1)} %bitcast.30), calls=%async_computation.2 | async-start | bytes 524288 | tf_op jit(solution)/shard_map/all_to_all | solution.py:24
  73.1 4.4 %collective-permute-start.2 = (bf16[448,256]{1,0:T(8,128)(2,1)S(1)}, bf16[448,256]{1,0:T(8,128)(2,1)S(1)}, u32[]{:S(2)}, u32[]{:S(2)}) collective-permute-start(bf16[448,256]{1,0:T(8,128)(2,1)S(1)} %get-tuple-element.43), channel_id=1, source_target_pairs={{0,3},{1,0},{2,1},{3,2},{4,7},{5,4},{6,5},{7,6},{8,11},{9,8},{10,9... | collective-permute-start | bytes 688136 | tf_op jit(solution)/shard_map/ppermute | solution.py:143
  77.5 2.4 %collective-permute-start.1 = (bf16[448,256]{1,0:T(8,128)(2,1)S(1)}, bf16[448,256]{1,0:T(8,128)(2,1)S(1)}, u32[]{:S(2)}, u32[]{:S(2)}) collective-permute-start(bf16[448,256]{1,0:T(8,128)(2,1)S(1)} %get-tuple-element.43), channel_id=1, source_target_pairs={{0,2},{1,3},{2,0},{3,1},{4,6},{5,7},{6,4},{7,5},{8,10},{9,11},{10,... | collective-permute-start | bytes 688136 | tf_op jit(solution)/shard_map/ppermute | solution.py:143
  79.9 2.5 %collective-permute-start = (bf16[448,256]{1,0:T(8,128)(2,1)S(1)}, bf16[448,256]{1,0:T(8,128)(2,1)S(1)}, u32[]{:S(2)}, u32[]{:S(2)}) collective-permute-start(bf16[448,256]{1,0:T(8,128)(2,1)S(1)} %get-tuple-element.43), channel_id=1, source_target_pairs={{0,1},{1,2},{2,3},{3,0},{4,5},{5,6},{6,7},{7,4},{8,9},{9,10},{10,1... | collective-permute-start | bytes 688136 | tf_op jit(solution)/shard_map/ppermute | solution.py:143
  86.7 6.2 %collective-permute-done.refs_1_ = bf16[448,256]{1,0:T(8,128)(2,1)S(1)} collective-permute-done((bf16[448,256]{1,0:T(8,128)(2,1)S(1)}, bf16[448,256]{1,0:T(8,128)(2,1)S(1)}, u32[]{:S(2)}, u32[]{:S(2)}) %collective-permute-start) | collective-permute-done | bytes 229408 | tf_op jit(solution)/shard_map/ppermute | solution.py:143
  92.9 4.9 %shard_map.175 = (bf16[464,256]{1,0:T(8,128)(2,1)S(1)}, bf16[464,256]{1,0:T(8,128)(2,1)}, bf16[464,256]{1,0:T(8,128)(2,1)}, bf16[464,256]{1,0:T(8,128)(2,1)}, f32[1,256]{1,0:T(1,128)S(1)}) custom-call(s32[5]{0:T(128)S(1)} %shard_map.171.facts_ref, bf16[448,256]{1,0:T(8,128)(2,1)S(1)} %get-tuple-element.42.refs_0_, ...), custom_call_target="tpu_custom_call" | custom-call | tf_op jit(solution)/shard_map/pallas_call | solution.py:65
  98.5 2.0 %collective-permute-start.3 = (bf16[464,256]{1,0:T(8,128)(2,1)}, bf16[464,256]{1,0:T(8,128)(2,1)S(1)}, u32[]{:S(2)}, u32[]{:S(2)}) collective-permute-start(bf16[464,256]{1,0:T(8,128)(2,1)} %get-tuple-element.45), channel_id=1, source_target_pairs={{0,1},{1,2},{2,3},{3,0},{4,5},{5,6},{6,7},{7,4},{8,9},{9,10},{10,1... | collective-permute-start | bytes 712712 | tf_op jit(solution)/shard_map/ppermute | solution.py:143
  100.5 2.3 %collective-permute-start.4 = (bf16[464,256]{1,0:T(8,128)(2,1)}, bf16[464,256]{1,0:T(8,128)(2,1)S(1)}, u32[]{:S(2)}, u32[]{:S(2)}) collective-permute-start(bf16[464,256]{1,0:T(8,128)(2,1)} %get-tuple-element.46), channel_id=1, source_target_pairs={{0,2},{1,3},{2,0},{3,1},{4,6},{5,7},{6,4},{7,5},{8,10},{9,11},{10,... | collective-permute-start | bytes 712712 | tf_op jit(solution)/shard_map/ppermute | solution.py:143
  102.9 4.1 %collective-permute-start.5 = (bf16[464,256]{1,0:T(8,128)(2,1)}, bf16[464,256]{1,0:T(8,128)(2,1)S(1)}, u32[]{:S(2)}, u32[]{:S(2)}) collective-permute-start(bf16[464,256]{1,0:T(8,128)(2,1)} %get-tuple-element.47), channel_id=1, source_target_pairs={{0,3},{1,0},{2,1},{3,2},{4,7},{5,4},{6,5},{7,6},{8,11},{9,8},{10,9... | collective-permute-start | bytes 712712 | tf_op jit(solution)/shard_map/ppermute | solution.py:143
  107.0 2.5 %collective-permute-start.6 = (bf16[224,128]{1,0:T(8,128)(2,1)}, bf16[224,128]{1,0:T(8,128)(2,1)S(1)}, u32[]{:S(2)}, u32[]{:S(2)}) collective-permute-start(bf16[224,128]{1,0:T(8,128)(2,1)} %get-tuple-element.53), channel_id=1, source_target_pairs={{0,1},{1,2},{2,3},{3,0},{4,5},{5,6},{6,7},{7,4},{8,9},{9,10},{10,1... | collective-permute-start | bytes 172040 | tf_op jit(solution)/shard_map/ppermute | solution.py:143
  109.5 3.7 %collective-permute-start.7 = (bf16[224,128]{1,0:T(8,128)(2,1)}, bf16[224,128]{1,0:T(8,128)(2,1)S(1)}, u32[]{:S(2)}, u32[]{:S(2)}) collective-permute-start(bf16[224,128]{1,0:T(8,128)(2,1)} %get-tuple-element.54), channel_id=1, source_target_pairs={{0,2},{1,3},{2,0},{3,1},{4,6},{5,7},{6,4},{7,5},{8,10},{9,11},{10,... | collective-permute-start | bytes 172040 | tf_op jit(solution)/shard_map/ppermute | solution.py:143
  114.4 4.0 %collective-permute-start.8 = (bf16[224,128]{1,0:T(8,128)(2,1)}, bf16[224,128]{1,0:T(8,128)(2,1)S(1)}, u32[]{:S(2)}, u32[]{:S(2)}) collective-permute-start(bf16[224,128]{1,0:T(8,128)(2,1)} %copy-done.17), channel_id=1, source_target_pairs={{0,3},{1,0},{2,1},{3,2},{4,7},{5,4},{6,5},{7,6},{8,11},{9,8},{10,9... | collective-permute-start | bytes 172040 | tf_op jit(solution)/shard_map/ppermute | solution.py:143
  121.6 12.5 %all-gather = bf16[1792,256]{1,0:T(8,128)(2,1)S(1)} all-gather(bf16[448,256]{1,0:T(8,128)(2,1)S(1)} %get-tuple-element.51), channel_id=2, replica_groups=mesh['seq_0'=8,'seq_1'=8,'seq_2'=2,'mp'=4] {'mp'}, dimensions={0}, use_global_device_ids=true | all-gather | bytes 1146880 | tf_op jit(solution)/shard_map/all_gather | solution.py:457
  134.2 4.2 %shard_map.178 = (bf16[512,384]{1,0:T(8,128)(2,1)S(1)}, bf16[512,384]{1,0:T(8,128)(2,1)S(1)}, bf16[3,256,128]{2,1,0:T(8,128)(2,1)S(1)}, bf16[4,224,128]{2,1,0:T(...) custom-call(s32[5]{0:T(128)S(1)} %shard_map.171.facts_ref, bf16[4,448,256]{2,1,0:T(8,128)(2,1)S(1)} %bitcast.23, ...), custom_call_target="tpu_custom_call" | custom-call | tf_op jit(solution)/shard_map/pallas_call | solution.py:65
  138.3 7.0 %collective-permute-start.12 = (bf16[512,384]{1,0:T(8,128)(2,1)S(1)}, bf16[512,384]{1,0:T(8,128)(2,1)S(1)}, u32[]{:S(2)}, u32[]{:S(2)}) collective-permute-start(bf16[512,384]{1,0:T(8,128)(2,1)S(1)} %get-tuple-element.69), channel_id=1, source_target_pairs={{0,4},{4,0},{1,5},{5,1},{2,6},{6,2},{3,7},{7,3},{8,12},{12,8},{9,1... | collective-permute-start | bytes 1179656 | tf_op jit(solution)/shard_map/ppermute | solution.py:478
  147.5 12.7 %all-to-all-start.3 = ((bf16[64,8,384]{2,1,0:T(8,128)(2,1)}), bf16[64,8,384]{2,1,0:T(8,128)(2,1)S(1)}, u32[]{:S(2)}, u32[]{:S(2)}) async-start(bf16[64,8,384]{2,1,0:T(8,128)(2,1)} %bitcast.20), calls=%async_computation.3 | async-start | bytes 786432 | tf_op jit(solution)/shard_map/all_to_all | solution.py:24
  161.4 1.9 %collective-permute-start.9 = (bf16[464,256]{1,0:T(8,128)(2,1)S(1)}, bf16[464,256]{1,0:T(8,128)(2,1)S(1)}, u32[]{:S(2)}, u32[]{:S(2)}) collective-permute-start(bf16[464,256]{1,0:T(8,128)(2,1)S(1)} %get-tuple-element.60), channel_id=1, source_target_pairs={{0,1},{1,2},{2,3},{3,0},{4,5},{5,6},{6,7},{7,4},{8,9},{9,10},{10,1... | collective-permute-start | bytes 712712 | tf_op jit(solution)/shard_map/ppermute | solution.py:143
  163.4 3.1 %collective-permute-start.10 = (bf16[464,256]{1,0:T(8,128)(2,1)S(1)}, bf16[464,256]{1,0:T(8,128)(2,1)S(1)}, u32[]{:S(2)}, u32[]{:S(2)}) collective-permute-start(bf16[464,256]{1,0:T(8,128)(2,1)S(1)} %get-tuple-element.61), channel_id=1, source_target_pairs={{0,2},{1,3},{2,0},{3,1},{4,6},{5,7},{6,4},{7,5},{8,10},{9,11},{10,... | collective-permute-start | bytes 712712 | tf_op jit(solution)/shard_map/ppermute | solution.py:143
  166.5 4.0 %collective-permute-start.11 = (bf16[464,256]{1,0:T(8,128)(2,1)S(1)}, bf16[464,256]{1,0:T(8,128)(2,1)S(1)}, u32[]{:S(2)}, u32[]{:S(2)}) collective-permute-start(bf16[464,256]{1,0:T(8,128)(2,1)S(1)} %get-tuple-element.62), channel_id=1, source_target_pairs={{0,3},{1,0},{2,1},{3,2},{4,7},{5,4},{6,5},{7,6},{8,11},{9,8},{10,9... | collective-permute-start | bytes 712712 | tf_op jit(solution)/shard_map/ppermute | solution.py:143
  170.4 5.1 %all-to-all-done.3.grads_ref = bf16[64,8,384]{2,1,0:T(8,128)(2,1)S(1)} async-done(((bf16[64,8,384]{2,1,0:T(8,128)(2,1)}), bf16[64,8,384]{2,1,0:T(8,128)(2,1)S(1)}, u32[]{:S(2)}, u32[]{:S(2)}) %all-to-all-start.3) | async-done | bytes 393248 | tf_op jit(solution)/shard_map/all_to_all | solution.py:24
  176.3 3.2 %all-to-all-start.4 = ((f32[4,7,128]{2,1,0:T(8,128)}), f32[4,7,128]{2,1,0:T(8,128)S(1)}, u32[]{:S(2)}, u32[]{:S(2)}) async-start(f32[4,7,128]{2,1,0:T(8,128)} %get-tuple-element.71), calls=%async_computation.4 | async-start | bytes 32768 | tf_op jit(solution)/shard_map/all_to_all | solution.py:24
  180.9 2.7 %all-to-all-done.4.shares_ref = f32[4,7,128]{2,1,0:T(8,128)S(1)} async-done(((f32[4,7,128]{2,1,0:T(8,128)}), f32[4,7,128]{2,1,0:T(8,128)S(1)}, u32[]{:S(2)}, u32[]{:S(2)}) %all-to-all-start.4) | async-done | bytes 14368 | tf_op jit(solution)/shard_map/all_to_all | solution.py:24
  (61 shorter events, 21.9 us)
Async XLA Ops:
  0.6 92.2 %copy-start.1 = (bf16[640,896]{1,0:T(8,128)(2,1)S(1)}, bf16[640,896]{1,0:T(8,128)(2,1)}, u32[]{:S(2)}) copy-start(bf16[640,896]{1,0:T(8,128)(2,1)} %refs_5_.1) | copy-start | bytes 3440644
  0.6 92.2 %copy-start = (bf16[2,896,640]{2,1,0:T(8,128)(2,1)S(1)}, bf16[2,896,640]{2,1,0:T(8,128)(2,1)}, u32[]{:S(2)}) copy-start(bf16[2,896,640]{2,1,0:T(8,128)(2,1)} %param.22) | copy-start | bytes 6881284
  44.2 20.6 %copy-start.8 = (bf16[1024,128]{1,0:T(8,128)(2,1)}, bf16[1024,128]{1,0:T(8,128)(2,1)S(1)}, u32[]{:S(2)}) copy-start(bf16[1024,128]{1,0:T(8,128)(2,1)S(1)} %get-tuple-element.49) | copy-start | bytes 786436
  64.8 48.5 %all-to-all-start.2 = ((bf16[128,8,128]{2,1,0:T(8,128)(2,1)}), bf16[128,8,128]{2,1,0:T(8,128)(2,1)}, u32[]{:S(2)}, u32[]{:S(2)}) async-start(bf16[128,8,128]{2,1,0:T(8,128)(2,1)} %bitcast.30), calls=%async_computation.2 | async-start | bytes 524288 | tf_op jit(solution)/shard_map/all_to_all | solution.py:24
  71.3 1.0 copy-start.2
  73.1 12.3 %collective-permute-start.2 = (bf16[448,256]{1,0:T(8,128)(2,1)S(1)}, bf16[448,256]{1,0:T(8,128)(2,1)S(1)}, u32[]{:S(2)}, u32[]{:S(2)}) collective-permute-start(bf16[448,256]{1,0:T(8,128)(2,1)S(1)} %get-tuple-element.43), channel_id=1, source_target_pairs={{0,3},{1,0},{2,1},{3,2},{4,7},{5,4},{6,5},{7,6},{8,11},{9,8},{10,9... | collective-permute-start | bytes 688136 | tf_op jit(solution)/shard_map/ppermute | solution.py:143
  77.5 9.2 %collective-permute-start.1 = (bf16[448,256]{1,0:T(8,128)(2,1)S(1)}, bf16[448,256]{1,0:T(8,128)(2,1)S(1)}, u32[]{:S(2)}, u32[]{:S(2)}) collective-permute-start(bf16[448,256]{1,0:T(8,128)(2,1)S(1)} %get-tuple-element.43), channel_id=1, source_target_pairs={{0,2},{1,3},{2,0},{3,1},{4,6},{5,7},{6,4},{7,5},{8,10},{9,11},{10,... | collective-permute-start | bytes 688136 | tf_op jit(solution)/shard_map/ppermute | solution.py:143
  79.9 12.9 %collective-permute-start = (bf16[448,256]{1,0:T(8,128)(2,1)S(1)}, bf16[448,256]{1,0:T(8,128)(2,1)S(1)}, u32[]{:S(2)}, u32[]{:S(2)}) collective-permute-start(bf16[448,256]{1,0:T(8,128)(2,1)S(1)} %get-tuple-element.43), channel_id=1, source_target_pairs={{0,1},{1,2},{2,3},{3,0},{4,5},{5,6},{6,7},{7,4},{8,9},{9,10},{10,1... | collective-permute-start | bytes 688136 | tf_op jit(solution)/shard_map/ppermute | solution.py:143
  98.5 35.7 %copy-start.3 = (bf16[896,128]{1,0:T(8,128)(2,1)S(1)}, bf16[896,128]{1,0:T(8,128)(2,1)}, u32[]{:S(2)}) copy-start(bf16[896,128]{1,0:T(8,128)(2,1)} %param.19) | copy-start | bytes 688132
  98.5 35.7 %copy-start.4 = (bf16[128,896]{1,0:T(8,128)(2,1)S(1)}, bf16[128,896]{1,0:T(8,128)(2,1)}, u32[]{:S(2)}) copy-start(bf16[128,896]{1,0:T(8,128)(2,1)} %proj_ref.3) | copy-start | bytes 688132
  98.5 15.9 %collective-permute-start.3 = (bf16[464,256]{1,0:T(8,128)(2,1)}, bf16[464,256]{1,0:T(8,128)(2,1)S(1)}, u32[]{:S(2)}, u32[]{:S(2)}) collective-permute-start(bf16[464,256]{1,0:T(8,128)(2,1)} %get-tuple-element.45), channel_id=1, source_target_pairs={{0,1},{1,2},{2,3},{3,0},{4,5},{5,6},{6,7},{7,4},{8,9},{9,10},{10,1... | collective-permute-start | bytes 712712 | tf_op jit(solution)/shard_map/ppermute | solution.py:143
  100.5 17.8 %collective-permute-start.4 = (bf16[464,256]{1,0:T(8,128)(2,1)}, bf16[464,256]{1,0:T(8,128)(2,1)S(1)}, u32[]{:S(2)}, u32[]{:S(2)}) collective-permute-start(bf16[464,256]{1,0:T(8,128)(2,1)} %get-tuple-element.46), channel_id=1, source_target_pairs={{0,2},{1,3},{2,0},{3,1},{4,6},{5,7},{6,4},{7,5},{8,10},{9,11},{10,... | collective-permute-start | bytes 712712 | tf_op jit(solution)/shard_map/ppermute | solution.py:143
  102.9 15.5 %collective-permute-start.5 = (bf16[464,256]{1,0:T(8,128)(2,1)}, bf16[464,256]{1,0:T(8,128)(2,1)S(1)}, u32[]{:S(2)}, u32[]{:S(2)}) collective-permute-start(bf16[464,256]{1,0:T(8,128)(2,1)} %get-tuple-element.47), channel_id=1, source_target_pairs={{0,3},{1,0},{2,1},{3,2},{4,7},{5,4},{6,5},{7,6},{8,11},{9,8},{10,9... | collective-permute-start | bytes 712712 | tf_op jit(solution)/shard_map/ppermute | solution.py:143
  107.0 27.1 %collective-permute-start.6 = (bf16[224,128]{1,0:T(8,128)(2,1)}, bf16[224,128]{1,0:T(8,128)(2,1)S(1)}, u32[]{:S(2)}, u32[]{:S(2)}) collective-permute-start(bf16[224,128]{1,0:T(8,128)(2,1)} %get-tuple-element.53), channel_id=1, source_target_pairs={{0,1},{1,2},{2,3},{3,0},{4,5},{5,6},{6,7},{7,4},{8,9},{9,10},{10,1... | collective-permute-start | bytes 172040 | tf_op jit(solution)/shard_map/ppermute | solution.py:143
  109.5 24.6 %collective-permute-start.7 = (bf16[224,128]{1,0:T(8,128)(2,1)}, bf16[224,128]{1,0:T(8,128)(2,1)S(1)}, u32[]{:S(2)}, u32[]{:S(2)}) collective-permute-start(bf16[224,128]{1,0:T(8,128)(2,1)} %get-tuple-element.54), channel_id=1, source_target_pairs={{0,2},{1,3},{2,0},{3,1},{4,6},{5,7},{6,4},{7,5},{8,10},{9,11},{10,... | collective-permute-start | bytes 172040 | tf_op jit(solution)/shard_map/ppermute | solution.py:143
  114.4 19.7 %collective-permute-start.8 = (bf16[224,128]{1,0:T(8,128)(2,1)}, bf16[224,128]{1,0:T(8,128)(2,1)S(1)}, u32[]{:S(2)}, u32[]{:S(2)}) collective-permute-start(bf16[224,128]{1,0:T(8,128)(2,1)} %copy-done.17), channel_id=1, source_target_pairs={{0,3},{1,0},{2,1},{3,2},{4,7},{5,4},{6,5},{7,6},{8,11},{9,8},{10,9... | collective-permute-start | bytes 172040 | tf_op jit(solution)/shard_map/ppermute | solution.py:143
  134.1 45.4 %copy-start.7 = (bf16[448,256]{1,0:T(8,128)(2,1)S(1)}, bf16[448,256]{1,0:T(8,128)(2,1)}, u32[]{:S(2)}) copy-start(bf16[448,256]{1,0:T(8,128)(2,1)} %copy-done.5) | copy-start | bytes 688132
  134.1 45.4 %copy-start.12 = (bf16[224,256]{1,0:T(8,128)(2,1)S(1)}, bf16[224,256]{1,0:T(8,128)(2,1)}, u32[]{:S(2)}) copy-start(bf16[224,256]{1,0:T(8,128)(2,1)} %get-tuple-element.63.refs_5_) | copy-start | bytes 344068
  138.3 8.4 %collective-permute-start.12 = (bf16[512,384]{1,0:T(8,128)(2,1)S(1)}, bf16[512,384]{1,0:T(8,128)(2,1)S(1)}, u32[]{:S(2)}, u32[]{:S(2)}) collective-permute-start(bf16[512,384]{1,0:T(8,128)(2,1)S(1)} %get-tuple-element.69), channel_id=1, source_target_pairs={{0,4},{4,0},{1,5},{5,1},{2,6},{6,2},{3,7},{7,3},{8,12},{12,8},{9,1... | collective-permute-start | bytes 1179656 | tf_op jit(solution)/shard_map/ppermute | solution.py:478
  147.5 28.0 %all-to-all-start.3 = ((bf16[64,8,384]{2,1,0:T(8,128)(2,1)}), bf16[64,8,384]{2,1,0:T(8,128)(2,1)S(1)}, u32[]{:S(2)}, u32[]{:S(2)}) async-start(bf16[64,8,384]{2,1,0:T(8,128)(2,1)} %bitcast.20), calls=%async_computation.3 | async-start | bytes 786432 | tf_op jit(solution)/shard_map/all_to_all | solution.py:24
  161.4 18.1 %collective-permute-start.9 = (bf16[464,256]{1,0:T(8,128)(2,1)S(1)}, bf16[464,256]{1,0:T(8,128)(2,1)S(1)}, u32[]{:S(2)}, u32[]{:S(2)}) collective-permute-start(bf16[464,256]{1,0:T(8,128)(2,1)S(1)} %get-tuple-element.60), channel_id=1, source_target_pairs={{0,1},{1,2},{2,3},{3,0},{4,5},{5,6},{6,7},{7,4},{8,9},{9,10},{10,1... | collective-permute-start | bytes 712712 | tf_op jit(solution)/shard_map/ppermute | solution.py:143
  163.4 16.1 %collective-permute-start.10 = (bf16[464,256]{1,0:T(8,128)(2,1)S(1)}, bf16[464,256]{1,0:T(8,128)(2,1)S(1)}, u32[]{:S(2)}, u32[]{:S(2)}) collective-permute-start(bf16[464,256]{1,0:T(8,128)(2,1)S(1)} %get-tuple-element.61), channel_id=1, source_target_pairs={{0,2},{1,3},{2,0},{3,1},{4,6},{5,7},{6,4},{7,5},{8,10},{9,11},{10,... | collective-permute-start | bytes 712712 | tf_op jit(solution)/shard_map/ppermute | solution.py:143
  166.5 13.1 %collective-permute-start.11 = (bf16[464,256]{1,0:T(8,128)(2,1)S(1)}, bf16[464,256]{1,0:T(8,128)(2,1)S(1)}, u32[]{:S(2)}, u32[]{:S(2)}) collective-permute-start(bf16[464,256]{1,0:T(8,128)(2,1)S(1)} %get-tuple-element.62), channel_id=1, source_target_pairs={{0,3},{1,0},{2,1},{3,2},{4,7},{5,4},{6,5},{7,6},{8,11},{9,8},{10,9... | collective-permute-start | bytes 712712 | tf_op jit(solution)/shard_map/ppermute | solution.py:143
  176.3 7.4 %all-to-all-start.4 = ((f32[4,7,128]{2,1,0:T(8,128)}), f32[4,7,128]{2,1,0:T(8,128)S(1)}, u32[]{:S(2)}, u32[]{:S(2)}) async-start(f32[4,7,128]{2,1,0:T(8,128)} %get-tuple-element.71), calls=%async_computation.4 | async-start | bytes 32768 | tf_op jit(solution)/shard_map/all_to_all | solution.py:24
  (10 other events, 7.5 us)

commit v6 on v4

--- a/solution.py
+++ b/solution.py
@@ -17,7 +17,7 @@
 BF16 = jnp.bfloat16
 
 
-PAD = 16
+PAD = 8
 
 
 def exchange(value, axis):
@@ -35,7 +35,7 @@
 
 def facts_kernel(blocks_ref, fill_ref, plan_ref, out_ref):
     docs = blocks_ref.shape[1]
-    counts = jnp.broadcast_to(blocks_ref[...], (PAD, docs)).astype(F32)
+    counts = jnp.broadcast_to(blocks_ref[...], (8, docs)).astype(F32)
     fills = fill_ref[...].astype(F32)
     row = lax.broadcasted_iota(jnp.int32, (docs, docs), 0)
     col = lax.broadcasted_iota(jnp.int32, (docs, docs), 1)
@@ -260,7 +260,10 @@
 def last_kernel(
     facts_ref, *refs
 ):
-    *parts, kept_ref, second_ref, inverse_ref, first_ref, cot_ref = refs
+    *parts, kept_ref, second_ref, first_cot_ref, inverse_ref = refs[:-4]
+    first_ref, cot_ref, second_out_ref, first_cot_out_ref = refs[-4:]
+    second_out_ref[...] = second_ref[...]
+    first_cot_out_ref[...] = first_cot_ref[...]
     width = second_ref.shape[0]
     total = parts[0][...].astype(F32)
     for part in parts[1:]:
@@ -480,8 +483,17 @@
     )
     with jax.named_scope("last_sum"):
         parts = [parts[0]] + [turn(parts[k], k) for k in range(1, MP)]
-    first_in, second_cot = call(
-        last_kernel, (stream, stream), facts, *parts, kept, second_in, r_two, smem=1, name="last"
+    first_in, second_cot, second_in, first_cot = call(
+        last_kernel,
+        (stream,) * 4,
+        facts,
+        *parts,
+        kept,
+        second_in,
+        first_cot,
+        r_two,
+        smem=1,
+        name="last",
     )
     share = jax.ShapeDtypeStruct((7 * BLOCK // seq_size, 128), F32)
     query_grad, out_grad, own = call(

time: 158 us -> 157 us (level)
  no operation moved by 1% of the time
where the time goes in v6:
time: 157 us; the launch traced here: 155 us
  blocking collectives  78.6 us (50%)
  starting transfers between devices  39.8 us (25%)
  waiting for transfers between devices  18.4 us (12%)
  Pallas kernels  15.7 us (10%)
    all_to_all x2, blocking collectives, exchange(): return lax.all_to_all(value, axis, split_axis=0, concat_axis=0, tiled=True)  53.6 us
    all_gather x2, blocking collectives, shards(): rows = lax.all_gather(send, 'mp', axis=0)  25 us
    ppermute x6, starting transfers between devices, turn(): return lax.ppermute(value, 'mp', [(i, (i + by) % MP) for i in range(MP)])  19.5 us
    all_to_all x3, waiting for transfers between devices, exchange(): return lax.all_to_all(value, axis, split_axis=0, concat_axis=0, tiled=True)  17.1 us
    pallas_call x12, Pallas kernels, call(): pl.pallas_call(kernel, in_specs=[pl.BlockSpec(memory_space=s) for s in sp...  15.7 us
    all_to_all x3, starting transfers between devices, exchange(): return lax.all_to_all(value, axis, split_axis=0, concat_axis=0, tiled=True)  13.3 us
    ppermute x1, starting transfers between devices, shards(): given = lax.ppermute(given, 'seq_2', [(0, 1), (1, 0)])  7.01 us
  transfers between devices with their start and end apart: 10, of which 4 were waited for; matrix products, arithmetic and copies ran while one was open for 0% of the time, Pallas kernels for 3%

profile of v6, /device:TPU:1, one launch (start us, length us, event | category | flops | bytes accessed | tf_op | source)
XLA Modules:
  0.0 154.6 jit_solution(16558832873798259265)
XLA Ops:
  0.7 1.2 pad_maximum_fusion.streams_ref
  2.1 38.9 %all_to_all.25 = bf16[128,8,256]{2,1,0:T(8,128)(2,1)S(1)} all-to-all(bf16[128,8,256]{2,1,0:T(8,128)(2,1)S(1)} %bitcast.25), channel_id=1, replica_groups=mesh['seq_0'=8,'seq_1'=8,'seq_2'=2,'mp'=4] {'seq_0','seq_1','seq_2'}, dimensions={0} | all-to-all | bytes 1048576 | tf_op jit(solution)/shard_map/hop_one/all_to_all | solution.py:24
  41.0 1.2 reorder.1
  42.3 5.4 %all-to-all-start.1 = ((bf16[128,8,256]{2,1,0:T(8,128)(2,1)}), bf16[128,8,256]{2,1,0:T(8,128)(2,1)S(1)}, u32[]{:S(2)}, u32[]{:S(2)}) async-start(bf16[128,8,256]{2,1,0:T(8,128)(2,1)} %bitcast.7), calls=%async_computation.1 | async-start | bytes 1048576 | tf_op jit(solution)/shard_map/hop_two/all_to_all | solution.py:24
  47.7 3.1 %collective-permute-start = (bf16[224,128]{1,0:T(8,128)(2,1)}, bf16[224,128]{1,0:T(8,128)(2,1)S(1)}, u32[]{:S(2)}, u32[]{:S(2)}) collective-permute-start(bf16[224,128]{1,0:T(8,128)(2,1)} %get-tuple-element.45), channel_id=1, source_target_pairs={{0,1},{1,2},{2,3},{3,0},{4,5},{5,6},{6,7},{7,4},{8,9},{9,10},{10,1... | collective-permute-start | bytes 172040 | tf_op jit(solution)/shard_map/weights/ppermute | solution.py:125
  50.8 4.3 %collective-permute-start.1 = (bf16[224,128]{1,0:T(8,128)(2,1)}, bf16[224,128]{1,0:T(8,128)(2,1)S(1)}, u32[]{:S(2)}, u32[]{:S(2)}) collective-permute-start(bf16[224,128]{1,0:T(8,128)(2,1)} %get-tuple-element.46), channel_id=1, source_target_pairs={{0,2},{1,3},{2,0},{3,1},{4,6},{5,7},{6,4},{7,5},{8,10},{9,11},{10,... | collective-permute-start | bytes 172040 | tf_op jit(solution)/shard_map/weights/ppermute | solution.py:125
  55.2 3.1 %collective-permute-start.2 = (bf16[224,128]{1,0:T(8,128)(2,1)}, bf16[224,128]{1,0:T(8,128)(2,1)S(1)}, u32[]{:S(2)}, u32[]{:S(2)}) collective-permute-start(bf16[224,128]{1,0:T(8,128)(2,1)} %get-tuple-element.47), channel_id=1, source_target_pairs={{0,3},{1,0},{2,1},{3,2},{4,7},{5,4},{6,5},{7,6},{8,11},{9,8},{10,9... | collective-permute-start | bytes 172040 | tf_op jit(solution)/shard_map/weights/ppermute | solution.py:125
  59.1 9.1 %all-to-all-done.1 = bf16[128,8,256]{2,1,0:T(8,128)(2,1)S(1)} async-done(((bf16[128,8,256]{2,1,0:T(8,128)(2,1)}), bf16[128,8,256]{2,1,0:T(8,128)(2,1)S(1)}, u32[]{:S(2)}, u32[]{:S(2)}) %all-to-all-start.1) | async-done | bytes 524320 | tf_op jit(solution)/shard_map/hop_two/all_to_all | solution.py:24
  68.5 13.2 %all-gather = bf16[1792,256]{1,0:T(8,128)(2,1)S(1)} all-gather(bf16[448,256]{1,0:T(8,128)(2,1)S(1)} %get-tuple-element.49), channel_id=2, replica_groups=mesh['seq_0'=8,'seq_1'=8,'seq_2'=2,'mp'=4] {'mp'}, dimensions={0}, use_global_device_ids=true | all-gather | bytes 1146880 | tf_op jit(solution)/shard_map/gather_one/all_gather | solution.py:420
  81.8 3.4 %feed_forward.1 = (bf16[4,456,256]{2,1,0:T(8,128)(2,1)S(1)}, f32[1,256]{1,0:T(1,128)S(1)}) custom-call(bf16[4,448,256]{2,1,0:T(8,128)(2,1)S(1)} %bitcast.21, bf16[2,896,640]{2,1,0:T(8,128)(2,1)S(1)} %copy-done, bf16[640,896]{1,0:T(8,128)(2,1)S(1)} %copy-done.1), custom_call_target="tpu_custom_call" | custom-call | tf_op jit(solution)/shard_map/feed_forward/pallas_call | solution.py:65
  85.2 14.7 %all_to_all.26.parts_ref = bf16[4,456,256]{2,1,0:T(8,128)(2,1)S(1)} all-to-all(bf16[4,456,256]{2,1,0:T(8,128)(2,1)S(1)} %get-tuple-element.50), channel_id=1, replica_groups=mesh['seq_0'=8,'seq_1'=8,'seq_2'=2,'mp'=4] {'mp'}, dimensions={0} | all-to-all | bytes 1867776 | tf_op jit(solution)/shard_map/sum_one/all_to_all | solution.py:24
  100.7 11.8 %all-gather.1 = bf16[1792,256]{1,0:T(8,128)(2,1)S(1)} all-gather(bf16[448,256]{1,0:T(8,128)(2,1)S(1)} %get-tuple-element.53), channel_id=3, replica_groups=mesh['seq_0'=8,'seq_1'=8,'seq_2'=2,'mp'=4] {'mp'}, dimensions={0}, use_global_device_ids=true | all-gather | bytes 1146880 | tf_op jit(solution)/shard_map/gather_two/all_gather | solution.py:444
  112.5 4.2 %attention.1 = (bf16[512,384]{1,0:T(8,128)(2,1)S(1)}, bf16[512,384]{1,0:T(8,128)(2,1)S(1)}, bf16[3,256,128]{2,1,0:T(8,128)(2,1)S(1)}, bf16[4,224,128]{2,1,0:T(8,...) custom-call(s32[5]{0:T(128)S(1)} %facts.1.facts_ref, bf16[4,448,256]{2,1,0:T(8,128)(2,1)S(1)} %bitcast.22, ...), custom_call_target="tpu_custom_call" | custom-call | tf_op jit(solution)/shard_map/attention/pallas_call | solution.py:65
  116.7 7.0 %collective-permute-start.6 = (bf16[512,384]{1,0:T(8,128)(2,1)S(1)}, bf16[512,384]{1,0:T(8,128)(2,1)S(1)}, u32[]{:S(2)}, u32[]{:S(2)}) collective-permute-start(bf16[512,384]{1,0:T(8,128)(2,1)S(1)} %get-tuple-element.73), channel_id=1, source_target_pairs={{0,4},{4,0},{1,5},{5,1},{2,6},{6,2},{3,7},{7,3},{8,12},{12,8},{9,1... | collective-permute-start | bytes 1179656 | tf_op jit(solution)/shard_map/core_sum/ppermute | solution.py:467
  123.7 1.3 collective-permute-done.6.right_ref
  125.9 4.6 %all-to-all-start.3 = ((bf16[64,8,384]{2,1,0:T(8,128)(2,1)}), bf16[64,8,384]{2,1,0:T(8,128)(2,1)S(1)}, u32[]{:S(2)}, u32[]{:S(2)}) async-start(bf16[64,8,384]{2,1,0:T(8,128)(2,1)} %bitcast.18), calls=%async_computation.3 | async-start | bytes 786432 | tf_op jit(solution)/shard_map/weight_grads/all_to_all | solution.py:24
  130.5 1.2 pieces.1
  131.7 2.4 %collective-permute-start.3 = (bf16[456,256]{1,0:T(8,128)(2,1)S(1)}, bf16[456,256]{1,0:T(8,128)(2,1)S(1)}, u32[]{:S(2)}, u32[]{:S(2)}) collective-permute-start(bf16[456,256]{1,0:T(8,128)(2,1)S(1)} %get-tuple-element.62), channel_id=1, source_target_pairs={{0,1},{1,2},{2,3},{3,0},{4,5},{5,6},{6,7},{7,4},{8,9},{9,10},{10,1... | collective-permute-start | bytes 700424 | tf_op jit(solution)/shard_map/last_sum/ppermute | solution.py:125
  134.1 4.3 %collective-permute-start.4 = (bf16[456,256]{1,0:T(8,128)(2,1)S(1)}, bf16[456,256]{1,0:T(8,128)(2,1)S(1)}, u32[]{:S(2)}, u32[]{:S(2)}) collective-permute-start(bf16[456,256]{1,0:T(8,128)(2,1)S(1)} %get-tuple-element.63), channel_id=1, source_target_pairs={{0,2},{1,3},{2,0},{3,1},{4,6},{5,7},{6,4},{7,5},{8,10},{9,11},{10,... | collective-permute-start | bytes 700424 | tf_op jit(solution)/shard_map/last_sum/ppermute | solution.py:125
  138.4 2.3 %collective-permute-start.5 = (bf16[456,256]{1,0:T(8,128)(2,1)S(1)}, bf16[456,256]{1,0:T(8,128)(2,1)S(1)}, u32[]{:S(2)}, u32[]{:S(2)}) collective-permute-start(bf16[456,256]{1,0:T(8,128)(2,1)S(1)} %get-tuple-element.64), channel_id=1, source_target_pairs={{0,3},{1,0},{2,1},{3,2},{4,7},{5,4},{6,5},{7,6},{8,11},{9,8},{10,9... | collective-permute-start | bytes 700424 | tf_op jit(solution)/shard_map/last_sum/ppermute | solution.py:125
  140.7 5.2 %all-to-all-done.3.grads_ref = bf16[64,8,384]{2,1,0:T(8,128)(2,1)S(1)} async-done(((bf16[64,8,384]{2,1,0:T(8,128)(2,1)}), bf16[64,8,384]{2,1,0:T(8,128)(2,1)S(1)}, u32[]{:S(2)}, u32[]{:S(2)}) %all-to-all-start.3) | async-done | bytes 393248 | tf_op jit(solution)/shard_map/weight_grads/all_to_all | solution.py:24
  146.6 3.2 %all-to-all-start.4 = ((f32[4,7,128]{2,1,0:T(8,128)}), f32[4,7,128]{2,1,0:T(8,128)S(1)}, u32[]{:S(2)}, u32[]{:S(2)}) async-start(f32[4,7,128]{2,1,0:T(8,128)} %get-tuple-element.75), calls=%async_computation.4 | async-start | bytes 32768 | tf_op jit(solution)/shard_map/key_grads/all_to_all | solution.py:24
  149.9 1.4 last.1
  151.3 2.8 %all-to-all-done.4.shares_ref = f32[4,7,128]{2,1,0:T(8,128)S(1)} async-done(((f32[4,7,128]{2,1,0:T(8,128)}), f32[4,7,128]{2,1,0:T(8,128)S(1)}, u32[]{:S(2)}, u32[]{:S(2)}) %all-to-all-start.4) | async-done | bytes 14368 | tf_op jit(solution)/shard_map/key_grads/all_to_all | solution.py:24
  (29 shorter events, 4.3 us)
Async XLA Ops:
  0.6 40.4 %copy-start.4 = (bf16[2,224,128]{2,1,0:T(8,128)(2,1)S(1)}, bf16[2,224,128]{2,1,0:T(8,128)(2,1)}, u32[]{:S(2)}) copy-start(bf16[2,224,128]{2,1,0:T(8,128)(2,1)} %keyval_ref.1) | copy-start | bytes 344068
  0.6 40.4 %copy-start.5 = (s32[256]{0:T(256)S(1)}, s32[256]{0:T(256)}, u32[]{:S(2)}) copy-start(s32[256]{0:T(256)} %param.18) | copy-start | bytes 3076
  0.7 57.6 %copy-start.6 = (s32[192]{0:T(256)S(1)}, s32[192]{0:T(256)}, u32[]{:S(2)}) copy-start(s32[192]{0:T(256)} %param.16) | copy-start | bytes 2308
  0.7 57.6 %copy-start.7 = (s32[192]{0:T(256)S(1)}, s32[192]{0:T(256)}, u32[]{:S(2)}) copy-start(s32[192]{0:T(256)} %param.17) | copy-start | bytes 2308
  2.1 79.6 %copy-start = (bf16[2,896,640]{2,1,0:T(8,128)(2,1)S(1)}, bf16[2,896,640]{2,1,0:T(8,128)(2,1)}, u32[]{:S(2)}) copy-start(bf16[2,896,640]{2,1,0:T(8,128)(2,1)} %gate_up_ref.1) | copy-start | bytes 6881284
  42.3 26.0 %all-to-all-start.1 = ((bf16[128,8,256]{2,1,0:T(8,128)(2,1)}), bf16[128,8,256]{2,1,0:T(8,128)(2,1)S(1)}, u32[]{:S(2)}, u32[]{:S(2)}) async-start(bf16[128,8,256]{2,1,0:T(8,128)(2,1)} %bitcast.7), calls=%async_computation.1 | async-start | bytes 1048576 | tf_op jit(solution)/shard_map/hop_two/all_to_all | solution.py:24
  47.7 20.8 %collective-permute-start = (bf16[224,128]{1,0:T(8,128)(2,1)}, bf16[224,128]{1,0:T(8,128)(2,1)S(1)}, u32[]{:S(2)}, u32[]{:S(2)}) collective-permute-start(bf16[224,128]{1,0:T(8,128)(2,1)} %get-tuple-element.45), channel_id=1, source_target_pairs={{0,1},{1,2},{2,3},{3,0},{4,5},{5,6},{6,7},{7,4},{8,9},{9,10},{10,1... | collective-permute-start | bytes 172040 | tf_op jit(solution)/shard_map/weights/ppermute | solution.py:125
  50.8 17.7 %collective-permute-start.1 = (bf16[224,128]{1,0:T(8,128)(2,1)}, bf16[224,128]{1,0:T(8,128)(2,1)S(1)}, u32[]{:S(2)}, u32[]{:S(2)}) collective-permute-start(bf16[224,128]{1,0:T(8,128)(2,1)} %get-tuple-element.46), channel_id=1, source_target_pairs={{0,2},{1,3},{2,0},{3,1},{4,6},{5,7},{6,4},{7,5},{8,10},{9,11},{10,... | collective-permute-start | bytes 172040 | tf_op jit(solution)/shard_map/weights/ppermute | solution.py:125
  55.2 13.4 %collective-permute-start.2 = (bf16[224,128]{1,0:T(8,128)(2,1)}, bf16[224,128]{1,0:T(8,128)(2,1)S(1)}, u32[]{:S(2)}, u32[]{:S(2)}) collective-permute-start(bf16[224,128]{1,0:T(8,128)(2,1)} %get-tuple-element.47), channel_id=1, source_target_pairs={{0,3},{1,0},{2,1},{3,2},{4,7},{5,4},{6,5},{7,6},{8,11},{9,8},{10,9... | collective-permute-start | bytes 172040 | tf_op jit(solution)/shard_map/weights/ppermute | solution.py:125
  68.2 13.5 %copy-start.1 = (bf16[640,896]{1,0:T(8,128)(2,1)S(1)}, bf16[640,896]{1,0:T(8,128)(2,1)}, u32[]{:S(2)}) copy-start(bf16[640,896]{1,0:T(8,128)(2,1)} %down_ref.1) | copy-start | bytes 3440644
  85.2 27.3 %copy-start.2 = (bf16[896,128]{1,0:T(8,128)(2,1)S(1)}, bf16[896,128]{1,0:T(8,128)(2,1)}, u32[]{:S(2)}) copy-start(bf16[896,128]{1,0:T(8,128)(2,1)} %param.19) | copy-start | bytes 688132
  85.2 27.3 %copy-start.3 = (bf16[128,896]{1,0:T(8,128)(2,1)S(1)}, bf16[128,896]{1,0:T(8,128)(2,1)}, u32[]{:S(2)}) copy-start(bf16[128,896]{1,0:T(8,128)(2,1)} %proj_ref.3) | copy-start | bytes 688132
  116.7 8.3 %collective-permute-start.6 = (bf16[512,384]{1,0:T(8,128)(2,1)S(1)}, bf16[512,384]{1,0:T(8,128)(2,1)S(1)}, u32[]{:S(2)}, u32[]{:S(2)}) collective-permute-start(bf16[512,384]{1,0:T(8,128)(2,1)S(1)} %get-tuple-element.73), channel_id=1, source_target_pairs={{0,4},{4,0},{1,5},{5,1},{2,6},{6,2},{3,7},{7,3},{8,12},{12,8},{9,1... | collective-permute-start | bytes 1179656 | tf_op jit(solution)/shard_map/core_sum/ppermute | solution.py:467
  125.9 20.0 %all-to-all-start.3 = ((bf16[64,8,384]{2,1,0:T(8,128)(2,1)}), bf16[64,8,384]{2,1,0:T(8,128)(2,1)S(1)}, u32[]{:S(2)}, u32[]{:S(2)}) async-start(bf16[64,8,384]{2,1,0:T(8,128)(2,1)} %bitcast.18), calls=%async_computation.3 | async-start | bytes 786432 | tf_op jit(solution)/shard_map/weight_grads/all_to_all | solution.py:24
  131.7 18.2 %collective-permute-start.3 = (bf16[456,256]{1,0:T(8,128)(2,1)S(1)}, bf16[456,256]{1,0:T(8,128)(2,1)S(1)}, u32[]{:S(2)}, u32[]{:S(2)}) collective-permute-start(bf16[456,256]{1,0:T(8,128)(2,1)S(1)} %get-tuple-element.62), channel_id=1, source_target_pairs={{0,1},{1,2},{2,3},{3,0},{4,5},{5,6},{6,7},{7,4},{8,9},{9,10},{10,1... | collective-permute-start | bytes 700424 | tf_op jit(solution)/shard_map/last_sum/ppermute | solution.py:125
  134.1 15.8 %collective-permute-start.4 = (bf16[456,256]{1,0:T(8,128)(2,1)S(1)}, bf16[456,256]{1,0:T(8,128)(2,1)S(1)}, u32[]{:S(2)}, u32[]{:S(2)}) collective-permute-start(bf16[456,256]{1,0:T(8,128)(2,1)S(1)} %get-tuple-element.63), channel_id=1, source_target_pairs={{0,2},{1,3},{2,0},{3,1},{4,6},{5,7},{6,4},{7,5},{8,10},{9,11},{10,... | collective-permute-start | bytes 700424 | tf_op jit(solution)/shard_map/last_sum/ppermute | solution.py:125
  138.4 11.5 %collective-permute-start.5 = (bf16[456,256]{1,0:T(8,128)(2,1)S(1)}, bf16[456,256]{1,0:T(8,128)(2,1)S(1)}, u32[]{:S(2)}, u32[]{:S(2)}) collective-permute-start(bf16[456,256]{1,0:T(8,128)(2,1)S(1)} %get-tuple-element.64), channel_id=1, source_target_pairs={{0,3},{1,0},{2,1},{3,2},{4,7},{5,4},{6,5},{7,6},{8,11},{9,8},{10,9... | collective-permute-start | bytes 700424 | tf_op jit(solution)/shard_map/last_sum/ppermute | solution.py:125
  146.6 7.4 %all-to-all-start.4 = ((f32[4,7,128]{2,1,0:T(8,128)}), f32[4,7,128]{2,1,0:T(8,128)S(1)}, u32[]{:S(2)}, u32[]{:S(2)}) async-start(f32[4,7,128]{2,1,0:T(8,128)} %get-tuple-element.75), calls=%async_computation.4 | async-start | bytes 32768 | tf_op jit(solution)/shard_map/key_grads/all_to_all | solution.py:24
